TPU v7x, 512 devices: a 8x2x16 block of a 8x16x16 slice. The times are simulated.
512 devices in a mesh: groups: 2 (over y), seq: 32 (over z, core), rep: 8 (over x).
Axes of the slice: x: 8, y: 2, z: 16, core: 2. Of those that a mesh axis runs over, the one named last changes fastest.
The devices are a block of a 8x16x16 slice.
Arguments:
- queries: bfloat16 [1024, 4096], P(('groups', 'seq'), 'rep'), parts along dimension 0, may hold values from -128 to 128
- keys_new: bfloat16 [1024, 1024], P(('groups', 'seq'), 'rep'), parts along dimension 0, may hold values from -4 to 4
- values_new: bfloat16 [1024, 1024], P(('groups', 'seq'), 'rep'), parts along dimension 0, may hold values from -6 to 6
- keys_past: bfloat16 [16384, 1024], P(('groups', 'seq'), 'rep'), parts along dimension 0, may hold values from -4 to 4
- values_past: bfloat16 [16384, 1024], P(('groups', 'seq'), 'rep'), parts along dimension 0, may hold values from -6 to 6
- block_order: int32 [64], P('groups'), parts along dimension 0, may hold values from 0 to 31, each once
- residual: bfloat16 [1024, 4096], P(('groups', 'seq'), 'rep'), parts along dimension 0, may hold values from -6 to 6
- out_proj: bfloat16 [4096, 4096], P('seq', 'rep'), may hold values from -0.09375 to 0.09375
- norm_gain: float32 [4096], replicated, may hold values from 0.5 to 1.5
- router: float32 [4096, 4], replicated, may hold values from -0.09375 to 0.09375
- w_gate: bfloat16 [8, 4096, 4096], P('rep', None, 'seq'), may hold values from -0.09375 to 0.09375
- w_up: bfloat16 [8, 4096, 4096], P('rep', None, 'seq'), may hold values from -0.09375 to 0.09375
- w_down: bfloat16 [8, 4096, 4096], P('rep', 'seq'), may hold values from -0.0625 to 0.0625
- expert_ids: int32 [1024, 2], P(('groups', 'seq')), parts along dimension 0, may hold values from 0 to 3, all different within a row; in each aligned block of 16 rows (0 to 15, 16 to 31, ...) at most 12 rows name the same one
Outputs:
- attended: bfloat16 [1024, 4096], P(('groups', 'seq'), 'rep'), parts along dimension 0
- layer_out: bfloat16 [1024, 4096], P(('groups', 'seq'), 'rep'), parts along dimension 0
- keys_cache: bfloat16 [1024, 1024], P(('groups', 'seq')), parts along dimension 0
- values_cache: bfloat16 [1024, 1024], P(('groups', 'seq')), parts along dimension 0
There are 2 independent parts, one for each index of `groups`. A program takes and returns all parts, laid end to end along the dimension named above; an argument that names none is the same for every part. Nothing has to cross between parts.
Inputs may be any that keep to these rules, and one draw needn't show every extreme that they name: `block_order`: each block index 0 to 32 - 1 appears once. `expert_ids`: each row names 2 different experts; in the rows of one device (aligned blocks of 16 rows) no expert is named by more than 12 rows, and in some block one expert is named by exactly 12.
All inputs are finite; a program needn't handle non-finite values.
Results may differ from a plain program's by a relative error of at most 0.011.
Values may be sent and summed in bfloat16 or wider, within the bound.
No kernel may reach another device: no remote copies, remote signals or barrier semaphores. Data moves between devices by JAX's collectives and lax.ppermute only.
A program may use at most 64 MiB of HBM per device.

v0:
```python
import math

import jax
import jax.numpy as jnp
from jax import lax
from jax.sharding import Mesh
from jax.sharding import PartitionSpec as P


EXPERTS = 4
CAP = 12
LANES = 128
PAIR = 2
CORES = 2
SEQ = ("far", "near", "core")
TOKENS = ("groups", "far", "near", "core")
SHARE = ("near", "core")
CLASS = ("far",)
EARLY_PART = 9 / 16


def swapped(array, axis):
    return lax.ppermute(array, axis, [(0, 1), (1, 0)])


def after(array, ready):
    return lax.optimization_barrier((array, ready))[0]


def owners_by(axes):
    place = {a: lax.axis_index(a) for a in SEQ}
    held = [place]
    for axis in axes:
        held = held + [{**p, axis: 1 - p[axis]} for p in held]
    sizes = {a: lax.axis_size(a) for a in SEQ}
    return [(p["far"] * sizes["near"] + p["near"]) * sizes["core"] + p["core"] for p in held]


def exchanged(tiles, axis):
    return lax.all_to_all(tiles, axis, 0, 0, tiled=True)


def sent_to_all(array, axis):
    return exchanged(jnp.broadcast_to(array[None], (lax.axis_size(axis), *array.shape)), axis)


def side_by_side(tiles):
    return jnp.concatenate([tiles[i] for i in range(tiles.shape[0])], axis=1)


def block_lookup(owners, block_order):
    width = block_order.shape[0]
    hits = owners[:, None] == jnp.arange(width, dtype=jnp.int32)[None, :]
    return jnp.sum(jnp.where(hits, block_order[None, :], 0), axis=1)


def class_places(axes):
    sizes = {a: lax.axis_size(a) for a in SEQ}
    count = lax.axis_size(axes)
    index = jnp.arange(count, dtype=jnp.int32)
    place = {a: jnp.full((count,), lax.axis_index(a), jnp.int32) for a in SEQ}
    for axis in reversed(axes):
        place[axis] = index % sizes[axis]
        index = index // sizes[axis]
    return (place["far"] * sizes["near"] + place["near"]) * sizes["core"] + place["core"]


def body(
    queries,
    keys_new,
    values_new,
    keys_past,
    values_past,
    block_order,
    residual,
    out_proj,
    norm_gain,
    router,
    w_gate,
    w_up,
    w_down,
    expert_ids,
):
    bf16, f32 = jnp.bfloat16, jnp.float32
    tok = queries.shape[0]
    head_dim = keys_new.shape[1]
    q_per = queries.shape[1] // head_dim
    width = queries.shape[1]
    past_len = keys_past.shape[0]
    rep_count = lax.axis_size("rep")
    scaling = 1.0 / math.sqrt(head_dim)

    count = lax.axis_size(CLASS)
    rows = count * tok
    kv_local = jnp.concatenate(
        [
            jnp.concatenate([keys_past, keys_new], axis=0),
            jnp.concatenate([values_past, values_new], axis=0),
        ],
        axis=1,
    )
    kv_pair = jnp.concatenate([kv_local, swapped(kv_local, "near")], axis=0)
    kv_all = jnp.concatenate([kv_pair, swapped(kv_pair, "core")], axis=0)
    out_proj_own = lax.all_gather(out_proj, ("far", "near"), axis=0, tiled=True)
    out_proj_other = swapped(out_proj_own, "core")

    ids_wide = jnp.pad(expert_ids.astype(bf16), ((0, 0), (0, LANES - expert_ids.shape[1])))
    query_class = sent_to_all(jnp.concatenate([queries, ids_wide], axis=1), CLASS)
    query_class = query_class.reshape(rows, width + LANES)
    ids = query_class[:, width : width + 2].astype(jnp.int32)
    query_pos = (
        block_lookup(class_places(CLASS), block_order)[:, None] * tok
        + jnp.arange(tok, dtype=jnp.int32)[None, :]
    ).reshape(rows)

    key_span = past_len + tok
    key_owner_pos = block_lookup(jnp.stack(owners_by(SHARE)), block_order)
    offset = jnp.arange(key_span, dtype=jnp.int32) - past_len
    key_pos = jnp.where(
        offset[None, :] >= 0, key_owner_pos[:, None] * tok + offset[None, :], -1
    ).reshape(-1)
    visible = key_pos[None, :] <= query_pos[:, None]
    keys, values = kv_all[:, :head_dim], kv_all[:, head_dim:]
    heads = jnp.stack(
        [query_class[:, j * head_dim : (j + 1) * head_dim] for j in range(q_per)], axis=0
    )
    scores = jnp.einsum("jtd,kd->jtk", heads, keys, preferred_element_type=f32) * scaling
    scores = jnp.where(visible[None], scores, -1e30)
    shift = jnp.max(scores, axis=2).astype(bf16)
    weights = jnp.exp(scores - shift.astype(f32)[:, :, None])
    totals = jnp.sum(weights, axis=2)
    partial = jnp.einsum("jtk,kd->jtd", weights.astype(bf16), values, preferred_element_type=f32)
    totals_high = totals.astype(bf16)
    totals_low = (totals - totals_high.astype(f32)).astype(bf16)
    notes = jnp.concatenate([shift, totals_high, totals_low], axis=0).T
    notes = jnp.pad(notes, ((0, 0), (0, LANES - notes.shape[1])))
    message = jnp.concatenate([partial[j].astype(bf16) for j in range(q_per)] + [notes], axis=1)
    parts = exchanged(message.reshape(count, tok, width + LANES), CLASS)

    model = w_gate.shape[1]
    cut = int(model * EARLY_PART)
    gate_up = jnp.concatenate([w_gate[0], w_up[0]], axis=1)
    down = w_down[0]
    gate_up_core = swapped(gate_up, "core")
    down_core = swapped(down, "core")
    first_pair = swapped(after(gate_up[:cut], parts), "near")
    first_cross = swapped(first_pair, "core")

    part_shift = parts[:, :, width : width + q_per].astype(f32)
    part_total = parts[:, :, width + q_per : width + 2 * q_per].astype(f32) + parts[
        :, :, width + 2 * q_per : width + 3 * q_per
    ].astype(f32)
    level = jnp.exp(part_shift - jnp.max(part_shift, axis=0, keepdims=True))
    total = jnp.sum(level * part_total, axis=0)
    attn_local = jnp.concatenate(
        [
            jnp.sum(
                level[:, :, j : j + 1]
                * parts[:, :, j * head_dim : (j + 1) * head_dim].astype(f32),
                axis=0,
            )
            / total[:, j : j + 1]
            for j in range(q_per)
        ],
        axis=1,
    ).astype(bf16)

    spread = sent_to_all(jnp.concatenate([attn_local, keys_new, values_new], axis=1), "rep")
    keys_cache = side_by_side(spread[:, :, width : width + head_dim])
    values_cache = side_by_side(spread[:, :, width + head_dim :])
    core = lax.axis_index("core")
    rows_of = out_proj.shape[0]
    even, odd = (
        side_by_side(
            jnp.concatenate(
                [spread[:, :, j : j + rows_of] for j in range(first, width, CORES * rows_of)], axis=2
            )
        )
        for first in (0, rows_of)
    )
    projected = jnp.dot(
        jnp.where(core == 0, even, odd), out_proj_own, preferred_element_type=f32
    ) + jnp.dot(jnp.where(core == 0, odd, even), out_proj_other, preferred_element_type=f32)
    attended = (residual.astype(f32) + projected).astype(bf16)

    class_rows = rows
    class_width = attended.shape[1]
    class_attended = sent_to_all(attended, CLASS).reshape(class_rows, class_width)
    second_pair = swapped(after(gate_up[cut:], class_attended), "near")
    down_pair = swapped(after(down, class_attended), "near")
    experts = jnp.arange(EXPERTS, dtype=jnp.int32)
    first_pick = (ids[:, 0:1] == experts[None, :]).astype(f32)
    second_pick = (ids[:, 1:2] == experts[None, :]).astype(f32)
    member = first_pick + second_pick
    row = jnp.arange(class_rows, dtype=jnp.int32)
    earlier = (row[:, None] // tok == row[None, :] // tok) & (row[None, :] < row[:, None])
    ranking = jnp.dot(
        earlier.astype(bf16), member.astype(bf16), preferred_element_type=f32
    ).astype(jnp.int32)
    slot_of = jnp.where(member > 0, (row[:, None] // tok) * CAP + ranking, -1)
    slot_count = count * CAP
    slots = jnp.arange(slot_count, dtype=jnp.int32)
    selection = (slot_of.T[:, None, :] == slots[None, :, None]).astype(bf16)
    slot_rows = jnp.dot(
        selection.reshape(EXPERTS * slot_count, class_rows),
        class_attended,
        preferred_element_type=f32,
    ).astype(bf16)
    slot_rows = slot_rows.reshape(EXPERTS, slot_count, class_width)
    halves = rep_count // EXPERTS
    arrived = exchanged(jnp.concatenate([slot_rows] * halves, axis=0), "rep")
    features = side_by_side(arrived).astype(f32)

    mean_square = jnp.mean(features * features, axis=1, keepdims=True)
    normed = (features * norm_gain[None, :] * lax.rsqrt(mean_square + 1e-05)).astype(bf16)
    logits = jnp.dot(normed.astype(f32), router, precision=lax.Precision.HIGHEST)
    mine = lax.axis_index("rep") % EXPERTS
    my_selection = lax.dynamic_index_in_dim(selection, mine, axis=0, keepdims=False)
    slot_member = jnp.dot(my_selection, member.astype(bf16), preferred_element_type=f32)
    own = (experts == mine)[None, :]
    own_logit = jnp.sum(jnp.where(own, logits, 0.0), axis=1)
    other_logit = jnp.sum(jnp.where(own, 0.0, slot_member * logits), axis=1)
    share = jax.nn.sigmoid(own_logit - other_logit)
    hidden_width = w_gate.shape[2]

    def hidden_of(*parts_of):
        both, at = None, 0
        for part in parts_of:
            piece = jnp.dot(
                normed[:, at : at + part.shape[0]], part, preferred_element_type=f32
            )
            both, at = piece if both is None else both + piece, at + part.shape[0]
        return (jax.nn.silu(both[:, :hidden_width]) * both[:, hidden_width:]).astype(bf16)

    def out_of(hidden, rows_down):
        return jnp.dot(hidden, rows_down, preferred_element_type=f32)

    expert_out = out_of(hidden_of(gate_up), down) + out_of(hidden_of(gate_up_core), down_core)
    second_cross = swapped(after(second_pair, expert_out), "core")
    hidden_pair = hidden_of(first_pair, second_pair)
    down_cross = swapped(after(down_pair, hidden_pair), "core")
    expert_out = expert_out + out_of(hidden_pair, down_pair)
    expert_out = expert_out + out_of(hidden_of(first_cross, second_cross), down_cross)
    weighted = (expert_out * share[:, None]).astype(bf16)
    outgoing = jnp.stack(
        [weighted[:, i * class_width : (i + 1) * class_width] for i in range(rep_count)], axis=0
    )
    returned = exchanged(outgoing, "rep")

    back = jnp.concatenate([selection.reshape(EXPERTS * slot_count, class_rows)] * halves, axis=0)
    mixture = lax.dot_general(
        back,
        returned.reshape(rep_count * slot_count, class_width),
        (((0,), (0,)), ((), ())),
        preferred_element_type=f32,
    ).astype(bf16)
    pieces = exchanged(mixture.reshape(count, tok, class_width), CLASS)
    layer_out = (attended.astype(f32) + jnp.sum(pieces.astype(f32), axis=0)).astype(bf16)
    return (attended, layer_out, keys_cache, values_cache)


def solution(mesh):
    far = mesh.shape["seq"] // (PAIR * CORES)
    split = Mesh(
        mesh.devices.reshape(mesh.shape["groups"], far, PAIR, CORES, mesh.shape["rep"]),
        ("groups", "far", "near", "core", "rep"),
    )
    return jax.shard_map(
        body,
        mesh=split,
        in_specs=(
            P(TOKENS, "rep"),
            P(TOKENS, "rep"),
            P(TOKENS, "rep"),
            P(TOKENS, "rep"),
            P(TOKENS, "rep"),
            P("groups"),
            P(TOKENS, "rep"),
            P(SEQ, "rep"),
            P(),
            P(),
            P("rep", None, SEQ),
            P("rep", None, SEQ),
            P("rep", SEQ, None),
            P(TOKENS, None),
        ),
        out_specs=(
            P(TOKENS, "rep"),
            P(TOKENS, "rep"),
            P(TOKENS, None),
            P(TOKENS, None),
        ),
        check_vma=False,
    )
```

profile of v0, /device:TPU:80, one launch (start us, length us, event | category | flops | bytes accessed | tf_op | source)
XLA Modules:
  0.0 326.2 jit_solution(14526947771714551630)
XLA Ops:
  8.0 0.7 fusion.64
  9.4 41.6 %all-to-all-start = ((bf16[8,16,640]{2,1,0:T(8,128)(2,1)}), bf16[8,16,640]{2,1,0:T(8,128)(2,1)S(1)}, u32[]{:S(2)}, u32[]{:S(2)}) async-start(bf16[8,16,640]{2,1,0:T(8,128)(2,1)} %broadcast_in_dim.132), calls=%async_computation | async-start | bytes 327680 | tf_op jit(solution)/shard_map/all_to_all | solution.py:40
  51.1 0.9 maximum_maximum_fusion
  52.1 5.1 %collective-permute-start = (bf16[272,256]{1,0:T(8,128)(2,1)S(1)}, bf16[272,256]{1,0:T(8,128)(2,1)S(1)}, u32[]{:S(2)}, u32[]{:S(2)}) collective-permute-start(bf16[272,256]{1,0:T(8,128)(2,1)S(1)} %maximum_maximum_fusion), channel_id=1, source_target_pairs={{0,16},{16,0},{1,17},{17,1},{2,18},{18,2},{3,19},{19,3},{4,20},{20... | collective-permute-start | bytes 417800 | tf_op jit(solution)/shard_map/ppermute | solution.py:23
  57.4 0.8 select_reduce_fusion.2
  58.4 0.8 select_reduce_fusion
  59.4 4.5 %collective-permute-done = bf16[272,256]{1,0:T(8,128)(2,1)S(1)} collective-permute-done((bf16[272,256]{1,0:T(8,128)(2,1)S(1)}, bf16[272,256]{1,0:T(8,128)(2,1)S(1)}, u32[]{:S(2)}, u32[]{:S(2)}) %collective-permute-start) | collective-permute-done | bytes 139296 | tf_op jit(solution)/shard_map/ppermute | solution.py:23
  63.9 0.9 pad_maximum_fusion.3
  64.9 2.0 collective-permute-start.1
  67.1 1.3 collective-permute-done.1
  68.4 0.9 pad_maximum_fusion.2
  71.0 26.8 %all_to_all.35 = bf16[8,16,640]{2,1,0:T(8,128)(2,1)S(1)} all-to-all(bf16[8,16,640]{2,1,0:T(8,128)(2,1)S(1)} %bitcast.249), channel_id=1, replica_groups=mesh['groups'=2,'far'=8,'near'=2,'core'=2,'rep'=8] {'far'}, dimensions={0} | all-to-all | bytes 327680 | tf_op jit(solution)/shard_map/all_to_all | solution.py:40
  99.6 7.7 %all-to-all-start.2 = ((bf16[8,16,768]{2,1,0:T(8,128)(2,1)}), bf16[8,16,768]{2,1,0:T(8,128)(2,1)S(1)}, u32[]{:S(2)}, u32[]{:S(2)}) async-start(bf16[8,16,768]{2,1,0:T(8,128)(2,1)} %broadcast_in_dim.134), calls=%async_computation.2 | async-start | bytes 393216 | tf_op jit(solution)/shard_map/all_to_all | solution.py:40
  107.4 30.9 %all-gather.2.cloned.1.call-done = bf16[2048,512]{1,0:T(8,128)(2,1)} async-done(((bf16[128,512]{1,0:T(8,128)(2,1)}), bf16[2048,512]{1,0:T(8,128)(2,1)}) %all-gather.2.cloned.1.call-update) | async-done | bytes 2097168 | tf_op jit(solution)/shard_map/all_gather | solution.py:104
  138.3 1.9 collective-permute-start.2
  140.4 2.0 fusion.36
  142.4 2.1 collective-permute-done.2
  145.6 6.7 %all-to-all-start.3 = ((bf16[8,16,512]{2,1,0:T(8,128)(2,1)}), bf16[8,16,512]{2,1,0:T(8,128)(2,1)S(1)}, u32[]{:S(2)}, u32[]{:S(2)}) async-start(bf16[8,16,512]{2,1,0:T(8,128)(2,1)} %broadcast_in_dim.136), calls=%async_computation.3 | async-start | bytes 262144 | tf_op jit(solution)/shard_map/all_to_all | solution.py:40
  152.8 15.6 %all-to-all-done.3 = bf16[8,16,512]{2,1,0:T(8,128)(2,1)S(1)} async-done(((bf16[8,16,512]{2,1,0:T(8,128)(2,1)}), bf16[8,16,512]{2,1,0:T(8,128)(2,1)S(1)}, u32[]{:S(2)}, u32[]{:S(2)}) %all-to-all-start.3) | async-done | bytes 131104 | tf_op jit(solution)/shard_map/all_to_all | solution.py:40
  168.6 0.9 pad_maximum_fusion.1
  169.5 7.3 %all-to-all-start.4 = ((bf16[8,96,512]{2,1,0:T(8,128)(2,1)}), bf16[8,96,512]{2,1,0:T(8,128)(2,1)S(1)}, u32[]{:S(2)}, u32[]{:S(2)}) async-start(bf16[8,96,512]{2,1,0:T(8,128)(2,1)} %pad_maximum_fusion.1), calls=%async_computation.4 | async-start | bytes 1572864 | tf_op jit(solution)/shard_map/all_to_all | solution.py:40
  176.8 1.2 fusion.9
  178.0 2.3 collective-permute-start.5
  180.3 1.6 pad_maximum_fusion
  181.9 1.9 collective-permute-start.3
  183.9 2.4 collective-permute-start.4
  186.3 1.1 fusion.18
  187.4 17.7 %collective-permute-done.5 = bf16[2304,256]{1,0:T(8,128)(2,1)} collective-permute-done((bf16[2304,256]{1,0:T(8,128)(2,1)}, bf16[2304,256]{1,0:T(8,128)(2,1)}, u32[]{:S(2)}, u32[]{:S(2)}) %collective-permute-start.5) | collective-permute-done | bytes 1179680 | tf_op jit(solution)/shard_map/ppermute | solution.py:23
  205.1 1.9 collective-permute-start.8
  207.1 3.0 collective-permute-start.6
  210.1 2.9 collective-permute-start.7
  214.1 1.6 fusion.56
  215.7 2.1 fusion.95
  217.8 1.6 convolution_add_fusion.1
  219.4 13.2 %collective-permute-done.6 = bf16[1792,256]{1,0:T(8,128)(2,1)} collective-permute-done((bf16[1792,256]{1,0:T(8,128)(2,1)}, bf16[1792,256]{1,0:T(8,128)(2,1)}, u32[]{:S(2)}, u32[]{:S(2)}) %collective-permute-start.6) | collective-permute-done | bytes 917536 | tf_op jit(solution)/shard_map/ppermute | solution.py:23
  232.6 1.9 collective-permute-start.9
  234.5 1.5 fusion.26
  236.0 1.6 convolution_add_fusion.3
  237.6 16.9 %collective-permute-done.7 = bf16[128,4096]{1,0:T(8,128)(2,1)} collective-permute-done((bf16[128,4096]{1,0:T(8,128)(2,1)}, bf16[128,4096]{1,0:T(8,128)(2,1)}, u32[]{:S(2)}, u32[]{:S(2)}) %collective-permute-start.7) | collective-permute-done | bytes 1048608 | tf_op jit(solution)/shard_map/ppermute | solution.py:23
  254.6 1.9 collective-permute-start.10
  256.5 0.7 select_reduce_fusion.1
  257.9 1.6 convolution_add_fusion.2
  259.9 1.6 fusion.2
  266.6 6.9 %all-to-all-start.5 = ((bf16[8,96,512]{2,1,0:T(8,128)(2,1)}), bf16[8,96,512]{2,1,0:T(8,128)(2,1)S(1)}, u32[]{:S(2)}, u32[]{:S(2)}) async-start(bf16[8,96,512]{2,1,0:T(8,128)(2,1)} %constant_dynamic-update-slice_fusion.35), calls=%async_computation.5 | async-start | bytes 1572864 | tf_op jit(solution)/shard_map/all_to_all | solution.py:40
  273.8 23.5 %all-to-all-done.5 = bf16[8,96,512]{2,1,0:T(8,128)(2,1)S(1)} async-done(((bf16[8,96,512]{2,1,0:T(8,128)(2,1)}), bf16[8,96,512]{2,1,0:T(8,128)(2,1)S(1)}, u32[]{:S(2)}, u32[]{:S(2)}) %all-to-all-start.5) | async-done | bytes 786464 | tf_op jit(solution)/shard_map/all_to_all | solution.py:40
  297.4 0.9 convolution_convert_fusion.1
  298.3 4.5 %all-to-all-start.6 = ((bf16[8,16,512]{2,1,0:T(8,128)(2,1)}), bf16[8,16,512]{2,1,0:T(8,128)(2,1)S(1)}, u32[]{:S(2)}, u32[]{:S(2)}) async-start(bf16[8,16,512]{2,1,0:T(8,128)(2,1)} %bitcast.58), calls=%async_computation.6 | async-start | bytes 262144 | tf_op jit(solution)/shard_map/all_to_all | solution.py:40
  302.9 15.8 %all-to-all-done.6 = bf16[8,16,512]{2,1,0:T(8,128)(2,1)S(1)} async-done(((bf16[8,16,512]{2,1,0:T(8,128)(2,1)}), bf16[8,16,512]{2,1,0:T(8,128)(2,1)S(1)}, u32[]{:S(2)}, u32[]{:S(2)}) %all-to-all-start.6) | async-done | bytes 131104 | tf_op jit(solution)/shard_map/all_to_all | solution.py:40
  (133 shorter events, 15.5 us)
Async XLA Ops:
  7.2 249.3 %copy-start = (f32[4096,4]{0,1:T(4,128)S(1)}, f32[4096,4]{0,1:T(4,128)}, u32[]{:S(2)}) copy-start(f32[4096,4]{0,1:T(4,128)} %param.23) | copy-start | bytes 196612
  9.4 59.9 %all-to-all-start = ((bf16[8,16,640]{2,1,0:T(8,128)(2,1)}), bf16[8,16,640]{2,1,0:T(8,128)(2,1)S(1)}, u32[]{:S(2)}, u32[]{:S(2)}) async-start(bf16[8,16,640]{2,1,0:T(8,128)(2,1)} %broadcast_in_dim.132), calls=%async_computation | async-start | bytes 327680 | tf_op jit(solution)/shard_map/all_to_all | solution.py:40
  51.1 87.2 %all-gather.2.cloned.1.call-start = ((), (), s32[]{:S(2)}) async-start(), calls=%async_computation.7 | async-start | bytes 2228224 | tf_op jit(solution)/shard_map/all_gather | solution.py:104
  52.1 11.9 %collective-permute-start = (bf16[272,256]{1,0:T(8,128)(2,1)S(1)}, bf16[272,256]{1,0:T(8,128)(2,1)S(1)}, u32[]{:S(2)}, u32[]{:S(2)}) collective-permute-start(bf16[272,256]{1,0:T(8,128)(2,1)S(1)} %maximum_maximum_fusion), channel_id=1, source_target_pairs={{0,16},{16,0},{1,17},{17,1},{2,18},{18,2},{3,19},{19,3},{4,20},{20... | collective-permute-start | bytes 417800 | tf_op jit(solution)/shard_map/ppermute | solution.py:23
  64.9 3.5 %collective-permute-start.1 = (bf16[544,256]{1,0:T(8,128)(2,1)S(1)}, bf16[544,256]{1,0:T(8,128)(2,1)S(1)}, u32[]{:S(2)}, u32[]{:S(2)}) collective-permute-start(bf16[544,256]{1,0:T(8,128)(2,1)S(1)} %pad_maximum_fusion.3), channel_id=1, source_target_pairs={{0,8},{8,0},{1,9},{9,1},{2,10},{10,2},{3,11},{11,3},{4,12},{12,4},... | collective-permute-start | bytes 835592 | tf_op jit(solution)/shard_map/ppermute | solution.py:23
  70.2 28.7 %copy-start.4 = (bf16[16,128]{1,0:T(8,128)(2,1)S(1)}, bf16[16,128]{1,0:T(8,128)(2,1)}, u32[]{:S(2)}) copy-start(bf16[16,128]{1,0:T(8,128)(2,1)} %param.15) | copy-start | bytes 12292
  70.2 28.7 %copy-start.5 = (bf16[16,128]{1,0:T(8,128)(2,1)S(1)}, bf16[16,128]{1,0:T(8,128)(2,1)}, u32[]{:S(2)}) copy-start(bf16[16,128]{1,0:T(8,128)(2,1)} %param.16) | copy-start | bytes 12292
  99.6 40.6 %all-to-all-start.2 = ((bf16[8,16,768]{2,1,0:T(8,128)(2,1)}), bf16[8,16,768]{2,1,0:T(8,128)(2,1)S(1)}, u32[]{:S(2)}, u32[]{:S(2)}) async-start(bf16[8,16,768]{2,1,0:T(8,128)(2,1)} %broadcast_in_dim.134), calls=%async_computation.2 | async-start | bytes 393216 | tf_op jit(solution)/shard_map/all_to_all | solution.py:40
  107.4 37.2 %copy-start.6 = (bf16[16,512]{1,0:T(8,128)(2,1)S(1)}, bf16[16,512]{1,0:T(8,128)(2,1)}, u32[]{:S(2)}) copy-start(bf16[16,512]{1,0:T(8,128)(2,1)} %param.20) | copy-start | bytes 49156
  138.3 6.3 %collective-permute-start.2 = (bf16[2048,512]{1,0:T(8,128)(2,1)}, bf16[2048,512]{1,0:T(8,128)(2,1)S(1)}, u32[]{:S(2)}, u32[]{:S(2)}) collective-permute-start(bf16[2048,512]{1,0:T(8,128)(2,1)} %all-gather.2.cloned.1.call-done), channel_id=1, source_target_pairs={{0,8},{8,0},{1,9},{9,1},{2,10},{10,2},{3,11},{11,3},{4,12},{12,4},... | collective-permute-start | bytes 6291464 | tf_op jit(solution)/shard_map/ppermute | solution.py:23
  144.9 173.8 %copy-start.3 = (bf16[16,512]{1,0:T(8,128)(2,1)}, bf16[16,512]{1,0:T(8,128)(2,1)S(1)}, u32[]{:S(2)}) copy-start(bf16[16,512]{1,0:T(8,128)(2,1)S(1)} %fusion.13) | copy-start | bytes 49156
  145.6 22.8 %all-to-all-start.3 = ((bf16[8,16,512]{2,1,0:T(8,128)(2,1)}), bf16[8,16,512]{2,1,0:T(8,128)(2,1)S(1)}, u32[]{:S(2)}, u32[]{:S(2)}) async-start(bf16[8,16,512]{2,1,0:T(8,128)(2,1)} %broadcast_in_dim.136), calls=%async_computation.3 | async-start | bytes 262144 | tf_op jit(solution)/shard_map/all_to_all | solution.py:40
  152.3 24.6 %copy-start.1 = (bf16[1,4096,128]{2,1,0:T(8,128)(2,1)S(1)}, bf16[1,4096,128]{2,1,0:T(8,128)(2,1)}, u32[]{:S(2)}) copy-start(bf16[1,4096,128]{2,1,0:T(8,128)(2,1)} %param.24) | copy-start | bytes 3145732
  152.3 24.6 %copy-start.2 = (bf16[1,4096,128]{2,1,0:T(8,128)(2,1)S(1)}, bf16[1,4096,128]{2,1,0:T(8,128)(2,1)}, u32[]{:S(2)}) copy-start(bf16[1,4096,128]{2,1,0:T(8,128)(2,1)} %param.25) | copy-start | bytes 3145732
  169.5 43.5 %all-to-all-start.4 = ((bf16[8,96,512]{2,1,0:T(8,128)(2,1)}), bf16[8,96,512]{2,1,0:T(8,128)(2,1)S(1)}, u32[]{:S(2)}, u32[]{:S(2)}) async-start(bf16[8,96,512]{2,1,0:T(8,128)(2,1)} %pad_maximum_fusion.1), calls=%async_computation.4 | async-start | bytes 1572864 | tf_op jit(solution)/shard_map/all_to_all | solution.py:40
  178.0 27.1 %collective-permute-start.5 = (bf16[2304,256]{1,0:T(8,128)(2,1)}, bf16[2304,256]{1,0:T(8,128)(2,1)}, u32[]{:S(2)}, u32[]{:S(2)}) collective-permute-start(bf16[2304,256]{1,0:T(8,128)(2,1)} %fusion.9), channel_id=1, source_target_pairs={{0,16},{16,0},{1,17},{17,1},{2,18},{18,2},{3,19},{19,3},{4,20},{20... | collective-permute-start | bytes 3538952 | tf_op jit(solution)/shard_map/ppermute | solution.py:23
  181.9 33.8 %collective-permute-start.3 = (bf16[4096,256]{1,0:T(8,128)(2,1)}, bf16[4096,256]{1,0:T(8,128)(2,1)}, u32[]{:S(2)}, u32[]{:S(2)}) collective-permute-start(bf16[4096,256]{1,0:T(8,128)(2,1)} %pad_maximum_fusion), channel_id=1, source_target_pairs={{0,8},{8,0},{1,9},{9,1},{2,10},{10,2},{3,11},{11,3},{4,12},{12,4},... | collective-permute-start | bytes 6291464 | tf_op jit(solution)/shard_map/ppermute | solution.py:23
  183.9 33.9 %collective-permute-start.4 = (bf16[128,4096]{1,0:T(8,128)(2,1)}, bf16[128,4096]{1,0:T(8,128)(2,1)}, u32[]{:S(2)}, u32[]{:S(2)}) collective-permute-start(bf16[128,4096]{1,0:T(8,128)(2,1)} %bitcast.47), channel_id=1, source_target_pairs={{0,8},{8,0},{1,9},{9,1},{2,10},{10,2},{3,11},{11,3},{4,12},{12,4},... | collective-permute-start | bytes 3145736 | tf_op jit(solution)/shard_map/ppermute | solution.py:23
  187.4 26.0 %copy-start.7 = (f32[4096]{0:T(1024)S(1)}, f32[4096]{0:T(1024)}, u32[]{:S(2)}) copy-start(f32[4096]{0:T(1024)} %param.22) | copy-start | bytes 49156
  205.1 52.7 %collective-permute-start.8 = (bf16[2304,256]{1,0:T(8,128)(2,1)}, bf16[2304,256]{1,0:T(8,128)(2,1)}, u32[]{:S(2)}, u32[]{:S(2)}) collective-permute-start(bf16[2304,256]{1,0:T(8,128)(2,1)} %collective-permute-done.5), channel_id=1, source_target_pairs={{0,8},{8,0},{1,9},{9,1},{2,10},{10,2},{3,11},{11,3},{4,12},{12,4},... | collective-permute-start | bytes 3538952 | tf_op jit(solution)/shard_map/ppermute | solution.py:23
  207.1 25.5 %collective-permute-start.6 = (bf16[1792,256]{1,0:T(8,128)(2,1)}, bf16[1792,256]{1,0:T(8,128)(2,1)}, u32[]{:S(2)}, u32[]{:S(2)}) collective-permute-start(bf16[1792,256]{1,0:T(8,128)(2,1)} %fusion.18), channel_id=1, source_target_pairs={{0,16},{16,0},{1,17},{17,1},{2,18},{18,2},{3,19},{19,3},{4,20},{20... | collective-permute-start | bytes 2752520 | tf_op jit(solution)/shard_map/ppermute | solution.py:23
  210.1 44.4 %collective-permute-start.7 = (bf16[128,4096]{1,0:T(8,128)(2,1)}, bf16[128,4096]{1,0:T(8,128)(2,1)}, u32[]{:S(2)}, u32[]{:S(2)}) collective-permute-start(bf16[128,4096]{1,0:T(8,128)(2,1)} %bitcast.47), channel_id=1, source_target_pairs={{0,16},{16,0},{1,17},{17,1},{2,18},{18,2},{3,19},{19,3},{4,20},{20... | collective-permute-start | bytes 3145736 | tf_op jit(solution)/shard_map/ppermute | solution.py:23
  232.6 25.0 %collective-permute-start.9 = (bf16[1792,256]{1,0:T(8,128)(2,1)}, bf16[1792,256]{1,0:T(8,128)(2,1)S(1)}, u32[]{:S(2)}, u32[]{:S(2)}) collective-permute-start(bf16[1792,256]{1,0:T(8,128)(2,1)} %collective-permute-done.6), channel_id=1, source_target_pairs={{0,8},{8,0},{1,9},{9,1},{2,10},{10,2},{3,11},{11,3},{4,12},{12,4},... | collective-permute-start | bytes 2752520 | tf_op jit(solution)/shard_map/ppermute | solution.py:23
  254.6 4.9 %collective-permute-start.10 = (bf16[128,4096]{1,0:T(8,128)(2,1)}, bf16[128,4096]{1,0:T(8,128)(2,1)S(1)}, u32[]{:S(2)}, u32[]{:S(2)}) collective-permute-start(bf16[128,4096]{1,0:T(8,128)(2,1)} %collective-permute-done.7), channel_id=1, source_target_pairs={{0,8},{8,0},{1,9},{9,1},{2,10},{10,2},{3,11},{11,3},{4,12},{12,4},... | collective-permute-start | bytes 3145736 | tf_op jit(solution)/shard_map/ppermute | solution.py:23
  266.6 30.8 %all-to-all-start.5 = ((bf16[8,96,512]{2,1,0:T(8,128)(2,1)}), bf16[8,96,512]{2,1,0:T(8,128)(2,1)S(1)}, u32[]{:S(2)}, u32[]{:S(2)}) async-start(bf16[8,96,512]{2,1,0:T(8,128)(2,1)} %constant_dynamic-update-slice_fusion.35), calls=%async_computation.5 | async-start | bytes 1572864 | tf_op jit(solution)/shard_map/all_to_all | solution.py:40
  298.3 20.4 %all-to-all-start.6 = ((bf16[8,16,512]{2,1,0:T(8,128)(2,1)}), bf16[8,16,512]{2,1,0:T(8,128)(2,1)S(1)}, u32[]{:S(2)}, u32[]{:S(2)}) async-start(bf16[8,16,512]{2,1,0:T(8,128)(2,1)} %bitcast.58), calls=%async_computation.6 | async-start | bytes 262144 | tf_op jit(solution)/shard_map/all_to_all | solution.py:40
  302.9 16.5 %copy-start.8 = (bf16[16,1024]{1,0:T(8,128)(2,1)}, bf16[16,1024]{1,0:T(8,128)(2,1)S(1)}, u32[]{:S(2)}) copy-start(bf16[16,1024]{1,0:T(8,128)(2,1)S(1)} %get-tuple-element.30) | copy-start | bytes 98308
  302.9 16.5 %copy-start.9 = (bf16[16,1024]{1,0:T(8,128)(2,1)}, bf16[16,1024]{1,0:T(8,128)(2,1)S(1)}, u32[]{:S(2)}) copy-start(bf16[16,1024]{1,0:T(8,128)(2,1)S(1)} %get-tuple-element.31) | copy-start | bytes 98308
Sparse Core Ops, SparseCore 0:
  57.4 80.8 all-gather.1
where the time goes:
time: 328 us; the launch traced here: 326 us
  waiting for transfers between devices  142 us (43%)
  starting transfers between devices  102 us (31%)
  blocking collectives  26.8 us (8%)
  matrix products  18.5 us (6%)
  between operations  14.9 us (5%)
  other arithmetic  13.5 us (4%)
  local copies, waits for them, and re-layouts  8.63 us (3%)
    all_to_all x6, starting transfers between devices, exchanged(): return lax.all_to_all(tiles, axis, 0, 0, tiled=True)  74.8 us
    ppermute x11, waiting for transfers between devices, swapped(): return lax.ppermute(array, axis, [(0, 1), (1, 0)])  55.8 us
    all_to_all x6, waiting for transfers between devices, exchanged(): return lax.all_to_all(tiles, axis, 0, 0, tiled=True)  55 us
    all_gather x1, waiting for transfers between devices, body(): out_proj_own = lax.all_gather(out_proj, ('far', 'near'), axis=0, tiled=True)  30.9 us
    ppermute x11, starting transfers between devices, swapped(): return lax.ppermute(array, axis, [(0, 1), (1, 0)])  27.4 us
    all_to_all x1, blocking collectives, exchanged(): return lax.all_to_all(tiles, axis, 0, 0, tiled=True)  26.8 us
    dot_general x6, matrix products, hidden_of(): jnp.dot(normed[:, at:at + part.shape[0]], part, preferred_element_type=f32)  7.5 us
  transfers between devices with their start and end apart: 18, of which 10 were waited for; matrix products, arithmetic and copies ran while one was open for 8% of the time, Pallas kernels for 0%

commit v1 on v0

--- a/solution.py
+++ b/solution.py
@@ -1,8 +1,11 @@
+import functools
 import math
 
 import jax
 import jax.numpy as jnp
 from jax import lax
+from jax.experimental import pallas as pl
+from jax.experimental.pallas import tpu as pltpu
 from jax.sharding import Mesh
 from jax.sharding import PartitionSpec as P
 
@@ -63,6 +66,80 @@
         place[axis] = index % sizes[axis]
         index = index // sizes[axis]
     return (place["far"] * sizes["near"] + place["near"]) * sizes["core"] + place["core"]
+
+
+def expert_kernel(cuts, final, *refs):
+    parts = sum(len(c) for c in cuts)
+    x_ref, refs = refs[0], refs[1:]
+    if final:
+        before_ref, share_ref, refs = refs[0], refs[1], refs[2:]
+    gu_refs, refs = refs[:parts], refs[parts:]
+    down_refs, refs = refs[: len(cuts)], refs[len(cuts) :]
+    out_ref, gu_held, down_held, gu_sem, down_sem = refs
+    width = down_refs[0].shape[0]
+    copies, k = [], 0
+    for d, cut in enumerate(cuts):
+        at = 0
+        for size in cut:
+            copy = pltpu.make_async_copy(
+                gu_refs[k], gu_held.at[d, pl.ds(at, size)], gu_sem.at[k]
+            )
+            copy.start()
+            copies.append(copy)
+            at, k = at + size, k + 1
+    down_copies = []
+    for d in range(len(cuts)):
+        copy = pltpu.make_async_copy(
+            down_refs[d], down_held.at[pl.ds(d * width, width)], down_sem.at[d]
+        )
+        copy.start()
+        down_copies.append(copy)
+    hidden, k = [], 0
+    for d, cut in enumerate(cuts):
+        both, at = None, 0
+        for size in cut:
+            copies[k].wait()
+            piece = jnp.dot(
+                x_ref[:, at : at + size],
+                gu_held[d, at : at + size, :],
+                preferred_element_type=jnp.float32,
+            )
+            both = piece if both is None else both + piece
+            at, k = at + size, k + 1
+        gate, up = both[:, :width], both[:, width:]
+        hidden.append((gate * jax.nn.sigmoid(gate) * up).astype(jnp.bfloat16))
+    hidden = jnp.concatenate(hidden, axis=1)
+    for copy in down_copies:
+        copy.wait()
+    if final:
+        tiles, _, columns = out_ref.shape
+        for i in range(tiles):
+            span = slice(i * columns, (i + 1) * columns)
+            piece = jnp.dot(hidden, down_held[:, span], preferred_element_type=jnp.float32)
+            out_ref[i] = ((before_ref[:, span] + piece) * share_ref[...]).astype(out_ref.dtype)
+    else:
+        out_ref[...] = jnp.dot(hidden, down_held[...], preferred_element_type=jnp.float32)
+
+
+def expert_call(x, gate_ups, downs, out_shape, before=None, share=None):
+    cuts = tuple(tuple(g.shape[0] for g in parts) for parts in gate_ups)
+    flat = [g for parts in gate_ups for g in parts]
+    final = before is not None
+    extra = [before, share] if final else []
+    vmem = pl.BlockSpec(memory_space=pltpu.VMEM)
+    anywhere = pl.BlockSpec(memory_space=pl.ANY)
+    return pl.pallas_call(
+        functools.partial(expert_kernel, cuts, final),
+        out_shape=out_shape,
+        in_specs=[vmem] * (1 + len(extra)) + [anywhere] * (len(flat) + len(downs)),
+        out_specs=vmem,
+        scratch_shapes=[
+            pltpu.VMEM((len(cuts), sum(cuts[0]), flat[0].shape[1]), flat[0].dtype),
+            pltpu.VMEM((len(downs) * downs[0].shape[0], downs[0].shape[1]), downs[0].dtype),
+            pltpu.SemaphoreType.DMA((len(flat),)),
+            pltpu.SemaphoreType.DMA((len(downs),)),
+        ],
+    )(x, *extra, *flat, *downs)
 
 
 def body(
@@ -221,29 +298,21 @@
     own_logit = jnp.sum(jnp.where(own, logits, 0.0), axis=1)
     other_logit = jnp.sum(jnp.where(own, 0.0, slot_member * logits), axis=1)
     share = jax.nn.sigmoid(own_logit - other_logit)
-    hidden_width = w_gate.shape[2]
-
-    def hidden_of(*parts_of):
-        both, at = None, 0
-        for part in parts_of:
-            piece = jnp.dot(
-                normed[:, at : at + part.shape[0]], part, preferred_element_type=f32
-            )
-            both, at = piece if both is None else both + piece, at + part.shape[0]
-        return (jax.nn.silu(both[:, :hidden_width]) * both[:, hidden_width:]).astype(bf16)
-
-    def out_of(hidden, rows_down):
-        return jnp.dot(hidden, rows_down, preferred_element_type=f32)
-
-    expert_out = out_of(hidden_of(gate_up), down) + out_of(hidden_of(gate_up_core), down_core)
-    second_cross = swapped(after(second_pair, expert_out), "core")
-    hidden_pair = hidden_of(first_pair, second_pair)
-    down_cross = swapped(after(down_pair, hidden_pair), "core")
-    expert_out = expert_out + out_of(hidden_pair, down_pair)
-    expert_out = expert_out + out_of(hidden_of(first_cross, second_cross), down_cross)
-    weighted = (expert_out * share[:, None]).astype(bf16)
-    outgoing = jnp.stack(
-        [weighted[:, i * class_width : (i + 1) * class_width] for i in range(rep_count)], axis=0
+    near_out = expert_call(
+        normed,
+        ((gate_up,), (gate_up_core,)),
+        (down, down_core),
+        jax.ShapeDtypeStruct((slot_count, model), f32),
+    )
+    second_cross = swapped(after(second_pair, near_out), "core")
+    down_cross = swapped(after(down_pair, near_out), "core")
+    outgoing = expert_call(
+        normed,
+        ((first_pair, second_pair), (first_cross, second_cross)),
+        (down_pair, down_cross),
+        jax.ShapeDtypeStruct((rep_count, slot_count, class_width), bf16),
+        before=near_out,
+        share=share[:, None],
     )
     returned = exchanged(outgoing, "rep")
 

time: 328 us -> 327 us (level)
  matrix products: 18.5 us -> 5.77 us
  Pallas kernels: 0 us -> 12.3 us
  local copies, waits for them, and re-layouts: 8.63 us -> 5.31 us
    dot_general x10 -> x0, matrix products: 12.7 us -> none  [the longest x6 7.5 us: hidden_of(): jnp.dot(normed[:, at:at + part.shape[0]], part, preferred_element_type=f32)]
    pallas_call x0 -> x2, Pallas kernels: none -> 12.3 us  [expert_call(): pl.pallas_call(functools.partial(expert_kernel, cuts, final), out_shape=o...]
    unnamed x47 -> x46, local copies, waits for them, and re-layouts: 4.81 us -> 1.4 us
  transfers between devices with their start and end apart: 18 -> 18, of which waited for: 10 -> 11; matrix products, arithmetic and copies ran while one was open for 8% -> 5% of each run, Pallas kernels for 0% -> 2%
where the time goes in v1:
time: 327 us; the launch traced here: 326 us
  waiting for transfers between devices  144 us (44%)
  starting transfers between devices  103 us (31%)
  blocking collectives  26.8 us (8%)
  between operations  14.8 us (5%)
  other arithmetic  13.3 us (4%)
  Pallas kernels  12.3 us (4%)
  matrix products  5.77 us (2%)
  local copies, waits for them, and re-layouts  5.31 us (2%)
    all_to_all x6, starting transfers between devices, exchanged(): return lax.all_to_all(tiles, axis, 0, 0, tiled=True)  75.4 us
    ppermute x11, waiting for transfers between devices, swapped(): return lax.ppermute(array, axis, [(0, 1), (1, 0)])  57.5 us
    all_to_all x6, waiting for transfers between devices, exchanged(): return lax.all_to_all(tiles, axis, 0, 0, tiled=True)  55.7 us
    all_gather x1, waiting for transfers between devices, body(): out_proj_own = lax.all_gather(out_proj, ('far', 'near'), axis=0, tiled=True)  30.8 us
    ppermute x11, starting transfers between devices, swapped(): return lax.ppermute(array, axis, [(0, 1), (1, 0)])  27.9 us
    all_to_all x1, blocking collectives, exchanged(): return lax.all_to_all(tiles, axis, 0, 0, tiled=True)  26.8 us
    pallas_call x2, Pallas kernels, expert_call(): pl.pallas_call(functools.partial(expert_kernel, cuts, final), out_shape=o...  12.3 us
  transfers between devices with their start and end apart: 18, of which 11 were waited for; matrix products, arithmetic and copies ran while one was open for 5% of the time, Pallas kernels for 2%

profile of v1, /device:TPU:80, one launch (start us, length us, event | category | flops | bytes accessed | tf_op | source)
XLA Modules:
  0.0 325.6 jit_solution(5600991606307095967)
XLA Ops:
  7.2 0.7 convert_element_type.126
  8.0 0.7 fusion.43
  9.4 41.6 %all-to-all-start = ((bf16[8,16,640]{2,1,0:T(8,128)(2,1)}), bf16[8,16,640]{2,1,0:T(8,128)(2,1)S(1)}, u32[]{:S(2)}, u32[]{:S(2)}) async-start(bf16[8,16,640]{2,1,0:T(8,128)(2,1)} %broadcast_in_dim.132), calls=%async_computation | async-start | bytes 327680 | tf_op jit(solution)/shard_map/all_to_all | solution.py:43
  51.1 0.9 maximum_maximum_fusion
  52.1 5.1 %collective-permute-start = (bf16[272,256]{1,0:T(8,128)(2,1)S(1)}, bf16[272,256]{1,0:T(8,128)(2,1)S(1)}, u32[]{:S(2)}, u32[]{:S(2)}) collective-permute-start(bf16[272,256]{1,0:T(8,128)(2,1)S(1)} %maximum_maximum_fusion), channel_id=1, source_target_pairs={{0,16},{16,0},{1,17},{17,1},{2,18},{18,2},{3,19},{19,3},{4,20},{20... | collective-permute-start | bytes 417800 | tf_op jit(solution)/shard_map/ppermute | solution.py:26
  57.4 0.8 select_reduce_fusion.2
  58.4 0.8 select_reduce_fusion
  59.4 4.5 %collective-permute-done = bf16[272,256]{1,0:T(8,128)(2,1)S(1)} collective-permute-done((bf16[272,256]{1,0:T(8,128)(2,1)S(1)}, bf16[272,256]{1,0:T(8,128)(2,1)S(1)}, u32[]{:S(2)}, u32[]{:S(2)}) %collective-permute-start) | collective-permute-done | bytes 139296 | tf_op jit(solution)/shard_map/ppermute | solution.py:26
  63.9 0.9 pad_maximum_fusion.3
  64.9 2.0 collective-permute-start.1
  67.1 1.3 collective-permute-done.1
  68.4 0.9 pad_maximum_fusion.2
  71.0 26.8 %all_to_all.35 = bf16[8,16,640]{2,1,0:T(8,128)(2,1)S(1)} all-to-all(bf16[8,16,640]{2,1,0:T(8,128)(2,1)S(1)} %bitcast.204), channel_id=1, replica_groups=mesh['groups'=2,'far'=8,'near'=2,'core'=2,'rep'=8] {'far'}, dimensions={0} | all-to-all | bytes 327680 | tf_op jit(solution)/shard_map/all_to_all | solution.py:43
  98.9 0.7 broadcast_in_dim.134
  99.6 7.9 %all-to-all-start.2 = ((bf16[8,16,768]{2,1,0:T(8,128)(2,1)}), bf16[8,16,768]{2,1,0:T(8,128)(2,1)S(1)}, u32[]{:S(2)}, u32[]{:S(2)}) async-start(bf16[8,16,768]{2,1,0:T(8,128)(2,1)} %broadcast_in_dim.134), calls=%async_computation.2 | async-start | bytes 393216 | tf_op jit(solution)/shard_map/all_to_all | solution.py:43
  107.5 30.8 %all-gather.2.cloned.1.call-done = bf16[2048,512]{1,0:T(8,128)(2,1)} async-done(((bf16[128,512]{1,0:T(8,128)(2,1)}), bf16[2048,512]{1,0:T(8,128)(2,1)}) %all-gather.2.cloned.1.call-update) | async-done | bytes 2097168 | tf_op jit(solution)/shard_map/all_gather | solution.py:181
  138.3 1.9 collective-permute-start.2
  140.4 2.0 fusion.27
  142.4 2.1 collective-permute-done.2
  145.6 6.8 %all-to-all-start.3 = ((bf16[8,16,512]{2,1,0:T(8,128)(2,1)}), bf16[8,16,512]{2,1,0:T(8,128)(2,1)S(1)}, u32[]{:S(2)}, u32[]{:S(2)}) async-start(bf16[8,16,512]{2,1,0:T(8,128)(2,1)} %broadcast_in_dim.136), calls=%async_computation.3 | async-start | bytes 262144 | tf_op jit(solution)/shard_map/all_to_all | solution.py:43
  152.9 15.6 %all-to-all-done.3 = bf16[8,16,512]{2,1,0:T(8,128)(2,1)S(1)} async-done(((bf16[8,16,512]{2,1,0:T(8,128)(2,1)}), bf16[8,16,512]{2,1,0:T(8,128)(2,1)S(1)}, u32[]{:S(2)}, u32[]{:S(2)}) %all-to-all-start.3) | async-done | bytes 131104 | tf_op jit(solution)/shard_map/all_to_all | solution.py:43
  168.8 0.9 pad_maximum_fusion.1
  169.7 7.2 %all-to-all-start.4 = ((bf16[8,96,512]{2,1,0:T(8,128)(2,1)}), bf16[8,96,512]{2,1,0:T(8,128)(2,1)S(1)}, u32[]{:S(2)}, u32[]{:S(2)}) async-start(bf16[8,96,512]{2,1,0:T(8,128)(2,1)} %pad_maximum_fusion.1), calls=%async_computation.4 | async-start | bytes 1572864 | tf_op jit(solution)/shard_map/all_to_all | solution.py:43
  177.1 2.8 collective-permute-start.5
  179.9 1.6 pad_maximum_fusion.refs_1_
  181.5 1.9 collective-permute-start.3
  183.4 2.4 collective-permute-start.4
  185.9 1.1 fusion.15
  186.9 16.6 %collective-permute-done.5.refs_3_ = bf16[2304,256]{1,0:T(8,128)(2,1)} collective-permute-done((bf16[2304,256]{1,0:T(8,128)(2,1)S(1)}, bf16[2304,256]{1,0:T(8,128)(2,1)}, u32[]{:S(2)}, u32[]{:S(2)}) %collective-permute-start.5) | collective-permute-done | bytes 1179680 | tf_op jit(solution)/shard_map/ppermute | solution.py:26
  203.5 1.9 collective-permute-start.7
  205.5 3.6 %collective-permute-start.9 = (bf16[128,4096]{1,0:T(8,128)(2,1)}, bf16[128,4096]{1,0:T(8,128)(2,1)}, u32[]{:S(2)}, u32[]{:S(2)}) collective-permute-start(bf16[128,4096]{1,0:T(8,128)(2,1)} %bitcast.47.refs_3_), channel_id=1, source_target_pairs={{0,16},{16,0},{1,17},{17,1},{2,18},{18,2},{3,19},{19,3},{4,20},{20... | collective-permute-start | bytes 3145736 | tf_op jit(solution)/shard_map/ppermute | solution.py:26
  209.1 2.3 collective-permute-start.6
  211.8 1.1 fusion.4.refs_0_
  212.9 6.1 %shard_map.165.refs_1_ = f32[96,4096]{1,0:T(8,128)} custom-call(bf16[96,4096]{1,0:T(8,128)(2,1)} %fusion.4.refs_0_, bf16[4096,256]{1,0:T(8,128)(2,1)} %pad_maximum_fusion.refs_1_, bf16[4096,256]{1,0:T(8,128)(2,1)} %collective-permute-done.3.refs_2_, bf16[128,4096]{1,0:T(8,128)(2,1)} %bitcast.47.refs_3_, bf16[128,4096]{1,0:T(8,128)(2,1)} %collective-permute-done.4.refs_4_), custom_call_target="tpu_custom_call" | custom-call | tf_op jit(solution)/shard_map/pallas_call | solution.py:131
  219.1 14.7 %collective-permute-done.9.refs_7_ = bf16[128,4096]{1,0:T(8,128)(2,1)} collective-permute-done((bf16[128,4096]{1,0:T(8,128)(2,1)}, bf16[128,4096]{1,0:T(8,128)(2,1)}, u32[]{:S(2)}, u32[]{:S(2)}) %collective-permute-start.9) | collective-permute-done | bytes 1048608 | tf_op jit(solution)/shard_map/ppermute | solution.py:26
  233.8 1.9 collective-permute-start.10
  235.7 17.2 %collective-permute-done.6.refs_4_ = bf16[1792,256]{1,0:T(8,128)(2,1)} collective-permute-done((bf16[1792,256]{1,0:T(8,128)(2,1)}, bf16[1792,256]{1,0:T(8,128)(2,1)}, u32[]{:S(2)}, u32[]{:S(2)}) %collective-permute-start.6) | collective-permute-done | bytes 917536 | tf_op jit(solution)/shard_map/ppermute | solution.py:26
  252.9 1.9 collective-permute-start.8
  254.9 0.7 select_reduce_fusion.1
  256.0 0.7 copy.34.refs_2_
  256.7 1.0 collective-permute-done.8.refs_6_
  257.7 1.0 copy-done.5
  258.7 6.2 %shard_map.166 = bf16[8,96,512]{2,1,0:T(8,128)(2,1)} custom-call(bf16[96,4096]{1,0:T(8,128)(2,1)} %fusion.4.refs_0_, f32[96,4096]{1,0:T(8,128)} %shard_map.165.refs_1_, f32[96,1]{1,0:T(8,128)} %copy.34.refs_2_, bf16[2304,256]{1,0:T(8,128)(2,1)} %collective-permute-done.5.refs_3_, bf16[1792,256]{1,0:T(8,128)(2,1)} %collective-permute-done.6.refs_4_, ...), custom_call_target="tpu_custom_call" | custom-call | tf_op jit(solution)/shard_map/pallas_call | solution.py:131
  264.9 6.9 %all-to-all-start.5 = ((bf16[8,96,512]{2,1,0:T(8,128)(2,1)}), bf16[8,96,512]{2,1,0:T(8,128)(2,1)S(1)}, u32[]{:S(2)}, u32[]{:S(2)}) async-start(bf16[8,96,512]{2,1,0:T(8,128)(2,1)} %shard_map.166), calls=%async_computation.5 | async-start | bytes 1572864 | tf_op jit(solution)/shard_map/all_to_all | solution.py:43
  272.2 23.5 %all-to-all-done.5 = bf16[8,96,512]{2,1,0:T(8,128)(2,1)S(1)} async-done(((bf16[8,96,512]{2,1,0:T(8,128)(2,1)}), bf16[8,96,512]{2,1,0:T(8,128)(2,1)S(1)}, u32[]{:S(2)}, u32[]{:S(2)}) %all-to-all-start.5) | async-done | bytes 786464 | tf_op jit(solution)/shard_map/all_to_all | solution.py:43
  295.7 0.9 convolution_convert_fusion.1
  296.7 4.9 %all-to-all-start.6 = ((bf16[8,16,512]{2,1,0:T(8,128)(2,1)}), bf16[8,16,512]{2,1,0:T(8,128)(2,1)S(1)}, u32[]{:S(2)}, u32[]{:S(2)}) async-start(bf16[8,16,512]{2,1,0:T(8,128)(2,1)} %bitcast.51), calls=%async_computation.6 | async-start | bytes 262144 | tf_op jit(solution)/shard_map/all_to_all | solution.py:43
  301.6 16.5 %all-to-all-done.6 = bf16[8,16,512]{2,1,0:T(8,128)(2,1)S(1)} async-done(((bf16[8,16,512]{2,1,0:T(8,128)(2,1)}), bf16[8,16,512]{2,1,0:T(8,128)(2,1)S(1)}, u32[]{:S(2)}, u32[]{:S(2)}) %all-to-all-start.6) | async-done | bytes 131104 | tf_op jit(solution)/shard_map/all_to_all | solution.py:43
  (123 shorter events, 7.8 us)
Async XLA Ops:
  7.2 247.7 %copy-start = (f32[4096,4]{0,1:T(4,128)S(1)}, f32[4096,4]{0,1:T(4,128)}, u32[]{:S(2)}) copy-start(f32[4096,4]{0,1:T(4,128)} %param.23) | copy-start | bytes 196612
  9.4 59.9 %all-to-all-start = ((bf16[8,16,640]{2,1,0:T(8,128)(2,1)}), bf16[8,16,640]{2,1,0:T(8,128)(2,1)S(1)}, u32[]{:S(2)}, u32[]{:S(2)}) async-start(bf16[8,16,640]{2,1,0:T(8,128)(2,1)} %broadcast_in_dim.132), calls=%async_computation | async-start | bytes 327680 | tf_op jit(solution)/shard_map/all_to_all | solution.py:43
  51.1 87.2 %all-gather.2.cloned.1.call-start = ((), (), s32[]{:S(2)}) async-start(), calls=%async_computation.7 | async-start | bytes 2228224 | tf_op jit(solution)/shard_map/all_gather | solution.py:181
  52.1 11.9 %collective-permute-start = (bf16[272,256]{1,0:T(8,128)(2,1)S(1)}, bf16[272,256]{1,0:T(8,128)(2,1)S(1)}, u32[]{:S(2)}, u32[]{:S(2)}) collective-permute-start(bf16[272,256]{1,0:T(8,128)(2,1)S(1)} %maximum_maximum_fusion), channel_id=1, source_target_pairs={{0,16},{16,0},{1,17},{17,1},{2,18},{18,2},{3,19},{19,3},{4,20},{20... | collective-permute-start | bytes 417800 | tf_op jit(solution)/shard_map/ppermute | solution.py:26
  64.9 3.5 %collective-permute-start.1 = (bf16[544,256]{1,0:T(8,128)(2,1)S(1)}, bf16[544,256]{1,0:T(8,128)(2,1)S(1)}, u32[]{:S(2)}, u32[]{:S(2)}) collective-permute-start(bf16[544,256]{1,0:T(8,128)(2,1)S(1)} %pad_maximum_fusion.3), channel_id=1, source_target_pairs={{0,8},{8,0},{1,9},{9,1},{2,10},{10,2},{3,11},{11,3},{4,12},{12,4},... | collective-permute-start | bytes 835592 | tf_op jit(solution)/shard_map/ppermute | solution.py:26
  70.2 28.7 %copy-start.7 = (bf16[16,128]{1,0:T(8,128)(2,1)S(1)}, bf16[16,128]{1,0:T(8,128)(2,1)}, u32[]{:S(2)}) copy-start(bf16[16,128]{1,0:T(8,128)(2,1)} %param.15) | copy-start | bytes 12292
  70.2 28.7 %copy-start.8 = (bf16[16,128]{1,0:T(8,128)(2,1)S(1)}, bf16[16,128]{1,0:T(8,128)(2,1)}, u32[]{:S(2)}) copy-start(bf16[16,128]{1,0:T(8,128)(2,1)} %param.16) | copy-start | bytes 12292
  99.6 45.0 %copy-start.9 = (bf16[16,512]{1,0:T(8,128)(2,1)S(1)}, bf16[16,512]{1,0:T(8,128)(2,1)}, u32[]{:S(2)}) copy-start(bf16[16,512]{1,0:T(8,128)(2,1)} %param.20) | copy-start | bytes 49156
  99.6 40.6 %all-to-all-start.2 = ((bf16[8,16,768]{2,1,0:T(8,128)(2,1)}), bf16[8,16,768]{2,1,0:T(8,128)(2,1)S(1)}, u32[]{:S(2)}, u32[]{:S(2)}) async-start(bf16[8,16,768]{2,1,0:T(8,128)(2,1)} %broadcast_in_dim.134), calls=%async_computation.2 | async-start | bytes 393216 | tf_op jit(solution)/shard_map/all_to_all | solution.py:43
  138.3 6.3 %collective-permute-start.2 = (bf16[2048,512]{1,0:T(8,128)(2,1)}, bf16[2048,512]{1,0:T(8,128)(2,1)S(1)}, u32[]{:S(2)}, u32[]{:S(2)}) collective-permute-start(bf16[2048,512]{1,0:T(8,128)(2,1)} %all-gather.2.cloned.1.call-done), channel_id=1, source_target_pairs={{0,8},{8,0},{1,9},{9,1},{2,10},{10,2},{3,11},{11,3},{4,12},{12,4},... | collective-permute-start | bytes 6291464 | tf_op jit(solution)/shard_map/ppermute | solution.py:26
  144.9 173.2 %copy-start.6 = (bf16[16,512]{1,0:T(8,128)(2,1)}, bf16[16,512]{1,0:T(8,128)(2,1)S(1)}, u32[]{:S(2)}) copy-start(bf16[16,512]{1,0:T(8,128)(2,1)S(1)} %fusion.10) | copy-start | bytes 49156
  144.9 32.0 %copy-start.2 = (bf16[1,4096,128]{2,1,0:T(8,128)(2,1)S(1)}, bf16[1,4096,128]{2,1,0:T(8,128)(2,1)}, u32[]{:S(2)}) copy-start(bf16[1,4096,128]{2,1,0:T(8,128)(2,1)} %param.25) | copy-start | bytes 3145732
  144.9 32.0 %copy-start.3 = (bf16[1,4096,128]{2,1,0:T(8,128)(2,1)S(1)}, bf16[1,4096,128]{2,1,0:T(8,128)(2,1)}, u32[]{:S(2)}) copy-start(bf16[1,4096,128]{2,1,0:T(8,128)(2,1)} %param.24) | copy-start | bytes 3145732
  145.6 22.9 %all-to-all-start.3 = ((bf16[8,16,512]{2,1,0:T(8,128)(2,1)}), bf16[8,16,512]{2,1,0:T(8,128)(2,1)S(1)}, u32[]{:S(2)}, u32[]{:S(2)}) async-start(bf16[8,16,512]{2,1,0:T(8,128)(2,1)} %broadcast_in_dim.136), calls=%async_computation.3 | async-start | bytes 262144 | tf_op jit(solution)/shard_map/all_to_all | solution.py:43
  169.7 41.7 %all-to-all-start.4 = ((bf16[8,96,512]{2,1,0:T(8,128)(2,1)}), bf16[8,96,512]{2,1,0:T(8,128)(2,1)S(1)}, u32[]{:S(2)}, u32[]{:S(2)}) async-start(bf16[8,96,512]{2,1,0:T(8,128)(2,1)} %pad_maximum_fusion.1), calls=%async_computation.4 | async-start | bytes 1572864 | tf_op jit(solution)/shard_map/all_to_all | solution.py:43
  177.1 26.5 %collective-permute-start.5 = (bf16[2304,256]{1,0:T(8,128)(2,1)S(1)}, bf16[2304,256]{1,0:T(8,128)(2,1)}, u32[]{:S(2)}, u32[]{:S(2)}) collective-permute-start(bf16[2304,256]{1,0:T(8,128)(2,1)S(1)} %fusion.6), channel_id=1, source_target_pairs={{0,16},{16,0},{1,17},{17,1},{2,18},{18,2},{3,19},{19,3},{4,20},{20... | collective-permute-start | bytes 3538952 | tf_op jit(solution)/shard_map/ppermute | solution.py:26
  181.5 31.5 %collective-permute-start.3 = (bf16[4096,256]{1,0:T(8,128)(2,1)}, bf16[4096,256]{1,0:T(8,128)(2,1)}, u32[]{:S(2)}, u32[]{:S(2)}) collective-permute-start(bf16[4096,256]{1,0:T(8,128)(2,1)} %pad_maximum_fusion.refs_1_), channel_id=1, source_target_pairs={{0,8},{8,0},{1,9},{9,1},{2,10},{10,2},{3,11},{11,3},{4,12},{12,4},... | collective-permute-start | bytes 6291464 | tf_op jit(solution)/shard_map/ppermute | solution.py:26
  183.4 28.4 %copy-start.10 = (f32[4096]{0:T(1024)S(1)}, f32[4096]{0:T(1024)}, u32[]{:S(2)}) copy-start(f32[4096]{0:T(1024)} %param.22) | copy-start | bytes 49156
  183.4 29.5 %collective-permute-start.4 = (bf16[128,4096]{1,0:T(8,128)(2,1)}, bf16[128,4096]{1,0:T(8,128)(2,1)}, u32[]{:S(2)}, u32[]{:S(2)}) collective-permute-start(bf16[128,4096]{1,0:T(8,128)(2,1)} %bitcast.47.refs_3_), channel_id=1, source_target_pairs={{0,8},{8,0},{1,9},{9,1},{2,10},{10,2},{3,11},{11,3},{4,12},{12,4},... | collective-permute-start | bytes 3145736 | tf_op jit(solution)/shard_map/ppermute | solution.py:26
  203.5 53.2 %collective-permute-start.7 = (bf16[2304,256]{1,0:T(8,128)(2,1)}, bf16[2304,256]{1,0:T(8,128)(2,1)S(1)}, u32[]{:S(2)}, u32[]{:S(2)}) collective-permute-start(bf16[2304,256]{1,0:T(8,128)(2,1)} %collective-permute-done.5.refs_3_), channel_id=1, source_target_pairs={{0,8},{8,0},{1,9},{9,1},{2,10},{10,2},{3,11},{11,3},{4,12},{12,4},... | collective-permute-start | bytes 3538952 | tf_op jit(solution)/shard_map/ppermute | solution.py:26
  205.5 28.3 %collective-permute-start.9 = (bf16[128,4096]{1,0:T(8,128)(2,1)}, bf16[128,4096]{1,0:T(8,128)(2,1)}, u32[]{:S(2)}, u32[]{:S(2)}) collective-permute-start(bf16[128,4096]{1,0:T(8,128)(2,1)} %bitcast.47.refs_3_), channel_id=1, source_target_pairs={{0,16},{16,0},{1,17},{17,1},{2,18},{18,2},{3,19},{19,3},{4,20},{20... | collective-permute-start | bytes 3145736 | tf_op jit(solution)/shard_map/ppermute | solution.py:26
  209.1 43.9 %collective-permute-start.6 = (bf16[1792,256]{1,0:T(8,128)(2,1)}, bf16[1792,256]{1,0:T(8,128)(2,1)}, u32[]{:S(2)}, u32[]{:S(2)}) collective-permute-start(bf16[1792,256]{1,0:T(8,128)(2,1)} %fusion.15), channel_id=1, source_target_pairs={{0,16},{16,0},{1,17},{17,1},{2,18},{18,2},{3,19},{19,3},{4,20},{20... | collective-permute-start | bytes 2752520 | tf_op jit(solution)/shard_map/ppermute | solution.py:26
  212.9 42.0 %copy-start.1 = (bf16[96,4096]{1,0:T(8,128)(2,1)S(1)}, bf16[96,4096]{1,0:T(8,128)(2,1)}, u32[]{:S(2)}) copy-start(bf16[96,4096]{1,0:T(8,128)(2,1)} %fusion.4.refs_0_) | copy-start | bytes 2359300
  233.8 23.9 %collective-permute-start.10 = (bf16[128,4096]{1,0:T(8,128)(2,1)}, bf16[128,4096]{1,0:T(8,128)(2,1)S(1)}, u32[]{:S(2)}, u32[]{:S(2)}) collective-permute-start(bf16[128,4096]{1,0:T(8,128)(2,1)} %collective-permute-done.9.refs_7_), channel_id=1, source_target_pairs={{0,8},{8,0},{1,9},{9,1},{2,10},{10,2},{3,11},{11,3},{4,12},{12,4},... | collective-permute-start | bytes 3145736 | tf_op jit(solution)/shard_map/ppermute | solution.py:26
  252.9 4.7 %collective-permute-start.8 = (bf16[1792,256]{1,0:T(8,128)(2,1)}, bf16[1792,256]{1,0:T(8,128)(2,1)}, u32[]{:S(2)}, u32[]{:S(2)}) collective-permute-start(bf16[1792,256]{1,0:T(8,128)(2,1)} %collective-permute-done.6.refs_4_), channel_id=1, source_target_pairs={{0,8},{8,0},{1,9},{9,1},{2,10},{10,2},{3,11},{11,3},{4,12},{12,4},... | collective-permute-start | bytes 2752520 | tf_op jit(solution)/shard_map/ppermute | solution.py:26
  256.7 1.0 copy-start.4
  257.7 1.0 copy-start.5
  264.9 30.8 %all-to-all-start.5 = ((bf16[8,96,512]{2,1,0:T(8,128)(2,1)}), bf16[8,96,512]{2,1,0:T(8,128)(2,1)S(1)}, u32[]{:S(2)}, u32[]{:S(2)}) async-start(bf16[8,96,512]{2,1,0:T(8,128)(2,1)} %shard_map.166), calls=%async_computation.5 | async-start | bytes 1572864 | tf_op jit(solution)/shard_map/all_to_all | solution.py:43
  296.7 21.4 %all-to-all-start.6 = ((bf16[8,16,512]{2,1,0:T(8,128)(2,1)}), bf16[8,16,512]{2,1,0:T(8,128)(2,1)S(1)}, u32[]{:S(2)}, u32[]{:S(2)}) async-start(bf16[8,16,512]{2,1,0:T(8,128)(2,1)} %bitcast.51), calls=%async_computation.6 | async-start | bytes 262144 | tf_op jit(solution)/shard_map/all_to_all | solution.py:43
  301.6 17.2 %copy-start.11 = (bf16[16,1024]{1,0:T(8,128)(2,1)}, bf16[16,1024]{1,0:T(8,128)(2,1)S(1)}, u32[]{:S(2)}) copy-start(bf16[16,1024]{1,0:T(8,128)(2,1)S(1)} %get-tuple-element.30) | copy-start | bytes 98308
  301.6 17.2 %copy-start.12 = (bf16[16,1024]{1,0:T(8,128)(2,1)}, bf16[16,1024]{1,0:T(8,128)(2,1)S(1)}, u32[]{:S(2)}) copy-start(bf16[16,1024]{1,0:T(8,128)(2,1)S(1)} %get-tuple-element.31) | copy-start | bytes 98308
Sparse Core Ops, SparseCore 0:
  57.4 80.8 all-gather.1

commit v2 on v1

--- a/solution.py
+++ b/solution.py
@@ -68,8 +68,16 @@
     return (place["far"] * sizes["near"] + place["near"]) * sizes["core"] + place["core"]
 
 
+def _chunks(size, most=1024):
+    count = -(-size // most)
+    while size % (count * LANES) and count < size // LANES:
+        count += 1
+    return [(i * (size // count), size // count) for i in range(count)]
+
+
 def expert_kernel(cuts, final, *refs):
     parts = sum(len(c) for c in cuts)
+    chunks = [[_chunks(size) for size in cut] for cut in cuts]
     x_ref, refs = refs[0], refs[1:]
     if final:
         before_ref, share_ref, refs = refs[0], refs[1], refs[2:]
@@ -80,12 +88,15 @@
     copies, k = [], 0
     for d, cut in enumerate(cuts):
         at = 0
-        for size in cut:
-            copy = pltpu.make_async_copy(
-                gu_refs[k], gu_held.at[d, pl.ds(at, size)], gu_sem.at[k]
-            )
-            copy.start()
-            copies.append(copy)
+        for p, size in enumerate(cut):
+            for first, length in chunks[d][p]:
+                copy = pltpu.make_async_copy(
+                    gu_refs[k].at[pl.ds(first, length)],
+                    gu_held.at[d, pl.ds(at + first, length)],
+                    gu_sem.at[len(copies)],
+                )
+                copy.start()
+                copies.append(copy)
             at, k = at + size, k + 1
     down_copies = []
     for d in range(len(cuts)):
@@ -97,15 +108,16 @@
     hidden, k = [], 0
     for d, cut in enumerate(cuts):
         both, at = None, 0
-        for size in cut:
-            copies[k].wait()
-            piece = jnp.dot(
-                x_ref[:, at : at + size],
-                gu_held[d, at : at + size, :],
-                preferred_element_type=jnp.float32,
-            )
-            both = piece if both is None else both + piece
-            at, k = at + size, k + 1
+        for p, size in enumerate(cut):
+            for first, length in chunks[d][p]:
+                copies[k].wait()
+                span = slice(at + first, at + first + length)
+                piece = jnp.dot(
+                    x_ref[:, span], gu_held[d, span, :], preferred_element_type=jnp.float32
+                )
+                both = piece if both is None else both + piece
+                k += 1
+            at += size
         gate, up = both[:, :width], both[:, width:]
         hidden.append((gate * jax.nn.sigmoid(gate) * up).astype(jnp.bfloat16))
     hidden = jnp.concatenate(hidden, axis=1)
@@ -136,7 +148,7 @@
         scratch_shapes=[
             pltpu.VMEM((len(cuts), sum(cuts[0]), flat[0].shape[1]), flat[0].dtype),
             pltpu.VMEM((len(downs) * downs[0].shape[0], downs[0].shape[1]), downs[0].dtype),
-            pltpu.SemaphoreType.DMA((len(flat),)),
+            pltpu.SemaphoreType.DMA((sum(len(_chunks(g.shape[0])) for g in flat),)),
             pltpu.SemaphoreType.DMA((len(downs),)),
         ],
     )(x, *extra, *flat, *downs)
@@ -259,12 +271,16 @@
         jnp.where(core == 0, even, odd), out_proj_own, preferred_element_type=f32
     ) + jnp.dot(jnp.where(core == 0, odd, even), out_proj_other, preferred_element_type=f32)
     attended = (residual.astype(f32) + projected).astype(bf16)
+    down_both = lax.all_gather(after(down, out_proj_own), "near", axis=0, tiled=True)
+    down_pair = lax.dynamic_slice_in_dim(
+        down_both, (1 - lax.axis_index("near")) * down.shape[0], down.shape[0]
+    )
+    down_cross = swapped(down_pair, "core")
 
     class_rows = rows
     class_width = attended.shape[1]
     class_attended = sent_to_all(attended, CLASS).reshape(class_rows, class_width)
     second_pair = swapped(after(gate_up[cut:], class_attended), "near")
-    down_pair = swapped(after(down, class_attended), "near")
     experts = jnp.arange(EXPERTS, dtype=jnp.int32)
     first_pick = (ids[:, 0:1] == experts[None, :]).astype(f32)
     second_pick = (ids[:, 1:2] == experts[None, :]).astype(f32)
@@ -305,7 +321,6 @@
         jax.ShapeDtypeStruct((slot_count, model), f32),
     )
     second_cross = swapped(after(second_pair, near_out), "core")
-    down_cross = swapped(after(down_pair, near_out), "core")
     outgoing = expert_call(
         normed,
         ((first_pair, second_pair), (first_cross, second_cross)),

time: 327 us -> 319 us (0.976)
  waiting for transfers between devices: 144 us -> 121 us
  local copies, waits for them, and re-layouts: 5.31 us -> 13.6 us
  starting transfers between devices: 103 us -> 107 us
    ppermute x11 -> x10, waiting for transfers between devices: 57.5 us -> 37.6 us  [swapped(): return lax.ppermute(array, axis, [(0, 1), (1, 0)])]
    all_to_all x6, starting transfers between devices: 75.4 us -> 81.7 us  [exchanged(): return lax.all_to_all(tiles, axis, 0, 0, tiled=True)]
    unnamed x46 -> x48, local copies, waits for them, and re-layouts: 1.4 us -> 7.5 us
    ppermute x11 -> x10, starting transfers between devices: 27.9 us -> 25.4 us  [swapped(): return lax.ppermute(array, axis, [(0, 1), (1, 0)])]
  transfers between devices with their start and end apart: 18 -> 18, of which waited for: 11 -> 10; matrix products, arithmetic and copies ran while one was open for 5% -> 10% of each run, Pallas kernels for 2% -> 2%
where the time goes in v2:
time: 319 us; the launch traced here: 318 us
  waiting for transfers between devices  121 us (38%)
  starting transfers between devices  107 us (34%)
  blocking collectives  26.8 us (8%)
  between operations  14.8 us (5%)
  other arithmetic  14.4 us (5%)
  local copies, waits for them, and re-layouts  13.6 us (4%)
  Pallas kernels  11.6 us (4%)
  matrix products  8.27 us (3%)
    all_to_all x6, starting transfers between devices, exchanged(): return lax.all_to_all(tiles, axis, 0, 0, tiled=True)  81.7 us
    all_to_all x6, waiting for transfers between devices, exchanged(): return lax.all_to_all(tiles, axis, 0, 0, tiled=True)  53.4 us
    ppermute x10, waiting for transfers between devices, swapped(): return lax.ppermute(array, axis, [(0, 1), (1, 0)])  37.6 us
    all_gather x1, waiting for transfers between devices, body(): out_proj_own = lax.all_gather(out_proj, ('far', 'near'), axis=0, tiled=True)  29.8 us
    all_to_all x1, blocking collectives, exchanged(): return lax.all_to_all(tiles, axis, 0, 0, tiled=True)  26.8 us
    ppermute x10, starting transfers between devices, swapped(): return lax.ppermute(array, axis, [(0, 1), (1, 0)])  25.4 us
    pallas_call x2, Pallas kernels, expert_call(): pl.pallas_call(functools.partial(expert_kernel, cuts, final), out_shape=o...  11.6 us
    unnamed x48, local copies, waits for them, and re-layouts  7.5 us
  transfers between devices with their start and end apart: 18, of which 10 were waited for; matrix products, arithmetic and copies ran while one was open for 10% of the time, Pallas kernels for 2%

profile of v2, /device:TPU:80, one launch (start us, length us, event | category | flops | bytes accessed | tf_op | source)
XLA Modules:
  0.0 317.5 jit_solution(14011481116492547595)
XLA Ops:
  9.4 41.6 %all-to-all-start = ((bf16[8,16,640]{2,1,0:T(8,128)(2,1)}), bf16[8,16,640]{2,1,0:T(8,128)(2,1)S(1)}, u32[]{:S(2)}, u32[]{:S(2)}) async-start(bf16[8,16,640]{2,1,0:T(8,128)(2,1)} %broadcast_in_dim.132), calls=%async_computation | async-start | bytes 327680 | tf_op jit(solution)/shard_map/all_to_all | solution.py:43
  51.1 0.9 maximum_maximum_fusion
  52.0 5.1 %collective-permute-start = (bf16[272,256]{1,0:T(8,128)(2,1)S(1)}, bf16[272,256]{1,0:T(8,128)(2,1)S(1)}, u32[]{:S(2)}, u32[]{:S(2)}) collective-permute-start(bf16[272,256]{1,0:T(8,128)(2,1)S(1)} %maximum_maximum_fusion), channel_id=1, source_target_pairs={{0,16},{16,0},{1,17},{17,1},{2,18},{18,2},{3,19},{19,3},{4,20},{20... | collective-permute-start | bytes 417800 | tf_op jit(solution)/shard_map/ppermute | solution.py:26
  59.4 4.5 %collective-permute-done = bf16[272,256]{1,0:T(8,128)(2,1)S(1)} collective-permute-done((bf16[272,256]{1,0:T(8,128)(2,1)S(1)}, bf16[272,256]{1,0:T(8,128)(2,1)S(1)}, u32[]{:S(2)}, u32[]{:S(2)}) %collective-permute-start) | collective-permute-done | bytes 139296 | tf_op jit(solution)/shard_map/ppermute | solution.py:26
  63.9 0.9 pad_maximum_fusion.3
  64.9 2.0 collective-permute-start.1
  67.0 1.3 collective-permute-done.1
  68.3 0.9 pad_maximum_fusion.2
  71.0 26.8 %all_to_all.35 = bf16[8,16,640]{2,1,0:T(8,128)(2,1)S(1)} all-to-all(bf16[8,16,640]{2,1,0:T(8,128)(2,1)S(1)} %bitcast.207), channel_id=1, replica_groups=mesh['groups'=2,'far'=8,'near'=2,'core'=2,'rep'=8] {'far'}, dimensions={0} | all-to-all | bytes 327680 | tf_op jit(solution)/shard_map/all_to_all | solution.py:43
  99.5 7.9 %all-to-all-start.2 = ((bf16[8,16,768]{2,1,0:T(8,128)(2,1)}), bf16[8,16,768]{2,1,0:T(8,128)(2,1)S(1)}, u32[]{:S(2)}, u32[]{:S(2)}) async-start(bf16[8,16,768]{2,1,0:T(8,128)(2,1)} %broadcast_in_dim.134), calls=%async_computation.2 | async-start | bytes 393216 | tf_op jit(solution)/shard_map/all_to_all | solution.py:43
  107.5 1.2 fusion.6
  108.7 29.8 %all-gather.3.cloned.1.call-done = bf16[2048,512]{1,0:T(8,128)(2,1)} async-done(((bf16[128,512]{1,0:T(8,128)(2,1)}), bf16[2048,512]{1,0:T(8,128)(2,1)}) %all-gather.3.cloned.1.call-update) | async-done | bytes 2097168 | tf_op jit(solution)/shard_map/all_gather | solution.py:193
  138.5 1.9 collective-permute-start.2
  140.8 2.0 fusion.27
  142.8 2.2 collective-permute-done.2
  145.0 2.0 fusion.10
  147.6 6.7 %all-to-all-start.3 = ((bf16[8,16,512]{2,1,0:T(8,128)(2,1)}), bf16[8,16,512]{2,1,0:T(8,128)(2,1)}, u32[]{:S(2)}, u32[]{:S(2)}) async-start(bf16[8,16,512]{2,1,0:T(8,128)(2,1)} %broadcast_in_dim.136), calls=%async_computation.3 | async-start | bytes 262144 | tf_op jit(solution)/shard_map/all_to_all | solution.py:43
  154.8 2.5 collective-permute-start.5
  157.2 14.2 %all-to-all-done.3 = bf16[8,16,512]{2,1,0:T(8,128)(2,1)} async-done(((bf16[8,16,512]{2,1,0:T(8,128)(2,1)}), bf16[8,16,512]{2,1,0:T(8,128)(2,1)}, u32[]{:S(2)}, u32[]{:S(2)}) %all-to-all-start.3) | async-done | bytes 131104 | tf_op jit(solution)/shard_map/all_to_all | solution.py:43
  171.5 1.1 convolution_convert_fusion
  172.6 1.0 pad_maximum_fusion.1
  173.6 7.6 %all-to-all-start.4 = ((bf16[8,96,512]{2,1,0:T(8,128)(2,1)}), bf16[8,96,512]{2,1,0:T(8,128)(2,1)}, u32[]{:S(2)}, u32[]{:S(2)}) async-start(bf16[8,96,512]{2,1,0:T(8,128)(2,1)} %pad_maximum_fusion.1), calls=%async_computation.4 | async-start | bytes 1572864 | tf_op jit(solution)/shard_map/all_to_all | solution.py:43
  181.2 2.0 collective-permute-start.4
  183.1 1.6 pad_maximum_fusion.refs_1_
  184.7 2.4 collective-permute-start.3
  187.2 1.1 fusion.15
  188.2 21.8 %collective-permute-done.5.refs_3_ = bf16[2304,256]{1,0:T(8,128)(2,1)} collective-permute-done((bf16[2304,256]{1,0:T(8,128)(2,1)}, bf16[2304,256]{1,0:T(8,128)(2,1)}, u32[]{:S(2)}, u32[]{:S(2)}) %collective-permute-start.5) | collective-permute-done | bytes 1179680 | tf_op jit(solution)/shard_map/ppermute | solution.py:26
  210.0 1.9 collective-permute-start.7
  212.0 1.3 constant_dynamic-slice_fusion.refs_7_
  213.3 2.4 collective-permute-start.9
  215.8 3.2 %collective-permute-start.6 = (bf16[1792,256]{1,0:T(8,128)(2,1)}, bf16[1792,256]{1,0:T(8,128)(2,1)}, u32[]{:S(2)}, u32[]{:S(2)}) collective-permute-start(bf16[1792,256]{1,0:T(8,128)(2,1)} %fusion.15), channel_id=1, source_target_pairs={{0,16},{16,0},{1,17},{17,1},{2,18},{18,2},{3,19},{19,3},{4,20},{20... | collective-permute-start | bytes 2752520 | tf_op jit(solution)/shard_map/ppermute | solution.py:26
  219.9 0.9 constant_dynamic-update-slice_fusion.33
  220.8 0.9 constant_dynamic-update-slice_fusion.32
  221.7 0.9 constant_dynamic-update-slice_fusion.31
  222.6 0.9 constant_dynamic-update-slice_fusion.30
  224.4 0.9 constant_dynamic-update-slice_fusion.28
  225.3 0.9 constant_dynamic-update-slice_fusion.27
  226.5 1.1 fusion.4.refs_0_
  227.7 5.7 %shard_map.165.refs_1_ = f32[96,4096]{1,0:T(8,128)} custom-call(bf16[96,4096]{1,0:T(8,128)(2,1)} %fusion.4.refs_0_, bf16[4096,256]{1,0:T(8,128)(2,1)} %pad_maximum_fusion.refs_1_, bf16[4096,256]{1,0:T(8,128)(2,1)} %collective-permute-done.3.refs_2_, bf16[128,4096]{1,0:T(8,128)(2,1)} %bitcast.201, bf16[128,4096]{1,0:T(8,128)(2,1)} %collective-permute-done.4.refs_4_), custom_call_target="tpu_custom_call" | custom-call | tf_op jit(solution)/shard_map/pallas_call | solution.py:143
  233.4 6.9 %collective-permute-done.6.refs_4_ = bf16[1792,256]{1,0:T(8,128)(2,1)} collective-permute-done((bf16[1792,256]{1,0:T(8,128)(2,1)}, bf16[1792,256]{1,0:T(8,128)(2,1)}, u32[]{:S(2)}, u32[]{:S(2)}) %collective-permute-start.6) | collective-permute-done | bytes 917536 | tf_op jit(solution)/shard_map/ppermute | solution.py:26
  240.3 1.9 collective-permute-start.8
  244.9 0.9 copy-done.6
  245.8 5.9 %shard_map.166 = bf16[8,96,512]{2,1,0:T(8,128)(2,1)} custom-call(bf16[96,4096]{1,0:T(8,128)(2,1)} %fusion.4.refs_0_, f32[96,4096]{1,0:T(8,128)} %shard_map.165.refs_1_, f32[96,1]{1,0:T(8,128)} %copy.34.refs_2_, bf16[2304,256]{1,0:T(8,128)(2,1)} %collective-permute-done.5.refs_3_, bf16[1792,256]{1,0:T(8,128)(2,1)} %collective-permute-done.6.refs_4_, ...), custom_call_target="tpu_custom_call" | custom-call | tf_op jit(solution)/shard_map/pallas_call | solution.py:143
  251.7 7.0 %all-to-all-start.5 = ((bf16[8,96,512]{2,1,0:T(8,128)(2,1)}), bf16[8,96,512]{2,1,0:T(8,128)(2,1)S(1)}, u32[]{:S(2)}, u32[]{:S(2)}) async-start(bf16[8,96,512]{2,1,0:T(8,128)(2,1)} %shard_map.166), calls=%async_computation.5 | async-start | bytes 1572864 | tf_op jit(solution)/shard_map/all_to_all | solution.py:43
  259.0 23.1 %all-to-all-done.5 = bf16[8,96,512]{2,1,0:T(8,128)(2,1)S(1)} async-done(((bf16[8,96,512]{2,1,0:T(8,128)(2,1)}), bf16[8,96,512]{2,1,0:T(8,128)(2,1)S(1)}, u32[]{:S(2)}, u32[]{:S(2)}) %all-to-all-start.5) | async-done | bytes 786464 | tf_op jit(solution)/shard_map/all_to_all | solution.py:43
  282.1 0.9 convolution_convert_fusion.1
  283.1 10.9 %all-to-all-start.6 = ((bf16[8,16,512]{2,1,0:T(8,128)(2,1)}), bf16[8,16,512]{2,1,0:T(8,128)(2,1)S(1)}, u32[]{:S(2)}, u32[]{:S(2)}) async-start(bf16[8,16,512]{2,1,0:T(8,128)(2,1)} %bitcast.51), calls=%async_computation.6 | async-start | bytes 262144 | tf_op jit(solution)/shard_map/all_to_all | solution.py:43
  294.0 16.0 %all-to-all-done.6 = bf16[8,16,512]{2,1,0:T(8,128)(2,1)S(1)} async-done(((bf16[8,16,512]{2,1,0:T(8,128)(2,1)}), bf16[8,16,512]{2,1,0:T(8,128)(2,1)S(1)}, u32[]{:S(2)}, u32[]{:S(2)}) %all-to-all-start.6) | async-done | bytes 131104 | tf_op jit(solution)/shard_map/all_to_all | solution.py:43
  (127 shorter events, 15.0 us)
Async XLA Ops:
  7.2 235.1 %copy-start = (f32[4096,4]{0,1:T(4,128)S(1)}, f32[4096,4]{0,1:T(4,128)}, u32[]{:S(2)}) copy-start(f32[4096,4]{0,1:T(4,128)} %param.23) | copy-start | bytes 196612
  9.4 59.9 %all-to-all-start = ((bf16[8,16,640]{2,1,0:T(8,128)(2,1)}), bf16[8,16,640]{2,1,0:T(8,128)(2,1)S(1)}, u32[]{:S(2)}, u32[]{:S(2)}) async-start(bf16[8,16,640]{2,1,0:T(8,128)(2,1)} %broadcast_in_dim.132), calls=%async_computation | async-start | bytes 327680 | tf_op jit(solution)/shard_map/all_to_all | solution.py:43
  51.0 87.5 %all-gather.3.cloned.1.call-start = ((), (), s32[]{:S(2)}) async-start(), calls=%async_computation.7 | async-start | bytes 2228224 | tf_op jit(solution)/shard_map/all_gather | solution.py:193
  52.0 11.9 %collective-permute-start = (bf16[272,256]{1,0:T(8,128)(2,1)S(1)}, bf16[272,256]{1,0:T(8,128)(2,1)S(1)}, u32[]{:S(2)}, u32[]{:S(2)}) collective-permute-start(bf16[272,256]{1,0:T(8,128)(2,1)S(1)} %maximum_maximum_fusion), channel_id=1, source_target_pairs={{0,16},{16,0},{1,17},{17,1},{2,18},{18,2},{3,19},{19,3},{4,20},{20... | collective-permute-start | bytes 417800 | tf_op jit(solution)/shard_map/ppermute | solution.py:26
  64.9 3.5 %collective-permute-start.1 = (bf16[544,256]{1,0:T(8,128)(2,1)S(1)}, bf16[544,256]{1,0:T(8,128)(2,1)S(1)}, u32[]{:S(2)}, u32[]{:S(2)}) collective-permute-start(bf16[544,256]{1,0:T(8,128)(2,1)S(1)} %pad_maximum_fusion.3), channel_id=1, source_target_pairs={{0,8},{8,0},{1,9},{9,1},{2,10},{10,2},{3,11},{11,3},{4,12},{12,4},... | collective-permute-start | bytes 835592 | tf_op jit(solution)/shard_map/ppermute | solution.py:26
  70.1 28.7 %copy-start.8 = (bf16[16,128]{1,0:T(8,128)(2,1)S(1)}, bf16[16,128]{1,0:T(8,128)(2,1)}, u32[]{:S(2)}) copy-start(bf16[16,128]{1,0:T(8,128)(2,1)} %param.15) | copy-start | bytes 12292
  70.2 28.7 %copy-start.9 = (bf16[16,128]{1,0:T(8,128)(2,1)S(1)}, bf16[16,128]{1,0:T(8,128)(2,1)}, u32[]{:S(2)}) copy-start(bf16[16,128]{1,0:T(8,128)(2,1)} %param.16) | copy-start | bytes 12292
  70.2 37.4 %copy-start.2 = (bf16[1,4096,128]{2,1,0:T(8,128)(2,1)S(1)}, bf16[1,4096,128]{2,1,0:T(8,128)(2,1)}, u32[]{:S(2)}) copy-start(bf16[1,4096,128]{2,1,0:T(8,128)(2,1)} %param.25) | copy-start | bytes 3145732
  70.2 37.4 %copy-start.3 = (bf16[1,4096,128]{2,1,0:T(8,128)(2,1)S(1)}, bf16[1,4096,128]{2,1,0:T(8,128)(2,1)}, u32[]{:S(2)}) copy-start(bf16[1,4096,128]{2,1,0:T(8,128)(2,1)} %param.24) | copy-start | bytes 3145732
  99.5 41.0 %all-to-all-start.2 = ((bf16[8,16,768]{2,1,0:T(8,128)(2,1)}), bf16[8,16,768]{2,1,0:T(8,128)(2,1)S(1)}, u32[]{:S(2)}, u32[]{:S(2)}) async-start(bf16[8,16,768]{2,1,0:T(8,128)(2,1)} %broadcast_in_dim.134), calls=%async_computation.2 | async-start | bytes 393216 | tf_op jit(solution)/shard_map/all_to_all | solution.py:43
  107.5 104.5 %all-gather.5.cloned.1.call-start = ((), (), s32[]{:S(2)}) async-start(), calls=%async_computation.8 | async-start | bytes 3145728 | tf_op jit(solution)/shard_map/all_gather | solution.py:274
  138.5 6.4 %collective-permute-start.2 = (bf16[2048,512]{1,0:T(8,128)(2,1)}, bf16[2048,512]{1,0:T(8,128)(2,1)}, u32[]{:S(2)}, u32[]{:S(2)}) collective-permute-start(bf16[2048,512]{1,0:T(8,128)(2,1)} %all-gather.3.cloned.1.call-done), channel_id=1, source_target_pairs={{0,8},{8,0},{1,9},{9,1},{2,10},{10,2},{3,11},{11,3},{4,12},{12,4},... | collective-permute-start | bytes 6291464 | tf_op jit(solution)/shard_map/ppermute | solution.py:26
  140.6 4.4 %copy-start.10 = (bf16[16,512]{1,0:T(8,128)(2,1)S(1)}, bf16[16,512]{1,0:T(8,128)(2,1)}, u32[]{:S(2)}) copy-start(bf16[16,512]{1,0:T(8,128)(2,1)} %param.20) | copy-start | bytes 49156
  146.9 163.1 %copy-start.7 = (bf16[16,512]{1,0:T(8,128)(2,1)}, bf16[16,512]{1,0:T(8,128)(2,1)S(1)}, u32[]{:S(2)}) copy-start(bf16[16,512]{1,0:T(8,128)(2,1)S(1)} %fusion.10) | copy-start | bytes 49156
  146.9 34.3 %copy-start.5 = (bf16[1,128,4096]{2,1,0:T(8,128)(2,1)S(1)}, bf16[1,128,4096]{2,1,0:T(8,128)(2,1)}, u32[]{:S(2)}) copy-start(bf16[1,128,4096]{2,1,0:T(8,128)(2,1)} %param.26) | copy-start | bytes 3145732
  147.6 23.9 %all-to-all-start.3 = ((bf16[8,16,512]{2,1,0:T(8,128)(2,1)}), bf16[8,16,512]{2,1,0:T(8,128)(2,1)}, u32[]{:S(2)}, u32[]{:S(2)}) async-start(bf16[8,16,512]{2,1,0:T(8,128)(2,1)} %broadcast_in_dim.136), calls=%async_computation.3 | async-start | bytes 262144 | tf_op jit(solution)/shard_map/all_to_all | solution.py:43
  154.8 55.3 %collective-permute-start.5 = (bf16[2304,256]{1,0:T(8,128)(2,1)}, bf16[2304,256]{1,0:T(8,128)(2,1)}, u32[]{:S(2)}, u32[]{:S(2)}) collective-permute-start(bf16[2304,256]{1,0:T(8,128)(2,1)} %fusion.6), channel_id=1, source_target_pairs={{0,16},{16,0},{1,17},{17,1},{2,18},{18,2},{3,19},{19,3},{4,20},{20... | collective-permute-start | bytes 3538952 | tf_op jit(solution)/shard_map/ppermute | solution.py:26
  173.6 45.4 %all-to-all-start.4 = ((bf16[8,96,512]{2,1,0:T(8,128)(2,1)}), bf16[8,96,512]{2,1,0:T(8,128)(2,1)}, u32[]{:S(2)}, u32[]{:S(2)}) async-start(bf16[8,96,512]{2,1,0:T(8,128)(2,1)} %pad_maximum_fusion.1), calls=%async_computation.4 | async-start | bytes 1572864 | tf_op jit(solution)/shard_map/all_to_all | solution.py:43
  181.2 46.5 %collective-permute-start.4 = (bf16[128,4096]{1,0:T(8,128)(2,1)S(1)}, bf16[128,4096]{1,0:T(8,128)(2,1)}, u32[]{:S(2)}, u32[]{:S(2)}) collective-permute-start(bf16[128,4096]{1,0:T(8,128)(2,1)S(1)} %bitcast.202), channel_id=1, source_target_pairs={{0,8},{8,0},{1,9},{9,1},{2,10},{10,2},{3,11},{11,3},{4,12},{12,4},... | collective-permute-start | bytes 3145736 | tf_op jit(solution)/shard_map/ppermute | solution.py:26
  184.7 42.9 %collective-permute-start.3 = (bf16[4096,256]{1,0:T(8,128)(2,1)}, bf16[4096,256]{1,0:T(8,128)(2,1)}, u32[]{:S(2)}, u32[]{:S(2)}) collective-permute-start(bf16[4096,256]{1,0:T(8,128)(2,1)} %pad_maximum_fusion.refs_1_), channel_id=1, source_target_pairs={{0,8},{8,0},{1,9},{9,1},{2,10},{10,2},{3,11},{11,3},{4,12},{12,4},... | collective-permute-start | bytes 6291464 | tf_op jit(solution)/shard_map/ppermute | solution.py:26
  188.2 38.3 %copy-start.11 = (f32[4096]{0:T(1024)S(1)}, f32[4096]{0:T(1024)}, u32[]{:S(2)}) copy-start(f32[4096]{0:T(1024)} %param.22) | copy-start | bytes 49156
  210.0 34.0 %collective-permute-start.7 = (bf16[2304,256]{1,0:T(8,128)(2,1)}, bf16[2304,256]{1,0:T(8,128)(2,1)}, u32[]{:S(2)}, u32[]{:S(2)}) collective-permute-start(bf16[2304,256]{1,0:T(8,128)(2,1)} %collective-permute-done.5.refs_3_), channel_id=1, source_target_pairs={{0,8},{8,0},{1,9},{9,1},{2,10},{10,2},{3,11},{11,3},{4,12},{12,4},... | collective-permute-start | bytes 3538952 | tf_op jit(solution)/shard_map/ppermute | solution.py:26
  213.3 20.1 %copy-start.4 = (bf16[128,4096]{1,0:T(8,128)(2,1)}, bf16[128,4096]{1,0:T(8,128)(2,1)S(1)}, u32[]{:S(2)}) copy-start(bf16[128,4096]{1,0:T(8,128)(2,1)S(1)} %constant_dynamic-slice_fusion.refs_7_) | copy-start | bytes 3145732
  213.3 30.7 %collective-permute-start.9 = (bf16[128,4096]{1,0:T(8,128)(2,1)S(1)}, bf16[128,4096]{1,0:T(8,128)(2,1)}, u32[]{:S(2)}, u32[]{:S(2)}) collective-permute-start(bf16[128,4096]{1,0:T(8,128)(2,1)S(1)} %constant_dynamic-slice_fusion.refs_7_), channel_id=1, source_target_pairs={{0,8},{8,0},{1,9},{9,1},{2,10},{10,2},{3,11},{11,3},{4,12},{12,4},... | collective-permute-start | bytes 3145736 | tf_op jit(solution)/shard_map/ppermute | solution.py:26
  215.8 24.5 %collective-permute-start.6 = (bf16[1792,256]{1,0:T(8,128)(2,1)}, bf16[1792,256]{1,0:T(8,128)(2,1)}, u32[]{:S(2)}, u32[]{:S(2)}) collective-permute-start(bf16[1792,256]{1,0:T(8,128)(2,1)} %fusion.15), channel_id=1, source_target_pairs={{0,16},{16,0},{1,17},{17,1},{2,18},{18,2},{3,19},{19,3},{4,20},{20... | collective-permute-start | bytes 2752520 | tf_op jit(solution)/shard_map/ppermute | solution.py:26
  227.6 14.6 %copy-start.1 = (bf16[96,4096]{1,0:T(8,128)(2,1)S(1)}, bf16[96,4096]{1,0:T(8,128)(2,1)}, u32[]{:S(2)}) copy-start(bf16[96,4096]{1,0:T(8,128)(2,1)} %fusion.4.refs_0_) | copy-start | bytes 2359300
  240.3 4.6 %collective-permute-start.8 = (bf16[1792,256]{1,0:T(8,128)(2,1)}, bf16[1792,256]{1,0:T(8,128)(2,1)S(1)}, u32[]{:S(2)}, u32[]{:S(2)}) collective-permute-start(bf16[1792,256]{1,0:T(8,128)(2,1)} %collective-permute-done.6.refs_4_), channel_id=1, source_target_pairs={{0,8},{8,0},{1,9},{9,1},{2,10},{10,2},{3,11},{11,3},{4,12},{12,4},... | collective-permute-start | bytes 2752520 | tf_op jit(solution)/shard_map/ppermute | solution.py:26
  244.9 0.9 copy-start.6
  251.7 30.4 %all-to-all-start.5 = ((bf16[8,96,512]{2,1,0:T(8,128)(2,1)}), bf16[8,96,512]{2,1,0:T(8,128)(2,1)S(1)}, u32[]{:S(2)}, u32[]{:S(2)}) async-start(bf16[8,96,512]{2,1,0:T(8,128)(2,1)} %shard_map.166), calls=%async_computation.5 | async-start | bytes 1572864 | tf_op jit(solution)/shard_map/all_to_all | solution.py:43
  283.1 27.0 %all-to-all-start.6 = ((bf16[8,16,512]{2,1,0:T(8,128)(2,1)}), bf16[8,16,512]{2,1,0:T(8,128)(2,1)S(1)}, u32[]{:S(2)}, u32[]{:S(2)}) async-start(bf16[8,16,512]{2,1,0:T(8,128)(2,1)} %bitcast.51), calls=%async_computation.6 | async-start | bytes 262144 | tf_op jit(solution)/shard_map/all_to_all | solution.py:43
  294.0 16.7 %copy-start.12 = (bf16[16,1024]{1,0:T(8,128)(2,1)}, bf16[16,1024]{1,0:T(8,128)(2,1)S(1)}, u32[]{:S(2)}) copy-start(bf16[16,1024]{1,0:T(8,128)(2,1)S(1)} %get-tuple-element.28) | copy-start | bytes 98308
  294.0 16.7 %copy-start.13 = (bf16[16,1024]{1,0:T(8,128)(2,1)}, bf16[16,1024]{1,0:T(8,128)(2,1)S(1)}, u32[]{:S(2)}) copy-start(bf16[16,1024]{1,0:T(8,128)(2,1)S(1)} %get-tuple-element.29) | copy-start | bytes 98308
Sparse Core Ops, SparseCore 0:
  57.4 81.1 all-gather.2
  140.9 66.2 all-gather.4

commit v3 on v0

--- a/solution.py
+++ b/solution.py
@@ -1,8 +1,11 @@
+import functools
 import math
 
 import jax
 import jax.numpy as jnp
 from jax import lax
+from jax.experimental import pallas as pl
+from jax.experimental.pallas import tpu as pltpu
 from jax.sharding import Mesh
 from jax.sharding import PartitionSpec as P
 
@@ -63,6 +66,108 @@
         place[axis] = index % sizes[axis]
         index = index // sizes[axis]
     return (place["far"] * sizes["near"] + place["near"]) * sizes["core"] + place["core"]
+
+
+def dot(a, b):
+    return jnp.dot(a, b, preferred_element_type=jnp.float32)
+
+
+def hidden_units(x_ref, parts_of_each):
+    both, at = None, 0
+    for refs in zip(*parts_of_each):
+        size = refs[0].shape[0]
+        piece = dot(
+            x_ref[:, at : at + size], jnp.concatenate([ref[...] for ref in refs], axis=1)
+        )
+        both, at = piece if both is None else both + piece, at + size
+    width = refs[0].shape[1] // 2
+    hidden = []
+    for i in range(len(refs)):
+        gate = both[:, 2 * i * width : (2 * i + 1) * width]
+        up = both[:, (2 * i + 1) * width : (2 * i + 2) * width]
+        hidden.append((gate * jax.nn.sigmoid(gate) * up).astype(jnp.bfloat16))
+    return jnp.concatenate(hidden, axis=1)
+
+
+def first_expert_kernel(
+    tiles_ref, gain_ref, router_ref, sign_ref, gu_refs, down_refs, out_ref, x_ref, share_ref
+):
+    count, _, columns = tiles_ref.shape
+    squares = 0.0
+    for i in range(count):
+        tile = tiles_ref[i].astype(jnp.float32)
+        squares = squares + jnp.sum(tile * tile, axis=1, keepdims=True)
+    scale = lax.rsqrt(squares / (count * columns) + 1e-05)
+    logit = 0.0
+    for i in range(count):
+        span = slice(i * columns, (i + 1) * columns)
+        tile = tiles_ref[i].astype(jnp.float32) * gain_ref[:, span] * scale
+        x_ref[:, span] = tile.astype(jnp.bfloat16)
+        rounded = x_ref[:, span].astype(jnp.float32)
+        for e in range(EXPERTS):
+            part = jnp.sum(rounded * router_ref[e : e + 1, span], axis=1, keepdims=True)
+            logit = logit + part * sign_ref[:, e : e + 1]
+    share_ref[...] = jax.nn.sigmoid(logit)
+    hidden = hidden_units(x_ref, [(ref,) for ref in gu_refs])
+    for i in range(count):
+        span = slice(i * columns, (i + 1) * columns)
+        out_ref[:, span] = dot(
+            hidden, jnp.concatenate([ref[:, span] for ref in down_refs], axis=0)
+        )
+
+
+def last_expert_kernel(x_ref, before_ref, share_ref, gu_refs, down_refs, out_ref):
+    count, _, columns = out_ref.shape
+    hidden = hidden_units(x_ref, gu_refs)
+    for i in range(count):
+        span = slice(i * columns, (i + 1) * columns)
+        piece = before_ref[:, span] + dot(
+            hidden, jnp.concatenate([ref[:, span] for ref in down_refs], axis=0)
+        )
+        out_ref[i] = (piece * share_ref[...]).astype(out_ref.dtype)
+
+
+def heads_of(spread_ref, i, rows, width, other):
+    even = [spread_ref[i, :, j : j + rows] for j in range(0, width, CORES * rows)]
+    odd = [spread_ref[i, :, j : j + rows] for j in range(rows, width, CORES * rows)]
+    turn = (lax.axis_index("core") + other) % CORES == 0
+    return jnp.where(turn, jnp.concatenate(even, axis=1), jnp.concatenate(odd, axis=1))
+
+
+def project(spread_ref, proj_ref, rows, width, other):
+    count = spread_ref.shape[0]
+    depth = width // CORES
+    total = None
+    for i in range(count):
+        piece = dot(
+            heads_of(spread_ref, i, rows, width, other), proj_ref[i * depth : (i + 1) * depth, :]
+        )
+        total = piece if total is None else total + piece
+    return total
+
+
+def own_projection_kernel(rows, width, spread_ref, proj_ref, out_ref):
+    out_ref[...] = project(spread_ref, proj_ref, rows, width, 0)
+
+
+def other_projection_kernel(
+    rows, width, spread_ref, proj_ref, before_ref, residual_ref, out_ref, copies_ref
+):
+    total = before_ref[...] + project(spread_ref, proj_ref, rows, width, 1)
+    attended = (residual_ref[...].astype(jnp.float32) + total).astype(out_ref.dtype)
+    out_ref[...] = attended
+    for i in range(copies_ref.shape[0]):
+        copies_ref[i] = attended
+
+
+def in_vmem(kernel, out_shape, *operands):
+    whole = pl.BlockSpec(memory_space=pltpu.VMEM)
+    return pl.pallas_call(
+        kernel,
+        out_shape=out_shape,
+        in_specs=jax.tree.map(lambda _: whole, operands),
+        out_specs=jax.tree.map(lambda _: whole, out_shape),
+    )(*operands)
 
 
 def body(
@@ -168,26 +273,32 @@
     spread = sent_to_all(jnp.concatenate([attn_local, keys_new, values_new], axis=1), "rep")
     keys_cache = side_by_side(spread[:, :, width : width + head_dim])
     values_cache = side_by_side(spread[:, :, width + head_dim :])
-    core = lax.axis_index("core")
-    rows_of = out_proj.shape[0]
-    even, odd = (
-        side_by_side(
-            jnp.concatenate(
-                [spread[:, :, j : j + rows_of] for j in range(first, width, CORES * rows_of)], axis=2
-            )
-        )
-        for first in (0, rows_of)
-    )
-    projected = jnp.dot(
-        jnp.where(core == 0, even, odd), out_proj_own, preferred_element_type=f32
-    ) + jnp.dot(jnp.where(core == 0, odd, even), out_proj_other, preferred_element_type=f32)
-    attended = (residual.astype(f32) + projected).astype(bf16)
+    shape = jax.ShapeDtypeStruct
+    sizes = (out_proj.shape[0], width)
+    own_part = in_vmem(
+        functools.partial(own_projection_kernel, *sizes),
+        shape(residual.shape, f32),
+        spread,
+        out_proj_own,
+    )
+    attended, attended_copies = in_vmem(
+        functools.partial(other_projection_kernel, *sizes),
+        (shape(residual.shape, bf16), shape((count, *residual.shape), bf16)),
+        spread,
+        out_proj_other,
+        own_part,
+        residual,
+    )
+    down_both = lax.all_gather(after(down, out_proj_own), "near", axis=0, tiled=True)
+    down_pair = lax.dynamic_slice_in_dim(
+        down_both, (1 - lax.axis_index("near")) * down.shape[0], down.shape[0]
+    )
+    down_cross = swapped(down_pair, "core")
 
     class_rows = rows
     class_width = attended.shape[1]
-    class_attended = sent_to_all(attended, CLASS).reshape(class_rows, class_width)
+    class_attended = exchanged(attended_copies, CLASS).reshape(class_rows, class_width)
     second_pair = swapped(after(gate_up[cut:], class_attended), "near")
-    down_pair = swapped(after(down, class_attended), "near")
     experts = jnp.arange(EXPERTS, dtype=jnp.int32)
     first_pick = (ids[:, 0:1] == experts[None, :]).astype(f32)
     second_pick = (ids[:, 1:2] == experts[None, :]).astype(f32)
@@ -201,53 +312,41 @@
     slot_count = count * CAP
     slots = jnp.arange(slot_count, dtype=jnp.int32)
     selection = (slot_of.T[:, None, :] == slots[None, :, None]).astype(bf16)
-    slot_rows = jnp.dot(
-        selection.reshape(EXPERTS * slot_count, class_rows),
-        class_attended,
-        preferred_element_type=f32,
-    ).astype(bf16)
-    slot_rows = slot_rows.reshape(EXPERTS, slot_count, class_width)
     halves = rep_count // EXPERTS
-    arrived = exchanged(jnp.concatenate([slot_rows] * halves, axis=0), "rep")
-    features = side_by_side(arrived).astype(f32)
-
-    mean_square = jnp.mean(features * features, axis=1, keepdims=True)
-    normed = (features * norm_gain[None, :] * lax.rsqrt(mean_square + 1e-05)).astype(bf16)
-    logits = jnp.dot(normed.astype(f32), router, precision=lax.Precision.HIGHEST)
+    back = jnp.concatenate([selection.reshape(EXPERTS * slot_count, class_rows)] * halves, axis=0)
+    slot_rows = dot(back, class_attended).astype(bf16)
+    arrived = exchanged(slot_rows.reshape(rep_count, slot_count, class_width), "rep")
+
     mine = lax.axis_index("rep") % EXPERTS
     my_selection = lax.dynamic_index_in_dim(selection, mine, axis=0, keepdims=False)
     slot_member = jnp.dot(my_selection, member.astype(bf16), preferred_element_type=f32)
-    own = (experts == mine)[None, :]
-    own_logit = jnp.sum(jnp.where(own, logits, 0.0), axis=1)
-    other_logit = jnp.sum(jnp.where(own, 0.0, slot_member * logits), axis=1)
-    share = jax.nn.sigmoid(own_logit - other_logit)
-    hidden_width = w_gate.shape[2]
-
-    def hidden_of(*parts_of):
-        both, at = None, 0
-        for part in parts_of:
-            piece = jnp.dot(
-                normed[:, at : at + part.shape[0]], part, preferred_element_type=f32
-            )
-            both, at = piece if both is None else both + piece, at + part.shape[0]
-        return (jax.nn.silu(both[:, :hidden_width]) * both[:, hidden_width:]).astype(bf16)
-
-    def out_of(hidden, rows_down):
-        return jnp.dot(hidden, rows_down, preferred_element_type=f32)
-
-    expert_out = out_of(hidden_of(gate_up), down) + out_of(hidden_of(gate_up_core), down_core)
-    second_cross = swapped(after(second_pair, expert_out), "core")
-    hidden_pair = hidden_of(first_pair, second_pair)
-    down_cross = swapped(after(down_pair, hidden_pair), "core")
-    expert_out = expert_out + out_of(hidden_pair, down_pair)
-    expert_out = expert_out + out_of(hidden_of(first_cross, second_cross), down_cross)
-    weighted = (expert_out * share[:, None]).astype(bf16)
-    outgoing = jnp.stack(
-        [weighted[:, i * class_width : (i + 1) * class_width] for i in range(rep_count)], axis=0
+    sign = jnp.where((experts == mine)[None, :], slot_member, -slot_member)
+    near_out, normed, share = in_vmem(
+        first_expert_kernel,
+        (
+            shape((slot_count, model), f32),
+            shape((slot_count, model), bf16),
+            shape((slot_count, 1), f32),
+        ),
+        arrived,
+        norm_gain[None, :],
+        router.T,
+        sign,
+        (gate_up, gate_up_core),
+        (down, down_core),
+    )
+    second_cross = swapped(after(second_pair, near_out), "core")
+    outgoing = in_vmem(
+        last_expert_kernel,
+        shape((rep_count, slot_count, class_width), bf16),
+        normed,
+        near_out,
+        share,
+        ((first_pair, second_pair), (first_cross, second_cross)),
+        (down_pair, down_cross),
     )
     returned = exchanged(outgoing, "rep")
 
-    back = jnp.concatenate([selection.reshape(EXPERTS * slot_count, class_rows)] * halves, axis=0)
     mixture = lax.dot_general(
         back,
         returned.reshape(rep_count * slot_count, class_width),

time: 328 us -> 313 us (0.954)
  blocking collectives: 26.8 us -> 0 us
  Pallas kernels: 0 us -> 17.7 us
  matrix products: 18.5 us -> 4.27 us
  starting transfers between devices: 102 us -> 114 us
  waiting for transfers between devices: 142 us -> 137 us
    ppermute x11 -> x10, waiting for transfers between devices: 55.8 us -> 24.2 us  [swapped(): return lax.ppermute(array, axis, [(0, 1), (1, 0)])]
    all_to_all x1 -> x0, blocking collectives: 26.8 us -> none  [exchanged(): return lax.all_to_all(tiles, axis, 0, 0, tiled=True)]
    all_gather x1, waiting for transfers between devices: 30.9 us -> 53.5 us  [body(): out_proj_own = lax.all_gather(out_proj, ('far', 'near'), axis=0, tiled=True)]
    pallas_call x0 -> x4, Pallas kernels: none -> 17.7 us  [in_vmem(): pl.pallas_call(kernel, out_shape=out_shape, in_specs=jax.tree.map(lambda...]
    dot_general x14 -> x1, matrix products: 16 us -> 1.22 us  [dot(): return jnp.dot(a, b, preferred_element_type=jnp.float32)]
    all_to_all x6 -> x7, starting transfers between devices: 74.8 us -> 89 us  [exchanged(): return lax.all_to_all(tiles, axis, 0, 0, tiled=True)]
    all_to_all x6 -> x7, waiting for transfers between devices: 55 us -> 59.3 us  [exchanged(): return lax.all_to_all(tiles, axis, 0, 0, tiled=True)]
    ppermute x11 -> x10, starting transfers between devices: 27.4 us -> 25.4 us  [swapped(): return lax.ppermute(array, axis, [(0, 1), (1, 0)])]
  transfers between devices with their start and end apart: 18 -> 19, of which waited for: 10 -> 11; matrix products, arithmetic and copies ran while one was open for 8% -> 7% of each run, Pallas kernels for 0% -> 4%
where the time goes in v3:
time: 313 us; the launch traced here: 312 us
  waiting for transfers between devices  137 us (44%)
  starting transfers between devices  114 us (36%)
  Pallas kernels  17.7 us (6%)
  between operations  14.5 us (5%)
  other arithmetic  11.8 us (4%)
  local copies, waits for them, and re-layouts  11.7 us (4%)
  matrix products  4.27 us (1%)
    all_to_all x7, starting transfers between devices, exchanged(): return lax.all_to_all(tiles, axis, 0, 0, tiled=True)  89 us
    all_to_all x7, waiting for transfers between devices, exchanged(): return lax.all_to_all(tiles, axis, 0, 0, tiled=True)  59.3 us
    all_gather x1, waiting for transfers between devices, body(): out_proj_own = lax.all_gather(out_proj, ('far', 'near'), axis=0, tiled=True)  53.5 us
    ppermute x10, starting transfers between devices, swapped(): return lax.ppermute(array, axis, [(0, 1), (1, 0)])  25.4 us
    ppermute x10, waiting for transfers between devices, swapped(): return lax.ppermute(array, axis, [(0, 1), (1, 0)])  24.2 us
    pallas_call x4, Pallas kernels, in_vmem(): pl.pallas_call(kernel, out_shape=out_shape, in_specs=jax.tree.map(lambda...  17.7 us
    unnamed x37, local copies, waits for them, and re-layouts  6.6 us
  transfers between devices with their start and end apart: 19, of which 11 were waited for; matrix products, arithmetic and copies ran while one was open for 7% of the time, Pallas kernels for 4%

profile of v3, /device:TPU:80, one launch (start us, length us, event | category | flops | bytes accessed | tf_op | source)
XLA Modules:
  0.0 311.5 jit_solution(613091119578424465)
XLA Ops:
  8.0 0.7 fusion.32
  9.4 41.6 %all-to-all-start = ((bf16[8,16,640]{2,1,0:T(8,128)(2,1)}), bf16[8,16,640]{2,1,0:T(8,128)(2,1)S(1)}, u32[]{:S(2)}, u32[]{:S(2)}) async-start(bf16[8,16,640]{2,1,0:T(8,128)(2,1)} %broadcast_in_dim.114), calls=%async_computation | async-start | bytes 327680 | tf_op jit(solution)/shard_map/all_to_all | solution.py:43
  51.1 0.9 maximum_maximum_fusion
  52.0 5.1 %collective-permute-start = (bf16[272,256]{1,0:T(8,128)(2,1)S(1)}, bf16[272,256]{1,0:T(8,128)(2,1)S(1)}, u32[]{:S(2)}, u32[]{:S(2)}) collective-permute-start(bf16[272,256]{1,0:T(8,128)(2,1)S(1)} %maximum_maximum_fusion), channel_id=1, source_target_pairs={{0,16},{16,0},{1,17},{17,1},{2,18},{18,2},{3,19},{19,3},{4,20},{20... | collective-permute-start | bytes 417800 | tf_op jit(solution)/shard_map/ppermute | solution.py:26
  57.3 0.8 select_reduce_fusion.1
  58.3 0.8 select_reduce_fusion
  59.3 4.5 %collective-permute-done = bf16[272,256]{1,0:T(8,128)(2,1)S(1)} collective-permute-done((bf16[272,256]{1,0:T(8,128)(2,1)S(1)}, bf16[272,256]{1,0:T(8,128)(2,1)S(1)}, u32[]{:S(2)}, u32[]{:S(2)}) %collective-permute-start) | collective-permute-done | bytes 139296 | tf_op jit(solution)/shard_map/ppermute | solution.py:26
  63.9 0.9 pad_maximum_fusion.2
  64.8 2.0 collective-permute-start.1
  67.0 1.3 collective-permute-done.1
  68.3 0.9 pad_maximum_fusion.1
  70.7 0.8 copy.38
  71.5 10.2 %all-to-all-start.1 = ((bf16[8,16,640]{2,1,0:T(8,128)(2,1)}), bf16[8,16,640]{2,1,0:T(8,128)(2,1)S(1)}, u32[]{:S(2)}, u32[]{:S(2)}) async-start(bf16[8,16,640]{2,1,0:T(8,128)(2,1)} %bitcast.16), calls=%async_computation.1 | async-start | bytes 327680 | tf_op jit(solution)/shard_map/all_to_all | solution.py:43
  81.9 1.6 pad_maximum_fusion.gu_refs_0_
  83.4 1.9 collective-permute-start.3
  85.5 53.5 %all-gather.3.cloned.1.call-done.proj_ref = bf16[2048,512]{1,0:T(8,128)(2,1)} async-done(((bf16[128,512]{1,0:T(8,128)(2,1)}), bf16[2048,512]{1,0:T(8,128)(2,1)}) %all-gather.3.cloned.1.call-update) | async-done | bytes 2097168 | tf_op jit(solution)/shard_map/all_gather | solution.py:209
  139.0 1.9 collective-permute-start.2
  142.8 6.9 %all-to-all-start.2 = ((bf16[8,16,768]{2,1,0:T(8,128)(2,1)}), bf16[8,16,768]{2,1,0:T(8,128)(2,1)S(1)}, u32[]{:S(2)}, u32[]{:S(2)}) async-start(bf16[8,16,768]{2,1,0:T(8,128)(2,1)} %broadcast_in_dim.116), calls=%async_computation.2 | async-start | bytes 393216 | tf_op jit(solution)/shard_map/all_to_all | solution.py:43
  149.6 1.2 fusion.3
  150.8 10.0 %all-to-all-done.2.spread_ref = bf16[8,16,768]{2,1,0:T(8,128)(2,1)S(1)} async-done(((bf16[8,16,768]{2,1,0:T(8,128)(2,1)}), bf16[8,16,768]{2,1,0:T(8,128)(2,1)S(1)}, u32[]{:S(2)}, u32[]{:S(2)}) %all-to-all-start.2) | async-done | bytes 196640 | tf_op jit(solution)/shard_map/all_to_all | solution.py:43
  161.4 2.7 shard_map.165.before_ref
  164.2 2.7 shard_map.166
  166.8 7.2 %all-to-all-start.3 = ((bf16[8,16,512]{2,1,0:T(8,128)(2,1)}), bf16[8,16,512]{2,1,0:T(8,128)(2,1)S(1)}, u32[]{:S(2)}, u32[]{:S(2)}) async-start(bf16[8,16,512]{2,1,0:T(8,128)(2,1)} %get-tuple-element.14), calls=%async_computation.3 | async-start | bytes 262144 | tf_op jit(solution)/shard_map/all_to_all | solution.py:43
  174.0 3.5 %collective-permute-start.5 = (bf16[2304,256]{1,0:T(8,128)(2,1)}, bf16[2304,256]{1,0:T(8,128)(2,1)}, u32[]{:S(2)}, u32[]{:S(2)}) collective-permute-start(bf16[2304,256]{1,0:T(8,128)(2,1)} %fusion.3), channel_id=1, source_target_pairs={{0,16},{16,0},{1,17},{17,1},{2,18},{18,2},{3,19},{19,3},{4,20},{20... | collective-permute-start | bytes 3538952 | tf_op jit(solution)/shard_map/ppermute | solution.py:26
  178.1 14.2 %all-to-all-done.3 = bf16[8,16,512]{2,1,0:T(8,128)(2,1)S(1)} async-done(((bf16[8,16,512]{2,1,0:T(8,128)(2,1)}), bf16[8,16,512]{2,1,0:T(8,128)(2,1)S(1)}, u32[]{:S(2)}, u32[]{:S(2)}) %all-to-all-start.3) | async-done | bytes 131104 | tf_op jit(solution)/shard_map/all_to_all | solution.py:43
  192.3 1.2 convolution_convert_fusion
  193.6 4.4 %all-to-all-start.4 = ((bf16[8,96,512]{2,1,0:T(8,128)(2,1)}), bf16[8,96,512]{2,1,0:T(8,128)(2,1)}, u32[]{:S(2)}, u32[]{:S(2)}) async-start(bf16[8,96,512]{2,1,0:T(8,128)(2,1)} %bitcast.131), calls=%async_computation.4 | async-start | bytes 1572864 | tf_op jit(solution)/shard_map/all_to_all | solution.py:43
  198.0 2.0 collective-permute-start.4
  199.9 1.0 fusion.8
  201.0 2.6 collective-permute-start.6
  203.6 10.3 %collective-permute-done.5.gu_refs_0__0_ = bf16[2304,256]{1,0:T(8,128)(2,1)} collective-permute-done((bf16[2304,256]{1,0:T(8,128)(2,1)}, bf16[2304,256]{1,0:T(8,128)(2,1)}, u32[]{:S(2)}, u32[]{:S(2)}) %collective-permute-start.5) | collective-permute-done | bytes 1179680 | tf_op jit(solution)/shard_map/ppermute | solution.py:26
  213.9 1.9 collective-permute-start.7
  215.8 1.3 constant_dynamic-slice_fusion.down_refs_0_
  217.2 2.4 collective-permute-start.9
  219.6 0.9 negate_select_fusion.sign_ref
  221.1 6.7 %shard_map.167 = (f32[96,4096]{1,0:T(8,128)}, bf16[96,4096]{1,0:T(8,128)(2,1)}, f32[96,1]{1,0:T(8,128)}) custom-call(bf16[8,96,512]{2,1,0:T(8,128)(2,1)} %all-to-all-done.4.tiles_ref, f32[1,4096]{1,0:T(1,128)} %bitcast.137, f32[4,4096]{1,0:T(4,128)} %bitcast.136, f32[96,4]{1,0:T(8,128)} %negate_select_fusion.sign_ref, ...), custom_call_target="tpu_custom_call" | custom-call | tf_op jit(solution)/shard_map/pallas_call | solution.py:165
  227.8 5.4 %collective-permute-done.6.gu_refs_0__1_ = bf16[1792,256]{1,0:T(8,128)(2,1)} collective-permute-done((bf16[1792,256]{1,0:T(8,128)(2,1)}, bf16[1792,256]{1,0:T(8,128)(2,1)}, u32[]{:S(2)}, u32[]{:S(2)}) %collective-permute-start.6) | collective-permute-done | bytes 917536 | tf_op jit(solution)/shard_map/ppermute | solution.py:26
  233.2 1.9 collective-permute-start.8
  235.2 2.6 collective-permute-done.8.gu_refs_1__1_
  237.8 0.9 copy-done.6
  238.7 5.7 %shard_map.168 = bf16[8,96,512]{2,1,0:T(8,128)(2,1)} custom-call(bf16[96,4096]{1,0:T(8,128)(2,1)} %get-tuple-element.15.x_ref, f32[96,4096]{1,0:T(8,128)} %get-tuple-element.16.before_ref, f32[96,1]{1,0:T(8,128)} %get-tuple-element.17.share_ref, bf16[2304,256]{1,0:T(8,128)(2,1)} %collective-permute-done.5.gu_refs_0__0_, ...), custom_call_target="tpu_custom_call" | custom-call | tf_op jit(solution)/shard_map/pallas_call | solution.py:165
  244.4 6.8 %all-to-all-start.5 = ((bf16[8,96,512]{2,1,0:T(8,128)(2,1)}), bf16[8,96,512]{2,1,0:T(8,128)(2,1)S(1)}, u32[]{:S(2)}, u32[]{:S(2)}) async-start(bf16[8,96,512]{2,1,0:T(8,128)(2,1)} %shard_map.168), calls=%async_computation.5 | async-start | bytes 1572864 | tf_op jit(solution)/shard_map/all_to_all | solution.py:43
  254.0 0.7 constant_dynamic-update-slice_fusion.22
  254.7 20.0 %all-to-all-done.5 = bf16[8,96,512]{2,1,0:T(8,128)(2,1)S(1)} async-done(((bf16[8,96,512]{2,1,0:T(8,128)(2,1)}), bf16[8,96,512]{2,1,0:T(8,128)(2,1)S(1)}, u32[]{:S(2)}, u32[]{:S(2)}) %all-to-all-start.5) | async-done | bytes 786464 | tf_op jit(solution)/shard_map/all_to_all | solution.py:43
  274.7 0.9 convolution_convert_fusion.1
  275.6 11.9 %all-to-all-start.6 = ((bf16[8,16,512]{2,1,0:T(8,128)(2,1)}), bf16[8,16,512]{2,1,0:T(8,128)(2,1)S(1)}, u32[]{:S(2)}, u32[]{:S(2)}) async-start(bf16[8,16,512]{2,1,0:T(8,128)(2,1)} %bitcast.27), calls=%async_computation.6 | async-start | bytes 262144 | tf_op jit(solution)/shard_map/all_to_all | solution.py:43
  288.9 0.7 constant_dynamic-update-slice_fusion.19
  289.6 14.4 %all-to-all-done.6 = bf16[8,16,512]{2,1,0:T(8,128)(2,1)S(1)} async-done(((bf16[8,16,512]{2,1,0:T(8,128)(2,1)}), bf16[8,16,512]{2,1,0:T(8,128)(2,1)S(1)}, u32[]{:S(2)}, u32[]{:S(2)}) %all-to-all-start.6) | async-done | bytes 131104 | tf_op jit(solution)/shard_map/all_to_all | solution.py:43
  (92 shorter events, 12.3 us)
Async XLA Ops:
  9.4 59.9 %all-to-all-start = ((bf16[8,16,640]{2,1,0:T(8,128)(2,1)}), bf16[8,16,640]{2,1,0:T(8,128)(2,1)S(1)}, u32[]{:S(2)}, u32[]{:S(2)}) async-start(bf16[8,16,640]{2,1,0:T(8,128)(2,1)} %broadcast_in_dim.114), calls=%async_computation | async-start | bytes 327680 | tf_op jit(solution)/shard_map/all_to_all | solution.py:43
  51.0 88.0 %all-gather.3.cloned.1.call-start = ((), (), s32[]{:S(2)}) async-start(), calls=%async_computation.7 | async-start | bytes 2228224 | tf_op jit(solution)/shard_map/all_gather | solution.py:209
  52.0 11.9 %collective-permute-start = (bf16[272,256]{1,0:T(8,128)(2,1)S(1)}, bf16[272,256]{1,0:T(8,128)(2,1)S(1)}, u32[]{:S(2)}, u32[]{:S(2)}) collective-permute-start(bf16[272,256]{1,0:T(8,128)(2,1)S(1)} %maximum_maximum_fusion), channel_id=1, source_target_pairs={{0,16},{16,0},{1,17},{17,1},{2,18},{18,2},{3,19},{19,3},{4,20},{20... | collective-permute-start | bytes 417800 | tf_op jit(solution)/shard_map/ppermute | solution.py:26
  64.8 3.5 %collective-permute-start.1 = (bf16[544,256]{1,0:T(8,128)(2,1)S(1)}, bf16[544,256]{1,0:T(8,128)(2,1)S(1)}, u32[]{:S(2)}, u32[]{:S(2)}) collective-permute-start(bf16[544,256]{1,0:T(8,128)(2,1)S(1)} %pad_maximum_fusion.2), channel_id=1, source_target_pairs={{0,8},{8,0},{1,9},{9,1},{2,10},{10,2},{3,11},{11,3},{4,12},{12,4},... | collective-permute-start | bytes 835592 | tf_op jit(solution)/shard_map/ppermute | solution.py:26
  70.1 11.7 %copy-start = (bf16[1,4096,128]{2,1,0:T(8,128)(2,1)S(1)}, bf16[1,4096,128]{2,1,0:T(8,128)(2,1)}, u32[]{:S(2)}) copy-start(bf16[1,4096,128]{2,1,0:T(8,128)(2,1)} %param.25) | copy-start | bytes 3145732
  70.1 11.7 %copy-start.1 = (bf16[1,4096,128]{2,1,0:T(8,128)(2,1)S(1)}, bf16[1,4096,128]{2,1,0:T(8,128)(2,1)}, u32[]{:S(2)}) copy-start(bf16[1,4096,128]{2,1,0:T(8,128)(2,1)} %param.24) | copy-start | bytes 3145732
  71.5 69.4 %all-to-all-start.1 = ((bf16[8,16,640]{2,1,0:T(8,128)(2,1)}), bf16[8,16,640]{2,1,0:T(8,128)(2,1)S(1)}, u32[]{:S(2)}, u32[]{:S(2)}) async-start(bf16[8,16,640]{2,1,0:T(8,128)(2,1)} %bitcast.16), calls=%async_computation.1 | async-start | bytes 327680 | tf_op jit(solution)/shard_map/all_to_all | solution.py:43
  81.7 134.1 %all-gather.5.cloned.1.call-start = ((), (), s32[]{:S(2)}) async-start(), calls=%async_computation.8 | async-start | bytes 3145728 | tf_op jit(solution)/shard_map/all_gather | solution.py:292
  81.8 60.2 %copy-start.7 = (bf16[16,128]{1,0:T(8,128)(2,1)S(1)}, bf16[16,128]{1,0:T(8,128)(2,1)}, u32[]{:S(2)}) copy-start(bf16[16,128]{1,0:T(8,128)(2,1)} %param.15) | copy-start | bytes 12292
  81.8 60.2 %copy-start.8 = (bf16[16,128]{1,0:T(8,128)(2,1)S(1)}, bf16[16,128]{1,0:T(8,128)(2,1)}, u32[]{:S(2)}) copy-start(bf16[16,128]{1,0:T(8,128)(2,1)} %param.16) | copy-start | bytes 12292
  83.4 137.0 %collective-permute-start.3 = (bf16[4096,256]{1,0:T(8,128)(2,1)}, bf16[4096,256]{1,0:T(8,128)(2,1)}, u32[]{:S(2)}, u32[]{:S(2)}) collective-permute-start(bf16[4096,256]{1,0:T(8,128)(2,1)} %pad_maximum_fusion.gu_refs_0_), channel_id=1, source_target_pairs={{0,8},{8,0},{1,9},{9,1},{2,10},{10,2},{3,11},{11,3},{4,12},{12,4},... | collective-permute-start | bytes 6291464 | tf_op jit(solution)/shard_map/ppermute | solution.py:26
  139.0 25.2 %collective-permute-start.2 = (bf16[2048,512]{1,0:T(8,128)(2,1)}, bf16[2048,512]{1,0:T(8,128)(2,1)}, u32[]{:S(2)}, u32[]{:S(2)}) collective-permute-start(bf16[2048,512]{1,0:T(8,128)(2,1)} %all-gather.3.cloned.1.call-done.proj_ref), channel_id=1, source_target_pairs={{0,8},{8,0},{1,9},{9,1},{2,10},{10,2},{3,11},{11,3},{4,12},{12,4},... | collective-permute-start | bytes 6291464 | tf_op jit(solution)/shard_map/ppermute | solution.py:26
  142.8 18.0 %all-to-all-start.2 = ((bf16[8,16,768]{2,1,0:T(8,128)(2,1)}), bf16[8,16,768]{2,1,0:T(8,128)(2,1)S(1)}, u32[]{:S(2)}, u32[]{:S(2)}) async-start(bf16[8,16,768]{2,1,0:T(8,128)(2,1)} %broadcast_in_dim.116), calls=%async_computation.2 | async-start | bytes 393216 | tf_op jit(solution)/shard_map/all_to_all | solution.py:43
  160.8 0.7 copy-start.4
  166.8 31.2 %copy-start.3 = (bf16[1,128,4096]{2,1,0:T(8,128)(2,1)S(1)}, bf16[1,128,4096]{2,1,0:T(8,128)(2,1)}, u32[]{:S(2)}) copy-start(bf16[1,128,4096]{2,1,0:T(8,128)(2,1)} %param.26) | copy-start | bytes 3145732
  166.8 25.5 %all-to-all-start.3 = ((bf16[8,16,512]{2,1,0:T(8,128)(2,1)}), bf16[8,16,512]{2,1,0:T(8,128)(2,1)S(1)}, u32[]{:S(2)}, u32[]{:S(2)}) async-start(bf16[8,16,512]{2,1,0:T(8,128)(2,1)} %get-tuple-element.14), calls=%async_computation.3 | async-start | bytes 262144 | tf_op jit(solution)/shard_map/all_to_all | solution.py:43
  174.0 39.9 %collective-permute-start.5 = (bf16[2304,256]{1,0:T(8,128)(2,1)}, bf16[2304,256]{1,0:T(8,128)(2,1)}, u32[]{:S(2)}, u32[]{:S(2)}) collective-permute-start(bf16[2304,256]{1,0:T(8,128)(2,1)} %fusion.3), channel_id=1, source_target_pairs={{0,16},{16,0},{1,17},{17,1},{2,18},{18,2},{3,19},{19,3},{4,20},{20... | collective-permute-start | bytes 3538952 | tf_op jit(solution)/shard_map/ppermute | solution.py:26
  193.6 27.6 %all-to-all-start.4 = ((bf16[8,96,512]{2,1,0:T(8,128)(2,1)}), bf16[8,96,512]{2,1,0:T(8,128)(2,1)}, u32[]{:S(2)}, u32[]{:S(2)}) async-start(bf16[8,96,512]{2,1,0:T(8,128)(2,1)} %bitcast.131), calls=%async_computation.4 | async-start | bytes 1572864 | tf_op jit(solution)/shard_map/all_to_all | solution.py:43
  198.0 22.5 %collective-permute-start.4 = (bf16[128,4096]{1,0:T(8,128)(2,1)S(1)}, bf16[128,4096]{1,0:T(8,128)(2,1)}, u32[]{:S(2)}, u32[]{:S(2)}) collective-permute-start(bf16[128,4096]{1,0:T(8,128)(2,1)S(1)} %bitcast.130), channel_id=1, source_target_pairs={{0,8},{8,0},{1,9},{9,1},{2,10},{10,2},{3,11},{11,3},{4,12},{12,4},... | collective-permute-start | bytes 3145736 | tf_op jit(solution)/shard_map/ppermute | solution.py:26
  201.0 32.2 %collective-permute-start.6 = (bf16[1792,256]{1,0:T(8,128)(2,1)}, bf16[1792,256]{1,0:T(8,128)(2,1)}, u32[]{:S(2)}, u32[]{:S(2)}) collective-permute-start(bf16[1792,256]{1,0:T(8,128)(2,1)} %fusion.8), channel_id=1, source_target_pairs={{0,16},{16,0},{1,17},{17,1},{2,18},{18,2},{3,19},{19,3},{4,20},{20... | collective-permute-start | bytes 2752520 | tf_op jit(solution)/shard_map/ppermute | solution.py:26
  213.9 21.3 %collective-permute-start.7 = (bf16[2304,256]{1,0:T(8,128)(2,1)}, bf16[2304,256]{1,0:T(8,128)(2,1)}, u32[]{:S(2)}, u32[]{:S(2)}) collective-permute-start(bf16[2304,256]{1,0:T(8,128)(2,1)} %collective-permute-done.5.gu_refs_0__0_), channel_id=1, source_target_pairs={{0,8},{8,0},{1,9},{9,1},{2,10},{10,2},{3,11},{11,3},{4,12},{12,4},... | collective-permute-start | bytes 3538952 | tf_op jit(solution)/shard_map/ppermute | solution.py:26
  217.2 10.6 %copy-start.2 = (bf16[128,4096]{1,0:T(8,128)(2,1)}, bf16[128,4096]{1,0:T(8,128)(2,1)S(1)}, u32[]{:S(2)}) copy-start(bf16[128,4096]{1,0:T(8,128)(2,1)S(1)} %constant_dynamic-slice_fusion.down_refs_0_) | copy-start | bytes 3145732
  217.2 18.0 %collective-permute-start.9 = (bf16[128,4096]{1,0:T(8,128)(2,1)S(1)}, bf16[128,4096]{1,0:T(8,128)(2,1)S(1)}, u32[]{:S(2)}, u32[]{:S(2)}) collective-permute-start(bf16[128,4096]{1,0:T(8,128)(2,1)S(1)} %constant_dynamic-slice_fusion.down_refs_0_), channel_id=1, source_target_pairs={{0,8},{8,0},{1,9},{9,1},{2,10},{10,2},{3,11},{11,3},{4,12},{12,4},... | collective-permute-start | bytes 3145736 | tf_op jit(solution)/shard_map/ppermute | solution.py:26
  233.2 4.6 %collective-permute-start.8 = (bf16[1792,256]{1,0:T(8,128)(2,1)}, bf16[1792,256]{1,0:T(8,128)(2,1)S(1)}, u32[]{:S(2)}, u32[]{:S(2)}) collective-permute-start(bf16[1792,256]{1,0:T(8,128)(2,1)} %collective-permute-done.6.gu_refs_0__1_), channel_id=1, source_target_pairs={{0,8},{8,0},{1,9},{9,1},{2,10},{10,2},{3,11},{11,3},{4,12},{12,4},... | collective-permute-start | bytes 2752520 | tf_op jit(solution)/shard_map/ppermute | solution.py:26
  235.2 2.6 copy-start.5
  237.8 0.9 copy-start.6
  244.4 59.6 %copy-start.9 = (bf16[16,512]{1,0:T(8,128)(2,1)S(1)}, bf16[16,512]{1,0:T(8,128)(2,1)}, u32[]{:S(2)}) copy-start(bf16[16,512]{1,0:T(8,128)(2,1)} %get-tuple-element.9) | copy-start | bytes 49156
  244.4 30.2 %all-to-all-start.5 = ((bf16[8,96,512]{2,1,0:T(8,128)(2,1)}), bf16[8,96,512]{2,1,0:T(8,128)(2,1)S(1)}, u32[]{:S(2)}, u32[]{:S(2)}) async-start(bf16[8,96,512]{2,1,0:T(8,128)(2,1)} %shard_map.168), calls=%async_computation.5 | async-start | bytes 1572864 | tf_op jit(solution)/shard_map/all_to_all | solution.py:43
  275.6 28.4 %all-to-all-start.6 = ((bf16[8,16,512]{2,1,0:T(8,128)(2,1)}), bf16[8,16,512]{2,1,0:T(8,128)(2,1)S(1)}, u32[]{:S(2)}, u32[]{:S(2)}) async-start(bf16[8,16,512]{2,1,0:T(8,128)(2,1)} %bitcast.27), calls=%async_computation.6 | async-start | bytes 262144 | tf_op jit(solution)/shard_map/all_to_all | solution.py:43
  289.6 15.1 %copy-start.10 = (bf16[16,1024]{1,0:T(8,128)(2,1)}, bf16[16,1024]{1,0:T(8,128)(2,1)S(1)}, u32[]{:S(2)}) copy-start(bf16[16,1024]{1,0:T(8,128)(2,1)S(1)} %get-tuple-element.38) | copy-start | bytes 98308
  289.6 15.1 %copy-start.11 = (bf16[16,1024]{1,0:T(8,128)(2,1)}, bf16[16,1024]{1,0:T(8,128)(2,1)S(1)}, u32[]{:S(2)}) copy-start(bf16[16,1024]{1,0:T(8,128)(2,1)S(1)} %get-tuple-element.39) | copy-start | bytes 98308
Sparse Core Ops, SparseCore 0:
  57.3 81.6 all-gather.2
  142.1 51.0 all-gather.4

commit v4 on v3

--- a/solution.py
+++ b/solution.py
@@ -19,7 +19,7 @@
 TOKENS = ("groups", "far", "near", "core")
 SHARE = ("near", "core")
 CLASS = ("far",)
-EARLY_PART = 9 / 16
+CUTS = (4 / 16, 13 / 16)
 
 
 def swapped(array, axis):
@@ -72,27 +72,69 @@
     return jnp.dot(a, b, preferred_element_type=jnp.float32)
 
 
-def hidden_units(x_ref, parts_of_each):
-    both, at = None, 0
-    for refs in zip(*parts_of_each):
-        size = refs[0].shape[0]
-        piece = dot(
-            x_ref[:, at : at + size], jnp.concatenate([ref[...] for ref in refs], axis=1)
-        )
-        both, at = piece if both is None else both + piece, at + size
-    width = refs[0].shape[1] // 2
-    hidden = []
-    for i in range(len(refs)):
-        gate = both[:, 2 * i * width : (2 * i + 1) * width]
-        up = both[:, (2 * i + 1) * width : (2 * i + 2) * width]
-        hidden.append((gate * jax.nn.sigmoid(gate) * up).astype(jnp.bfloat16))
-    return jnp.concatenate(hidden, axis=1)
-
-
-def first_expert_kernel(
-    tiles_ref, gain_ref, router_ref, sign_ref, gu_refs, down_refs, out_ref, x_ref, share_ref
+def row_chunks(parts_of_each):
+    edges = {0}
+    for parts in parts_of_each:
+        at = 0
+        for size in parts:
+            edges.add(at + size)
+            at += size
+    edges = sorted(edges)
+    fine = [edges[0]]
+    for edge in edges[1:]:
+        while edge - fine[-1] > 1280:
+            fine.append(fine[-1] + 1024)
+        fine.append(edge)
+    chunks = []
+    for first, last in zip(fine, fine[1:]):
+        sources = []
+        for parts in parts_of_each:
+            at = 0
+            for k, size in enumerate(parts):
+                if at <= first < at + size:
+                    sources.append((k, first - at))
+                at += size
+        chunks.append((first, last - first, sources))
+    return chunks
+
+
+def expert_kernel(
+    tiles_ref,
+    gain_ref,
+    router_ref,
+    sign_ref,
+    gu_refs,
+    down_refs,
+    out_ref,
+    x_ref,
+    both_ref,
+    gu_held,
+    down_held,
+    gu_sem,
+    down_sem,
 ):
     count, _, columns = tiles_ref.shape
+    devices = len(gu_refs)
+    width = down_refs[0].shape[0]
+    chunks = row_chunks([[ref.shape[0] for ref in parts] for parts in gu_refs])
+    copies = []
+    for c, (first, length, sources) in enumerate(chunks):
+        for d, (k, at) in enumerate(sources):
+            copy = pltpu.make_async_copy(
+                gu_refs[d][k].at[pl.ds(at, length)],
+                gu_held.at[pl.ds(first, length), pl.ds(d * 2 * width, 2 * width)],
+                gu_sem.at[c * devices + d],
+            )
+            copy.start()
+            copies.append(copy)
+    down_copies = []
+    for d in range(devices):
+        copy = pltpu.make_async_copy(
+            down_refs[d], down_held.at[pl.ds(d * width, width)], down_sem.at[d]
+        )
+        copy.start()
+        down_copies.append(copy)
+
     squares = 0.0
     for i in range(count):
         tile = tiles_ref[i].astype(jnp.float32)
@@ -107,24 +149,47 @@
         for e in range(EXPERTS):
             part = jnp.sum(rounded * router_ref[e : e + 1, span], axis=1, keepdims=True)
             logit = logit + part * sign_ref[:, e : e + 1]
-    share_ref[...] = jax.nn.sigmoid(logit)
-    hidden = hidden_units(x_ref, [(ref,) for ref in gu_refs])
+    share = jax.nn.sigmoid(logit)
+
+    for c, (first, length, _) in enumerate(chunks):
+        for d in range(devices):
+            copies[c * devices + d].wait()
+        span = slice(first, first + length)
+        piece = dot(x_ref[:, span], gu_held[span, :])
+        both_ref[...] = piece if c == 0 else both_ref[...] + piece
+    hidden = []
+    for d in range(devices):
+        gate = both_ref[:, 2 * d * width : (2 * d + 1) * width]
+        up = both_ref[:, (2 * d + 1) * width : (2 * d + 2) * width]
+        hidden.append((gate * jax.nn.sigmoid(gate) * up).astype(jnp.bfloat16))
+    hidden = jnp.concatenate(hidden, axis=1)
+    for copy in down_copies:
+        copy.wait()
     for i in range(count):
         span = slice(i * columns, (i + 1) * columns)
-        out_ref[:, span] = dot(
-            hidden, jnp.concatenate([ref[:, span] for ref in down_refs], axis=0)
-        )
-
-
-def last_expert_kernel(x_ref, before_ref, share_ref, gu_refs, down_refs, out_ref):
-    count, _, columns = out_ref.shape
-    hidden = hidden_units(x_ref, gu_refs)
-    for i in range(count):
-        span = slice(i * columns, (i + 1) * columns)
-        piece = before_ref[:, span] + dot(
-            hidden, jnp.concatenate([ref[:, span] for ref in down_refs], axis=0)
-        )
-        out_ref[i] = (piece * share_ref[...]).astype(out_ref.dtype)
+        out_ref[i] = (dot(hidden, down_held[:, span]) * share).astype(out_ref.dtype)
+
+
+def expert_call(out_shape, tiles, gain, router, sign, gate_ups, downs):
+    vmem = pl.BlockSpec(memory_space=pltpu.VMEM)
+    anywhere = pl.BlockSpec(memory_space=pl.ANY)
+    rows, model = tiles.shape[1], tiles.shape[0] * tiles.shape[2]
+    hidden = downs[0].shape[0]
+    chunks = row_chunks([[g.shape[0] for g in parts] for parts in gate_ups])
+    return pl.pallas_call(
+        expert_kernel,
+        out_shape=out_shape,
+        in_specs=[vmem] * 4 + jax.tree.map(lambda _: anywhere, [gate_ups, downs]),
+        out_specs=vmem,
+        scratch_shapes=[
+            pltpu.VMEM((rows, model), jnp.bfloat16),
+            pltpu.VMEM((rows, len(downs) * 2 * hidden), jnp.float32),
+            pltpu.VMEM((model, len(downs) * 2 * hidden), jnp.bfloat16),
+            pltpu.VMEM((len(downs) * hidden, model), jnp.bfloat16),
+            pltpu.SemaphoreType.DMA((len(chunks) * len(downs),)),
+            pltpu.SemaphoreType.DMA((len(downs),)),
+        ],
+    )(tiles, gain, router, sign, gate_ups, downs)
 
 
 def heads_of(spread_ref, i, rows, width, other):
@@ -209,6 +274,15 @@
     out_proj_own = lax.all_gather(out_proj, ("far", "near"), axis=0, tiled=True)
     out_proj_other = swapped(out_proj_own, "core")
 
+    model = w_gate.shape[1]
+    cuts = [int(model * c) for c in CUTS]
+    gate_up = jnp.concatenate([w_gate[0], w_up[0]], axis=1)
+    down = w_down[0]
+    gate_up_core = swapped(gate_up, "core")
+    down_core = swapped(down, "core")
+    zeroth_pair = swapped(gate_up[: cuts[0]], "near")
+    zeroth_cross = swapped(zeroth_pair, "core")
+
     ids_wide = jnp.pad(expert_ids.astype(bf16), ((0, 0), (0, LANES - expert_ids.shape[1])))
     query_class = sent_to_all(jnp.concatenate([queries, ids_wide], axis=1), CLASS)
     query_class = query_class.reshape(rows, width + LANES)
@@ -242,15 +316,8 @@
     message = jnp.concatenate([partial[j].astype(bf16) for j in range(q_per)] + [notes], axis=1)
     parts = exchanged(message.reshape(count, tok, width + LANES), CLASS)
 
-    model = w_gate.shape[1]
-    cut = int(model * EARLY_PART)
-    gate_up = jnp.concatenate([w_gate[0], w_up[0]], axis=1)
-    down = w_down[0]
-    gate_up_core = swapped(gate_up, "core")
-    down_core = swapped(down, "core")
-    first_pair = swapped(after(gate_up[:cut], parts), "near")
+    first_pair = swapped(after(gate_up[cuts[0] : cuts[1]], parts), "near")
     first_cross = swapped(first_pair, "core")
-
     part_shift = parts[:, :, width : width + q_per].astype(f32)
     part_total = parts[:, :, width + q_per : width + 2 * q_per].astype(f32) + parts[
         :, :, width + 2 * q_per : width + 3 * q_per
@@ -298,7 +365,8 @@
     class_rows = rows
     class_width = attended.shape[1]
     class_attended = exchanged(attended_copies, CLASS).reshape(class_rows, class_width)
-    second_pair = swapped(after(gate_up[cut:], class_attended), "near")
+    second_pair = swapped(after(gate_up[cuts[1] :], class_attended), "near")
+    second_cross = swapped(second_pair, "core")
     experts = jnp.arange(EXPERTS, dtype=jnp.int32)
     first_pick = (ids[:, 0:1] == experts[None, :]).astype(f32)
     second_pick = (ids[:, 1:2] == experts[None, :]).astype(f32)
@@ -321,29 +389,19 @@
     my_selection = lax.dynamic_index_in_dim(selection, mine, axis=0, keepdims=False)
     slot_member = jnp.dot(my_selection, member.astype(bf16), preferred_element_type=f32)
     sign = jnp.where((experts == mine)[None, :], slot_member, -slot_member)
-    near_out, normed, share = in_vmem(
-        first_expert_kernel,
-        (
-            shape((slot_count, model), f32),
-            shape((slot_count, model), bf16),
-            shape((slot_count, 1), f32),
-        ),
+    outgoing = expert_call(
+        shape((rep_count, slot_count, class_width), bf16),
         arrived,
         norm_gain[None, :],
         router.T,
         sign,
-        (gate_up, gate_up_core),
-        (down, down_core),
-    )
-    second_cross = swapped(after(second_pair, near_out), "core")
-    outgoing = in_vmem(
-        last_expert_kernel,
-        shape((rep_count, slot_count, class_width), bf16),
-        normed,
-        near_out,
-        share,
-        ((first_pair, second_pair), (first_cross, second_cross)),
-        (down_pair, down_cross),
+        [
+            [gate_up],
+            [gate_up_core],
+            [zeroth_pair, first_pair, second_pair],
+            [zeroth_cross, first_cross, second_cross],
+        ],
+        [down, down_core, down_pair, down_cross],
     )
     returned = exchanged(outgoing, "rep")
 

time: 313 us -> 317 us (1.013)
  waiting for transfers between devices: 137 us -> 141 us
    ppermute x10 -> x12, waiting for transfers between devices: 24.2 us -> 48.8 us  [swapped(): return lax.ppermute(array, axis, [(0, 1), (1, 0)])]
    all_gather x1, waiting for transfers between devices: 53.5 us -> 40 us  [body(): out_proj_own = lax.all_gather(out_proj, ('far', 'near'), axis=0, tiled=True)]
    pallas_call x4 -> x2, Pallas kernels: 17.7 us -> 5.36 us  [in_vmem(): pl.pallas_call(kernel, out_shape=out_shape, in_specs=jax.tree.map(lambda...]
    pallas_call x0 -> x1, Pallas kernels: none -> 9.72 us  [expert_call(): pl.pallas_call(expert_kernel, out_shape=out_shape, in_specs=[vmem] * 4 +...]
    all_to_all x7, waiting for transfers between devices: 59.3 us -> 51.8 us  [exchanged(): return lax.all_to_all(tiles, axis, 0, 0, tiled=True)]
    ppermute x10 -> x12, starting transfers between devices: 25.4 us -> 28.7 us  [swapped(): return lax.ppermute(array, axis, [(0, 1), (1, 0)])]
  transfers between devices with their start and end apart: 19 -> 21, of which waited for: 11 -> 11; matrix products, arithmetic and copies ran while one was open for 7% -> 7% of each run, Pallas kernels for 4% -> 2%
where the time goes in v4:
time: 317 us; the launch traced here: 315 us
  waiting for transfers between devices  141 us (44%)
  starting transfers between devices  117 us (37%)
  Pallas kernels  15.1 us (5%)
  between operations  14.6 us (5%)
  other arithmetic  12.1 us (4%)
  local copies, waits for them, and re-layouts  10.8 us (3%)
  matrix products  4.33 us (1%)
    all_to_all x7, starting transfers between devices, exchanged(): return lax.all_to_all(tiles, axis, 0, 0, tiled=True)  88.5 us
    all_to_all x7, waiting for transfers between devices, exchanged(): return lax.all_to_all(tiles, axis, 0, 0, tiled=True)  51.8 us
    ppermute x12, waiting for transfers between devices, swapped(): return lax.ppermute(array, axis, [(0, 1), (1, 0)])  48.8 us
    all_gather x1, waiting for transfers between devices, body(): out_proj_own = lax.all_gather(out_proj, ('far', 'near'), axis=0, tiled=True)  40 us
    ppermute x12, starting transfers between devices, swapped(): return lax.ppermute(array, axis, [(0, 1), (1, 0)])  28.7 us
    pallas_call x1, Pallas kernels, expert_call(): pl.pallas_call(expert_kernel, out_shape=out_shape, in_specs=[vmem] * 4 +...  9.72 us
  transfers between devices with their start and end apart: 21, of which 11 were waited for; matrix products, arithmetic and copies ran while one was open for 7% of the time, Pallas kernels for 2%

profile of v4, /device:TPU:80, one launch (start us, length us, event | category | flops | bytes accessed | tf_op | source)
XLA Modules:
  0.0 315.0 jit_solution(5320114439580560820)
XLA Ops:
  8.0 0.7 fusion.33
  9.4 41.6 %all-to-all-start = ((bf16[8,16,640]{2,1,0:T(8,128)(2,1)}), bf16[8,16,640]{2,1,0:T(8,128)(2,1)S(1)}, u32[]{:S(2)}, u32[]{:S(2)}) async-start(bf16[8,16,640]{2,1,0:T(8,128)(2,1)} %broadcast_in_dim.114), calls=%async_computation | async-start | bytes 327680 | tf_op jit(solution)/shard_map/all_to_all | solution.py:43
  51.1 0.9 maximum_maximum_fusion
  52.0 5.1 %collective-permute-start = (bf16[272,256]{1,0:T(8,128)(2,1)S(1)}, bf16[272,256]{1,0:T(8,128)(2,1)S(1)}, u32[]{:S(2)}, u32[]{:S(2)}) collective-permute-start(bf16[272,256]{1,0:T(8,128)(2,1)S(1)} %maximum_maximum_fusion), channel_id=1, source_target_pairs={{0,16},{16,0},{1,17},{17,1},{2,18},{18,2},{3,19},{19,3},{4,20},{20... | collective-permute-start | bytes 417800 | tf_op jit(solution)/shard_map/ppermute | solution.py:26
  57.3 0.8 select_reduce_fusion.1
  58.2 0.8 select_reduce_fusion
  59.3 4.6 %collective-permute-done = bf16[272,256]{1,0:T(8,128)(2,1)S(1)} collective-permute-done((bf16[272,256]{1,0:T(8,128)(2,1)S(1)}, bf16[272,256]{1,0:T(8,128)(2,1)S(1)}, u32[]{:S(2)}, u32[]{:S(2)}) %collective-permute-start) | collective-permute-done | bytes 139296 | tf_op jit(solution)/shard_map/ppermute | solution.py:26
  63.9 0.9 pad_maximum_fusion.2
  64.8 2.0 collective-permute-start.1
  67.0 1.3 collective-permute-done.1
  68.3 0.9 pad_maximum_fusion.1
  70.8 0.8 copy.38
  71.6 10.2 %all-to-all-start.1 = ((bf16[8,16,640]{2,1,0:T(8,128)(2,1)}), bf16[8,16,640]{2,1,0:T(8,128)(2,1)S(1)}, u32[]{:S(2)}, u32[]{:S(2)}) async-start(bf16[8,16,640]{2,1,0:T(8,128)(2,1)} %bitcast.16), calls=%async_computation.1 | async-start | bytes 327680 | tf_op jit(solution)/shard_map/all_to_all | solution.py:43
  81.9 0.8 fusion.8
  82.7 3.3 %collective-permute-start.4 = (bf16[1024,256]{1,0:T(8,128)(2,1)}, bf16[1024,256]{1,0:T(8,128)(2,1)}, u32[]{:S(2)}, u32[]{:S(2)}) collective-permute-start(bf16[1024,256]{1,0:T(8,128)(2,1)} %fusion.8), channel_id=1, source_target_pairs={{0,16},{16,0},{1,17},{17,1},{2,18},{18,2},{3,19},{19,3},{4,20},{20... | collective-permute-start | bytes 1572872 | tf_op jit(solution)/shard_map/ppermute | solution.py:26
  86.0 2.0 collective-permute-start.10
  88.1 11.8 %all-to-all-done.1 = bf16[8,16,640]{2,1,0:T(8,128)(2,1)S(1)} async-done(((bf16[8,16,640]{2,1,0:T(8,128)(2,1)}), bf16[8,16,640]{2,1,0:T(8,128)(2,1)S(1)}, u32[]{:S(2)}, u32[]{:S(2)}) %all-to-all-start.1) | async-done | bytes 163872 | tf_op jit(solution)/shard_map/all_to_all | solution.py:43
  100.0 40.0 %all-gather.3.cloned.1.call-done.proj_ref = bf16[2048,512]{1,0:T(8,128)(2,1)} async-done(((bf16[128,512]{1,0:T(8,128)(2,1)}), bf16[2048,512]{1,0:T(8,128)(2,1)}) %all-gather.3.cloned.1.call-update) | async-done | bytes 2097168 | tf_op jit(solution)/shard_map/all_gather | solution.py:274
  140.0 1.9 collective-permute-start.2
  143.8 7.1 %all-to-all-start.2 = ((bf16[8,16,768]{2,1,0:T(8,128)(2,1)}), bf16[8,16,768]{2,1,0:T(8,128)(2,1)S(1)}, u32[]{:S(2)}, u32[]{:S(2)}) async-start(bf16[8,16,768]{2,1,0:T(8,128)(2,1)} %broadcast_in_dim.116), calls=%async_computation.2 | async-start | bytes 393216 | tf_op jit(solution)/shard_map/all_to_all | solution.py:43
  150.9 2.1 collective-permute-start.5
  153.0 1.5 pad_maximum_fusion.gu_refs_0__0_
  154.5 2.0 collective-permute-start.3
  156.6 2.4 collective-permute-start.7
  159.0 3.0 all-to-all-done.2.spread_ref
  162.7 2.7 shard_map.165.before_ref
  165.4 2.6 shard_map.166
  168.0 6.6 %all-to-all-start.3 = ((bf16[8,16,512]{2,1,0:T(8,128)(2,1)}), bf16[8,16,512]{2,1,0:T(8,128)(2,1)S(1)}, u32[]{:S(2)}, u32[]{:S(2)}) async-start(bf16[8,16,512]{2,1,0:T(8,128)(2,1)} %get-tuple-element.10), calls=%async_computation.3 | async-start | bytes 262144 | tf_op jit(solution)/shard_map/all_to_all | solution.py:43
  174.6 0.8 slice_convert_fusion
  176.0 30.6 %collective-permute-done.5.gu_refs_2__1_ = bf16[2304,256]{1,0:T(8,128)(2,1)} collective-permute-done((bf16[2304,256]{1,0:T(8,128)(2,1)S(1)}, bf16[2304,256]{1,0:T(8,128)(2,1)}, u32[]{:S(2)}, u32[]{:S(2)}) %collective-permute-start.5) | collective-permute-done | bytes 1179680 | tf_op jit(solution)/shard_map/ppermute | solution.py:26
  206.6 1.9 collective-permute-start.8
  208.6 1.3 convolution_convert_fusion
  209.8 7.5 %all-to-all-start.4 = ((bf16[8,96,512]{2,1,0:T(8,128)(2,1)}), bf16[8,96,512]{2,1,0:T(8,128)(2,1)}, u32[]{:S(2)}, u32[]{:S(2)}) async-start(bf16[8,96,512]{2,1,0:T(8,128)(2,1)} %bitcast.19), calls=%async_computation.4 | async-start | bytes 1572864 | tf_op jit(solution)/shard_map/all_to_all | solution.py:43
  217.3 1.3 constant_dynamic-slice_fusion.down_refs_2_
  218.7 2.2 collective-permute-start.11
  220.8 0.8 fusion.9
  221.6 1.9 collective-permute-start.6
  223.6 11.5 %collective-permute-done.6.gu_refs_2__2_ = bf16[768,256]{1,0:T(8,128)(2,1)S(1)} collective-permute-done((bf16[768,256]{1,0:T(8,128)(2,1)}, bf16[768,256]{1,0:T(8,128)(2,1)S(1)}, u32[]{:S(2)}, u32[]{:S(2)}) %collective-permute-start.6) | collective-permute-done | bytes 393248 | tf_op jit(solution)/shard_map/ppermute | solution.py:26
  235.1 1.9 collective-permute-start.9
  237.1 0.9 negate_select_fusion.sign_ref
  237.9 0.8 collective-permute-done.9.gu_refs_3__2_
  238.7 2.5 all-to-all-done.4.tiles_ref
  241.3 9.7 %shard_map.167 = bf16[8,96,512]{2,1,0:T(8,128)(2,1)} custom-call(bf16[8,96,512]{2,1,0:T(8,128)(2,1)} %all-to-all-done.4.tiles_ref, f32[1,4096]{1,0:T(1,128)} %bitcast.135, f32[4,4096]{1,0:T(4,128)} %bitcast.134, f32[96,4]{1,0:T(8,128)} %negate_select_fusion.sign_ref, bf16[4096,256]{1,0:T(8,128)(2,1)} %pad_maximum_fusion.gu_refs_0__0_, ...), custom_call_target="tpu_custom_call" | custom-call | tf_op jit(solution)/shard_map/pallas_call | solution.py:179
  251.0 5.4 %all-to-all-start.5 = ((bf16[8,96,512]{2,1,0:T(8,128)(2,1)}), bf16[8,96,512]{2,1,0:T(8,128)(2,1)S(1)}, u32[]{:S(2)}, u32[]{:S(2)}) async-start(bf16[8,96,512]{2,1,0:T(8,128)(2,1)} %shard_map.167), calls=%async_computation.5 | async-start | bytes 1572864 | tf_op jit(solution)/shard_map/all_to_all | solution.py:43
  259.8 20.0 %all-to-all-done.5 = bf16[8,96,512]{2,1,0:T(8,128)(2,1)S(1)} async-done(((bf16[8,96,512]{2,1,0:T(8,128)(2,1)}), bf16[8,96,512]{2,1,0:T(8,128)(2,1)S(1)}, u32[]{:S(2)}, u32[]{:S(2)}) %all-to-all-start.5) | async-done | bytes 786464 | tf_op jit(solution)/shard_map/all_to_all | solution.py:43
  279.8 0.9 convolution_convert_fusion.1
  280.7 10.2 %all-to-all-start.6 = ((bf16[8,16,512]{2,1,0:T(8,128)(2,1)}), bf16[8,16,512]{2,1,0:T(8,128)(2,1)S(1)}, u32[]{:S(2)}, u32[]{:S(2)}) async-start(bf16[8,16,512]{2,1,0:T(8,128)(2,1)} %bitcast.27), calls=%async_computation.6 | async-start | bytes 262144 | tf_op jit(solution)/shard_map/all_to_all | solution.py:43
  293.0 14.5 %all-to-all-done.6 = bf16[8,16,512]{2,1,0:T(8,128)(2,1)S(1)} async-done(((bf16[8,16,512]{2,1,0:T(8,128)(2,1)}), bf16[8,16,512]{2,1,0:T(8,128)(2,1)S(1)}, u32[]{:S(2)}, u32[]{:S(2)}) %all-to-all-start.6) | async-done | bytes 131104 | tf_op jit(solution)/shard_map/all_to_all | solution.py:43
  (96 shorter events, 13.1 us)
Async XLA Ops:
  9.4 59.9 %all-to-all-start = ((bf16[8,16,640]{2,1,0:T(8,128)(2,1)}), bf16[8,16,640]{2,1,0:T(8,128)(2,1)S(1)}, u32[]{:S(2)}, u32[]{:S(2)}) async-start(bf16[8,16,640]{2,1,0:T(8,128)(2,1)} %broadcast_in_dim.114), calls=%async_computation | async-start | bytes 327680 | tf_op jit(solution)/shard_map/all_to_all | solution.py:43
  51.0 89.0 %all-gather.3.cloned.1.call-start = ((), (), s32[]{:S(2)}) async-start(), calls=%async_computation.7 | async-start | bytes 2228224 | tf_op jit(solution)/shard_map/all_gather | solution.py:274
  52.0 11.9 %collective-permute-start = (bf16[272,256]{1,0:T(8,128)(2,1)S(1)}, bf16[272,256]{1,0:T(8,128)(2,1)S(1)}, u32[]{:S(2)}, u32[]{:S(2)}) collective-permute-start(bf16[272,256]{1,0:T(8,128)(2,1)S(1)} %maximum_maximum_fusion), channel_id=1, source_target_pairs={{0,16},{16,0},{1,17},{17,1},{2,18},{18,2},{3,19},{19,3},{4,20},{20... | collective-permute-start | bytes 417800 | tf_op jit(solution)/shard_map/ppermute | solution.py:26
  64.8 3.5 %collective-permute-start.1 = (bf16[544,256]{1,0:T(8,128)(2,1)S(1)}, bf16[544,256]{1,0:T(8,128)(2,1)S(1)}, u32[]{:S(2)}, u32[]{:S(2)}) collective-permute-start(bf16[544,256]{1,0:T(8,128)(2,1)S(1)} %pad_maximum_fusion.2), channel_id=1, source_target_pairs={{0,8},{8,0},{1,9},{9,1},{2,10},{10,2},{3,11},{11,3},{4,12},{12,4},... | collective-permute-start | bytes 835592 | tf_op jit(solution)/shard_map/ppermute | solution.py:26
  69.3 0.9 copy-start.4
  70.1 11.7 %copy-start = (bf16[1,4096,128]{2,1,0:T(8,128)(2,1)S(1)}, bf16[1,4096,128]{2,1,0:T(8,128)(2,1)}, u32[]{:S(2)}) copy-start(bf16[1,4096,128]{2,1,0:T(8,128)(2,1)} %param.25) | copy-start | bytes 3145732
  70.1 11.7 %copy-start.1 = (bf16[1,4096,128]{2,1,0:T(8,128)(2,1)S(1)}, bf16[1,4096,128]{2,1,0:T(8,128)(2,1)}, u32[]{:S(2)}) copy-start(bf16[1,4096,128]{2,1,0:T(8,128)(2,1)} %param.24) | copy-start | bytes 3145732
  71.6 28.4 %all-to-all-start.1 = ((bf16[8,16,640]{2,1,0:T(8,128)(2,1)}), bf16[8,16,640]{2,1,0:T(8,128)(2,1)S(1)}, u32[]{:S(2)}, u32[]{:S(2)}) async-start(bf16[8,16,640]{2,1,0:T(8,128)(2,1)} %bitcast.16), calls=%async_computation.1 | async-start | bytes 327680 | tf_op jit(solution)/shard_map/all_to_all | solution.py:43
  81.8 135.6 %all-gather.5.cloned.1.call-start = ((), (), s32[]{:S(2)}) async-start(), calls=%async_computation.8 | async-start | bytes 3145728 | tf_op jit(solution)/shard_map/all_gather | solution.py:359
  82.7 73.9 %collective-permute-start.4 = (bf16[1024,256]{1,0:T(8,128)(2,1)}, bf16[1024,256]{1,0:T(8,128)(2,1)}, u32[]{:S(2)}, u32[]{:S(2)}) collective-permute-start(bf16[1024,256]{1,0:T(8,128)(2,1)} %fusion.8), channel_id=1, source_target_pairs={{0,16},{16,0},{1,17},{17,1},{2,18},{18,2},{3,19},{19,3},{4,20},{20... | collective-permute-start | bytes 1572872 | tf_op jit(solution)/shard_map/ppermute | solution.py:26
  86.0 57.1 %copy-start.7 = (bf16[16,128]{1,0:T(8,128)(2,1)S(1)}, bf16[16,128]{1,0:T(8,128)(2,1)}, u32[]{:S(2)}) copy-start(bf16[16,128]{1,0:T(8,128)(2,1)} %param.15) | copy-start | bytes 12292
  86.0 57.1 %copy-start.8 = (bf16[16,128]{1,0:T(8,128)(2,1)S(1)}, bf16[16,128]{1,0:T(8,128)(2,1)}, u32[]{:S(2)}) copy-start(bf16[16,128]{1,0:T(8,128)(2,1)} %param.16) | copy-start | bytes 12292
  86.0 151.9 %collective-permute-start.10 = (bf16[128,4096]{1,0:T(8,128)(2,1)}, bf16[128,4096]{1,0:T(8,128)(2,1)}, u32[]{:S(2)}, u32[]{:S(2)}) collective-permute-start(bf16[128,4096]{1,0:T(8,128)(2,1)} %bitcast.25.down_refs_0_), channel_id=1, source_target_pairs={{0,8},{8,0},{1,9},{9,1},{2,10},{10,2},{3,11},{11,3},{4,12},{12,4},... | collective-permute-start | bytes 3145736 | tf_op jit(solution)/shard_map/ppermute | solution.py:26
  140.0 25.4 %collective-permute-start.2 = (bf16[2048,512]{1,0:T(8,128)(2,1)}, bf16[2048,512]{1,0:T(8,128)(2,1)}, u32[]{:S(2)}, u32[]{:S(2)}) collective-permute-start(bf16[2048,512]{1,0:T(8,128)(2,1)} %all-gather.3.cloned.1.call-done.proj_ref), channel_id=1, source_target_pairs={{0,8},{8,0},{1,9},{9,1},{2,10},{10,2},{3,11},{11,3},{4,12},{12,4},... | collective-permute-start | bytes 6291464 | tf_op jit(solution)/shard_map/ppermute | solution.py:26
  143.8 18.2 %all-to-all-start.2 = ((bf16[8,16,768]{2,1,0:T(8,128)(2,1)}), bf16[8,16,768]{2,1,0:T(8,128)(2,1)S(1)}, u32[]{:S(2)}, u32[]{:S(2)}) async-start(bf16[8,16,768]{2,1,0:T(8,128)(2,1)} %broadcast_in_dim.116), calls=%async_computation.2 | async-start | bytes 393216 | tf_op jit(solution)/shard_map/all_to_all | solution.py:43
  150.9 55.7 %collective-permute-start.5 = (bf16[2304,256]{1,0:T(8,128)(2,1)S(1)}, bf16[2304,256]{1,0:T(8,128)(2,1)}, u32[]{:S(2)}, u32[]{:S(2)}) collective-permute-start(bf16[2304,256]{1,0:T(8,128)(2,1)S(1)} %fusion.3), channel_id=1, source_target_pairs={{0,16},{16,0},{1,17},{17,1},{2,18},{18,2},{3,19},{19,3},{4,20},{20... | collective-permute-start | bytes 3538952 | tf_op jit(solution)/shard_map/ppermute | solution.py:26
  154.5 83.4 %collective-permute-start.3 = (bf16[4096,256]{1,0:T(8,128)(2,1)}, bf16[4096,256]{1,0:T(8,128)(2,1)}, u32[]{:S(2)}, u32[]{:S(2)}) collective-permute-start(bf16[4096,256]{1,0:T(8,128)(2,1)} %pad_maximum_fusion.gu_refs_0__0_), channel_id=1, source_target_pairs={{0,8},{8,0},{1,9},{9,1},{2,10},{10,2},{3,11},{11,3},{4,12},{12,4},... | collective-permute-start | bytes 6291464 | tf_op jit(solution)/shard_map/ppermute | solution.py:26
  156.6 65.0 %collective-permute-start.7 = (bf16[1024,256]{1,0:T(8,128)(2,1)}, bf16[1024,256]{1,0:T(8,128)(2,1)}, u32[]{:S(2)}, u32[]{:S(2)}) collective-permute-start(bf16[1024,256]{1,0:T(8,128)(2,1)} %collective-permute-done.4.gu_refs_2__0_), channel_id=1, source_target_pairs={{0,8},{8,0},{1,9},{9,1},{2,10},{10,2},{3,11},{11,3},{4,12},{12,4},... | collective-permute-start | bytes 1572872 | tf_op jit(solution)/shard_map/ppermute | solution.py:26
  162.0 0.7 copy-start.3
  168.0 40.5 %all-to-all-start.3 = ((bf16[8,16,512]{2,1,0:T(8,128)(2,1)}), bf16[8,16,512]{2,1,0:T(8,128)(2,1)S(1)}, u32[]{:S(2)}, u32[]{:S(2)}) async-start(bf16[8,16,512]{2,1,0:T(8,128)(2,1)} %get-tuple-element.10), calls=%async_computation.3 | async-start | bytes 262144 | tf_op jit(solution)/shard_map/all_to_all | solution.py:43
  206.6 31.3 %collective-permute-start.8 = (bf16[2304,256]{1,0:T(8,128)(2,1)}, bf16[2304,256]{1,0:T(8,128)(2,1)}, u32[]{:S(2)}, u32[]{:S(2)}) collective-permute-start(bf16[2304,256]{1,0:T(8,128)(2,1)} %collective-permute-done.5.gu_refs_2__1_), channel_id=1, source_target_pairs={{0,8},{8,0},{1,9},{9,1},{2,10},{10,2},{3,11},{11,3},{4,12},{12,4},... | collective-permute-start | bytes 3538952 | tf_op jit(solution)/shard_map/ppermute | solution.py:26
  209.8 31.4 %all-to-all-start.4 = ((bf16[8,96,512]{2,1,0:T(8,128)(2,1)}), bf16[8,96,512]{2,1,0:T(8,128)(2,1)}, u32[]{:S(2)}, u32[]{:S(2)}) async-start(bf16[8,96,512]{2,1,0:T(8,128)(2,1)} %bitcast.19), calls=%async_computation.4 | async-start | bytes 1572864 | tf_op jit(solution)/shard_map/all_to_all | solution.py:43
  218.7 22.6 %copy-start.2 = (bf16[128,4096]{1,0:T(8,128)(2,1)}, bf16[128,4096]{1,0:T(8,128)(2,1)S(1)}, u32[]{:S(2)}) copy-start(bf16[128,4096]{1,0:T(8,128)(2,1)S(1)} %constant_dynamic-slice_fusion.down_refs_2_) | copy-start | bytes 3145732
  218.7 19.3 %collective-permute-start.11 = (bf16[128,4096]{1,0:T(8,128)(2,1)S(1)}, bf16[128,4096]{1,0:T(8,128)(2,1)}, u32[]{:S(2)}, u32[]{:S(2)}) collective-permute-start(bf16[128,4096]{1,0:T(8,128)(2,1)S(1)} %constant_dynamic-slice_fusion.down_refs_2_), channel_id=1, source_target_pairs={{0,8},{8,0},{1,9},{9,1},{2,10},{10,2},{3,11},{11,3},{4,12},{12,4},... | collective-permute-start | bytes 3145736 | tf_op jit(solution)/shard_map/ppermute | solution.py:26
  221.6 13.4 %collective-permute-start.6 = (bf16[768,256]{1,0:T(8,128)(2,1)}, bf16[768,256]{1,0:T(8,128)(2,1)S(1)}, u32[]{:S(2)}, u32[]{:S(2)}) collective-permute-start(bf16[768,256]{1,0:T(8,128)(2,1)} %fusion.9), channel_id=1, source_target_pairs={{0,16},{16,0},{1,17},{17,1},{2,18},{18,2},{3,19},{19,3},{4,20},{20... | collective-permute-start | bytes 1179656 | tf_op jit(solution)/shard_map/ppermute | solution.py:26
  235.1 6.2 %copy-start.5 = (bf16[768,256]{1,0:T(8,128)(2,1)}, bf16[768,256]{1,0:T(8,128)(2,1)S(1)}, u32[]{:S(2)}) copy-start(bf16[768,256]{1,0:T(8,128)(2,1)S(1)} %collective-permute-done.6.gu_refs_2__2_) | copy-start | bytes 1179652
  235.1 3.6 %collective-permute-start.9 = (bf16[768,256]{1,0:T(8,128)(2,1)S(1)}, bf16[768,256]{1,0:T(8,128)(2,1)S(1)}, u32[]{:S(2)}, u32[]{:S(2)}) collective-permute-start(bf16[768,256]{1,0:T(8,128)(2,1)S(1)} %collective-permute-done.6.gu_refs_2__2_), channel_id=1, source_target_pairs={{0,8},{8,0},{1,9},{9,1},{2,10},{10,2},{3,11},{11,3},{4,12},{12,4},... | collective-permute-start | bytes 1179656 | tf_op jit(solution)/shard_map/ppermute | solution.py:26
  238.7 2.5 copy-start.6
  251.0 56.5 %copy-start.9 = (bf16[16,512]{1,0:T(8,128)(2,1)S(1)}, bf16[16,512]{1,0:T(8,128)(2,1)}, u32[]{:S(2)}) copy-start(bf16[16,512]{1,0:T(8,128)(2,1)} %get-tuple-element.5) | copy-start | bytes 49156
  251.0 28.8 %all-to-all-start.5 = ((bf16[8,96,512]{2,1,0:T(8,128)(2,1)}), bf16[8,96,512]{2,1,0:T(8,128)(2,1)S(1)}, u32[]{:S(2)}, u32[]{:S(2)}) async-start(bf16[8,96,512]{2,1,0:T(8,128)(2,1)} %shard_map.167), calls=%async_computation.5 | async-start | bytes 1572864 | tf_op jit(solution)/shard_map/all_to_all | solution.py:43
  280.7 26.7 %all-to-all-start.6 = ((bf16[8,16,512]{2,1,0:T(8,128)(2,1)}), bf16[8,16,512]{2,1,0:T(8,128)(2,1)S(1)}, u32[]{:S(2)}, u32[]{:S(2)}) async-start(bf16[8,16,512]{2,1,0:T(8,128)(2,1)} %bitcast.27), calls=%async_computation.6 | async-start | bytes 262144 | tf_op jit(solution)/shard_map/all_to_all | solution.py:43
  293.0 15.1 %copy-start.10 = (bf16[16,1024]{1,0:T(8,128)(2,1)}, bf16[16,1024]{1,0:T(8,128)(2,1)S(1)}, u32[]{:S(2)}) copy-start(bf16[16,1024]{1,0:T(8,128)(2,1)S(1)} %get-tuple-element.30) | copy-start | bytes 98308
  293.0 15.1 %copy-start.11 = (bf16[16,1024]{1,0:T(8,128)(2,1)}, bf16[16,1024]{1,0:T(8,128)(2,1)S(1)}, u32[]{:S(2)}) copy-start(bf16[16,1024]{1,0:T(8,128)(2,1)S(1)} %get-tuple-element.31) | copy-start | bytes 98308
Sparse Core Ops, SparseCore 0:
  57.3 82.6 all-gather.2
  143.0 66.1 all-gather.4

commit v5 on v4

--- a/solution.py
+++ b/solution.py
@@ -19,7 +19,7 @@
 TOKENS = ("groups", "far", "near", "core")
 SHARE = ("near", "core")
 CLASS = ("far",)
-CUTS = (4 / 16, 13 / 16)
+CUTS = (9 / 32, 28 / 32)
 
 
 def swapped(array, axis):
@@ -135,32 +135,29 @@
         copy.start()
         down_copies.append(copy)
 
-    squares = 0.0
-    for i in range(count):
-        tile = tiles_ref[i].astype(jnp.float32)
-        squares = squares + jnp.sum(tile * tile, axis=1, keepdims=True)
-    scale = lax.rsqrt(squares / (count * columns) + 1e-05)
-    logit = 0.0
-    for i in range(count):
-        span = slice(i * columns, (i + 1) * columns)
-        tile = tiles_ref[i].astype(jnp.float32) * gain_ref[:, span] * scale
-        x_ref[:, span] = tile.astype(jnp.bfloat16)
-        rounded = x_ref[:, span].astype(jnp.float32)
-        for e in range(EXPERTS):
-            part = jnp.sum(rounded * router_ref[e : e + 1, span], axis=1, keepdims=True)
-            logit = logit + part * sign_ref[:, e : e + 1]
-    share = jax.nn.sigmoid(logit)
-
+    squares, logit, done = 0.0, 0.0, 0
     for c, (first, length, _) in enumerate(chunks):
+        while done * columns < first + length:
+            span = slice(done * columns, (done + 1) * columns)
+            tile = tiles_ref[done].astype(jnp.float32)
+            squares = squares + jnp.sum(tile * tile, axis=1, keepdims=True)
+            gained = tile * gain_ref[:, span]
+            x_ref[:, span] = gained.astype(jnp.bfloat16)
+            for e in range(EXPERTS):
+                part = jnp.sum(gained * router_ref[e : e + 1, span], axis=1, keepdims=True)
+                logit = logit + part * sign_ref[:, e : e + 1]
+            done += 1
         for d in range(devices):
             copies[c * devices + d].wait()
         span = slice(first, first + length)
         piece = dot(x_ref[:, span], gu_held[span, :])
         both_ref[...] = piece if c == 0 else both_ref[...] + piece
+    scale = lax.rsqrt(squares / (count * columns) + 1e-05)
+    share = jax.nn.sigmoid(logit * scale)
     hidden = []
     for d in range(devices):
-        gate = both_ref[:, 2 * d * width : (2 * d + 1) * width]
-        up = both_ref[:, (2 * d + 1) * width : (2 * d + 2) * width]
+        gate = both_ref[:, 2 * d * width : (2 * d + 1) * width] * scale
+        up = both_ref[:, (2 * d + 1) * width : (2 * d + 2) * width] * scale
         hidden.append((gate * jax.nn.sigmoid(gate) * up).astype(jnp.bfloat16))
     hidden = jnp.concatenate(hidden, axis=1)
     for copy in down_copies:

time: 317 us -> 315 us (level)
    ppermute x12, waiting for transfers between devices: 48.8 us -> 18.4 us  [swapped(): return lax.ppermute(array, axis, [(0, 1), (1, 0)])]
    all_to_all x7, waiting for transfers between devices: 51.8 us -> 70.2 us  [exchanged(): return lax.all_to_all(tiles, axis, 0, 0, tiled=True)]
    all_gather x1, waiting for transfers between devices: 40 us -> 51 us  [body(): out_proj_own = lax.all_gather(out_proj, ('far', 'near'), axis=0, tiled=True)]
  transfers between devices with their start and end apart: 21 -> 21, of which waited for: 11 -> 11; matrix products, arithmetic and copies ran while one was open for 7% -> 8% of each run, Pallas kernels for 2% -> 2%
where the time goes in v5:
time: 315 us; the launch traced here: 314 us
  waiting for transfers between devices  140 us (44%)
  starting transfers between devices  117 us (37%)
  between operations  14.6 us (5%)
  other arithmetic  13.5 us (4%)
  Pallas kernels  13.1 us (4%)
  local copies, waits for them, and re-layouts  11.3 us (4%)
  matrix products  4.3 us (1%)
    all_to_all x7, starting transfers between devices, exchanged(): return lax.all_to_all(tiles, axis, 0, 0, tiled=True)  87.5 us
    all_to_all x7, waiting for transfers between devices, exchanged(): return lax.all_to_all(tiles, axis, 0, 0, tiled=True)  70.2 us
    all_gather x1, waiting for transfers between devices, body(): out_proj_own = lax.all_gather(out_proj, ('far', 'near'), axis=0, tiled=True)  51 us
    ppermute x12, starting transfers between devices, swapped(): return lax.ppermute(array, axis, [(0, 1), (1, 0)])  29.5 us
    ppermute x12, waiting for transfers between devices, swapped(): return lax.ppermute(array, axis, [(0, 1), (1, 0)])  18.4 us
    pallas_call x1, Pallas kernels, expert_call(): pl.pallas_call(expert_kernel, out_shape=out_shape, in_specs=[vmem] * 4 +...  7.75 us
  transfers between devices with their start and end apart: 21, of which 11 were waited for; matrix products, arithmetic and copies ran while one was open for 8% of the time, Pallas kernels for 2%

profile of v5, /device:TPU:80, one launch (start us, length us, event | category | flops | bytes accessed | tf_op | source)
XLA Modules:
  0.0 313.6 jit_solution(10738980546423796713)
XLA Ops:
  9.4 41.6 %all-to-all-start = ((bf16[8,16,640]{2,1,0:T(8,128)(2,1)}), bf16[8,16,640]{2,1,0:T(8,128)(2,1)S(1)}, u32[]{:S(2)}, u32[]{:S(2)}) async-start(bf16[8,16,640]{2,1,0:T(8,128)(2,1)} %broadcast_in_dim.114), calls=%async_computation | async-start | bytes 327680 | tf_op jit(solution)/shard_map/all_to_all | solution.py:43
  51.1 0.9 maximum_maximum_fusion
  52.0 5.1 %collective-permute-start = (bf16[272,256]{1,0:T(8,128)(2,1)S(1)}, bf16[272,256]{1,0:T(8,128)(2,1)S(1)}, u32[]{:S(2)}, u32[]{:S(2)}) collective-permute-start(bf16[272,256]{1,0:T(8,128)(2,1)S(1)} %maximum_maximum_fusion), channel_id=1, source_target_pairs={{0,16},{16,0},{1,17},{17,1},{2,18},{18,2},{3,19},{19,3},{4,20},{20... | collective-permute-start | bytes 417800 | tf_op jit(solution)/shard_map/ppermute | solution.py:26
  57.3 0.8 select_reduce_fusion.1
  58.3 0.8 select_reduce_fusion
  59.3 4.5 %collective-permute-done = bf16[272,256]{1,0:T(8,128)(2,1)S(1)} collective-permute-done((bf16[272,256]{1,0:T(8,128)(2,1)S(1)}, bf16[272,256]{1,0:T(8,128)(2,1)S(1)}, u32[]{:S(2)}, u32[]{:S(2)}) %collective-permute-start) | collective-permute-done | bytes 139296 | tf_op jit(solution)/shard_map/ppermute | solution.py:26
  63.9 0.9 pad_maximum_fusion.2
  64.8 2.0 collective-permute-start.1
  67.0 1.3 collective-permute-done.1
  68.3 0.9 pad_maximum_fusion.1
  70.8 0.8 copy.38
  71.6 10.2 %all-to-all-start.1 = ((bf16[8,16,640]{2,1,0:T(8,128)(2,1)}), bf16[8,16,640]{2,1,0:T(8,128)(2,1)S(1)}, u32[]{:S(2)}, u32[]{:S(2)}) async-start(bf16[8,16,640]{2,1,0:T(8,128)(2,1)} %bitcast.16), calls=%async_computation.1 | async-start | bytes 327680 | tf_op jit(solution)/shard_map/all_to_all | solution.py:43
  81.9 1.6 pad_maximum_fusion.gu_refs_0__0_
  83.5 1.9 collective-permute-start.3
  85.4 2.6 collective-permute-start.10
  88.2 51.0 %all-gather.3.cloned.1.call-done.proj_ref = bf16[2048,512]{1,0:T(8,128)(2,1)} async-done(((bf16[128,512]{1,0:T(8,128)(2,1)}), bf16[2048,512]{1,0:T(8,128)(2,1)}) %all-gather.3.cloned.1.call-update) | async-done | bytes 2097168 | tf_op jit(solution)/shard_map/all_gather | solution.py:271
  139.2 1.9 collective-permute-start.2
  141.2 2.6 collective-permute-start.5
  145.0 0.7 constant_dynamic-update-slice_fusion.10
  145.8 0.7 constant_dynamic-update-slice_fusion.9
  147.4 6.9 %all-to-all-start.2 = ((bf16[8,16,768]{2,1,0:T(8,128)(2,1)}), bf16[8,16,768]{2,1,0:T(8,128)(2,1)S(1)}, u32[]{:S(2)}, u32[]{:S(2)}) async-start(bf16[8,16,768]{2,1,0:T(8,128)(2,1)} %broadcast_in_dim.116), calls=%async_computation.2 | async-start | bytes 393216 | tf_op jit(solution)/shard_map/all_to_all | solution.py:43
  154.3 0.9 fusion.8
  155.2 3.0 collective-permute-start.4
  158.3 6.8 %all-to-all-done.2.spread_ref = bf16[8,16,768]{2,1,0:T(8,128)(2,1)S(1)} async-done(((bf16[8,16,768]{2,1,0:T(8,128)(2,1)}), bf16[8,16,768]{2,1,0:T(8,128)(2,1)S(1)}, u32[]{:S(2)}, u32[]{:S(2)}) %all-to-all-start.2) | async-done | bytes 196640 | tf_op jit(solution)/shard_map/all_to_all | solution.py:43
  165.8 2.7 shard_map.165.before_ref
  168.5 2.6 shard_map.166
  171.2 6.9 %all-to-all-start.3 = ((bf16[8,16,512]{2,1,0:T(8,128)(2,1)}), bf16[8,16,512]{2,1,0:T(8,128)(2,1)S(1)}, u32[]{:S(2)}, u32[]{:S(2)}) async-start(bf16[8,16,512]{2,1,0:T(8,128)(2,1)} %get-tuple-element.10), calls=%async_computation.3 | async-start | bytes 262144 | tf_op jit(solution)/shard_map/all_to_all | solution.py:43
  178.1 0.8 slice_convert_fusion
  179.4 5.7 %collective-permute-done.5.gu_refs_2__1_ = bf16[2432,256]{1,0:T(8,128)(2,1)} collective-permute-done((bf16[2432,256]{1,0:T(8,128)(2,1)S(1)}, bf16[2432,256]{1,0:T(8,128)(2,1)}, u32[]{:S(2)}, u32[]{:S(2)}) %collective-permute-start.5) | collective-permute-done | bytes 1245216 | tf_op jit(solution)/shard_map/ppermute | solution.py:26
  185.1 1.9 collective-permute-start.8
  187.1 26.3 %all-to-all-done.3 = bf16[8,16,512]{2,1,0:T(8,128)(2,1)S(1)} async-done(((bf16[8,16,512]{2,1,0:T(8,128)(2,1)}), bf16[8,16,512]{2,1,0:T(8,128)(2,1)S(1)}, u32[]{:S(2)}, u32[]{:S(2)}) %all-to-all-start.3) | async-done | bytes 131104 | tf_op jit(solution)/shard_map/all_to_all | solution.py:43
  213.3 1.3 convolution_convert_fusion
  214.6 7.1 %all-to-all-start.4 = ((bf16[8,96,512]{2,1,0:T(8,128)(2,1)}), bf16[8,96,512]{2,1,0:T(8,128)(2,1)}, u32[]{:S(2)}, u32[]{:S(2)}) async-start(bf16[8,96,512]{2,1,0:T(8,128)(2,1)} %bitcast.19), calls=%async_computation.4 | async-start | bytes 1572864 | tf_op jit(solution)/shard_map/all_to_all | solution.py:43
  221.7 1.3 constant_dynamic-slice_fusion.down_refs_2_
  223.1 2.0 collective-permute-start.11
  225.0 0.7 fusion.9
  225.8 2.4 collective-permute-start.6
  228.2 2.2 collective-permute-start.7
  230.4 6.2 %collective-permute-done.6.gu_refs_2__2_ = bf16[512,256]{1,0:T(8,128)(2,1)S(1)} collective-permute-done((bf16[512,256]{1,0:T(8,128)(2,1)}, bf16[512,256]{1,0:T(8,128)(2,1)S(1)}, u32[]{:S(2)}, u32[]{:S(2)}) %collective-permute-start.6) | collective-permute-done | bytes 262176 | tf_op jit(solution)/shard_map/ppermute | solution.py:26
  236.6 1.9 collective-permute-start.9
  238.6 0.8 negate_select_fusion.sign_ref
  240.1 3.4 %all-to-all-done.4.tiles_ref = bf16[8,96,512]{2,1,0:T(8,128)(2,1)} async-done(((bf16[8,96,512]{2,1,0:T(8,128)(2,1)}), bf16[8,96,512]{2,1,0:T(8,128)(2,1)}, u32[]{:S(2)}, u32[]{:S(2)}) %all-to-all-start.4) | async-done | bytes 786464 | tf_op jit(solution)/shard_map/all_to_all | solution.py:43
  243.4 7.8 %shard_map.167 = bf16[8,96,512]{2,1,0:T(8,128)(2,1)} custom-call(bf16[8,96,512]{2,1,0:T(8,128)(2,1)} %all-to-all-done.4.tiles_ref, f32[1,4096]{1,0:T(1,128)} %bitcast.135, f32[4,4096]{1,0:T(4,128)} %bitcast.134, f32[96,4]{1,0:T(8,128)} %negate_select_fusion.sign_ref, bf16[4096,256]{1,0:T(8,128)(2,1)} %pad_maximum_fusion.gu_refs_0__0_, ...), custom_call_target="tpu_custom_call" | custom-call | tf_op jit(solution)/shard_map/pallas_call | solution.py:176
  251.2 4.5 %all-to-all-start.5 = ((bf16[8,96,512]{2,1,0:T(8,128)(2,1)}), bf16[8,96,512]{2,1,0:T(8,128)(2,1)S(1)}, u32[]{:S(2)}, u32[]{:S(2)}) async-start(bf16[8,96,512]{2,1,0:T(8,128)(2,1)} %shard_map.167), calls=%async_computation.5 | async-start | bytes 1572864 | tf_op jit(solution)/shard_map/all_to_all | solution.py:43
  259.2 20.0 %all-to-all-done.5 = bf16[8,96,512]{2,1,0:T(8,128)(2,1)S(1)} async-done(((bf16[8,96,512]{2,1,0:T(8,128)(2,1)}), bf16[8,96,512]{2,1,0:T(8,128)(2,1)S(1)}, u32[]{:S(2)}, u32[]{:S(2)}) %all-to-all-start.5) | async-done | bytes 786464 | tf_op jit(solution)/shard_map/all_to_all | solution.py:43
  279.1 1.0 convolution_convert_fusion.1
  280.1 10.1 %all-to-all-start.6 = ((bf16[8,16,512]{2,1,0:T(8,128)(2,1)}), bf16[8,16,512]{2,1,0:T(8,128)(2,1)S(1)}, u32[]{:S(2)}, u32[]{:S(2)}) async-start(bf16[8,16,512]{2,1,0:T(8,128)(2,1)} %bitcast.27), calls=%async_computation.6 | async-start | bytes 262144 | tf_op jit(solution)/shard_map/all_to_all | solution.py:43
  292.3 13.8 %all-to-all-done.6 = bf16[8,16,512]{2,1,0:T(8,128)(2,1)S(1)} async-done(((bf16[8,16,512]{2,1,0:T(8,128)(2,1)}), bf16[8,16,512]{2,1,0:T(8,128)(2,1)S(1)}, u32[]{:S(2)}, u32[]{:S(2)}) %all-to-all-start.6) | async-done | bytes 131104 | tf_op jit(solution)/shard_map/all_to_all | solution.py:43
  (98 shorter events, 14.8 us)
Async XLA Ops:
  9.4 59.9 %all-to-all-start = ((bf16[8,16,640]{2,1,0:T(8,128)(2,1)}), bf16[8,16,640]{2,1,0:T(8,128)(2,1)S(1)}, u32[]{:S(2)}, u32[]{:S(2)}) async-start(bf16[8,16,640]{2,1,0:T(8,128)(2,1)} %broadcast_in_dim.114), calls=%async_computation | async-start | bytes 327680 | tf_op jit(solution)/shard_map/all_to_all | solution.py:43
  51.0 88.2 %all-gather.3.cloned.1.call-start = ((), (), s32[]{:S(2)}) async-start(), calls=%async_computation.7 | async-start | bytes 2228224 | tf_op jit(solution)/shard_map/all_gather | solution.py:271
  52.0 11.9 %collective-permute-start = (bf16[272,256]{1,0:T(8,128)(2,1)S(1)}, bf16[272,256]{1,0:T(8,128)(2,1)S(1)}, u32[]{:S(2)}, u32[]{:S(2)}) collective-permute-start(bf16[272,256]{1,0:T(8,128)(2,1)S(1)} %maximum_maximum_fusion), channel_id=1, source_target_pairs={{0,16},{16,0},{1,17},{17,1},{2,18},{18,2},{3,19},{19,3},{4,20},{20... | collective-permute-start | bytes 417800 | tf_op jit(solution)/shard_map/ppermute | solution.py:26
  64.8 3.5 %collective-permute-start.1 = (bf16[544,256]{1,0:T(8,128)(2,1)S(1)}, bf16[544,256]{1,0:T(8,128)(2,1)S(1)}, u32[]{:S(2)}, u32[]{:S(2)}) collective-permute-start(bf16[544,256]{1,0:T(8,128)(2,1)S(1)} %pad_maximum_fusion.2), channel_id=1, source_target_pairs={{0,8},{8,0},{1,9},{9,1},{2,10},{10,2},{3,11},{11,3},{4,12},{12,4},... | collective-permute-start | bytes 835592 | tf_op jit(solution)/shard_map/ppermute | solution.py:26
  69.3 0.8 copy-start.4
  70.1 11.7 %copy-start = (bf16[1,4096,128]{2,1,0:T(8,128)(2,1)S(1)}, bf16[1,4096,128]{2,1,0:T(8,128)(2,1)}, u32[]{:S(2)}) copy-start(bf16[1,4096,128]{2,1,0:T(8,128)(2,1)} %param.25) | copy-start | bytes 3145732
  70.1 11.7 %copy-start.1 = (bf16[1,4096,128]{2,1,0:T(8,128)(2,1)S(1)}, bf16[1,4096,128]{2,1,0:T(8,128)(2,1)}, u32[]{:S(2)}) copy-start(bf16[1,4096,128]{2,1,0:T(8,128)(2,1)} %param.24) | copy-start | bytes 3145732
  71.6 69.5 %all-to-all-start.1 = ((bf16[8,16,640]{2,1,0:T(8,128)(2,1)}), bf16[8,16,640]{2,1,0:T(8,128)(2,1)S(1)}, u32[]{:S(2)}, u32[]{:S(2)}) async-start(bf16[8,16,640]{2,1,0:T(8,128)(2,1)} %bitcast.16), calls=%async_computation.1 | async-start | bytes 327680 | tf_op jit(solution)/shard_map/all_to_all | solution.py:43
  81.8 139.9 %all-gather.5.cloned.1.call-start = ((), (), s32[]{:S(2)}) async-start(), calls=%async_computation.8 | async-start | bytes 3145728 | tf_op jit(solution)/shard_map/all_gather | solution.py:356
  83.5 156.0 %collective-permute-start.3 = (bf16[4096,256]{1,0:T(8,128)(2,1)}, bf16[4096,256]{1,0:T(8,128)(2,1)}, u32[]{:S(2)}, u32[]{:S(2)}) collective-permute-start(bf16[4096,256]{1,0:T(8,128)(2,1)} %pad_maximum_fusion.gu_refs_0__0_), channel_id=1, source_target_pairs={{0,8},{8,0},{1,9},{9,1},{2,10},{10,2},{3,11},{11,3},{4,12},{12,4},... | collective-permute-start | bytes 6291464 | tf_op jit(solution)/shard_map/ppermute | solution.py:26
  85.4 61.3 %copy-start.8 = (bf16[16,128]{1,0:T(8,128)(2,1)S(1)}, bf16[16,128]{1,0:T(8,128)(2,1)}, u32[]{:S(2)}) copy-start(bf16[16,128]{1,0:T(8,128)(2,1)} %param.15) | copy-start | bytes 12292
  85.4 61.3 %copy-start.9 = (bf16[16,128]{1,0:T(8,128)(2,1)S(1)}, bf16[16,128]{1,0:T(8,128)(2,1)}, u32[]{:S(2)}) copy-start(bf16[16,128]{1,0:T(8,128)(2,1)} %param.16) | copy-start | bytes 12292
  85.4 142.7 %collective-permute-start.10 = (bf16[128,4096]{1,0:T(8,128)(2,1)}, bf16[128,4096]{1,0:T(8,128)(2,1)}, u32[]{:S(2)}, u32[]{:S(2)}) collective-permute-start(bf16[128,4096]{1,0:T(8,128)(2,1)} %bitcast.25.down_refs_0_), channel_id=1, source_target_pairs={{0,8},{8,0},{1,9},{9,1},{2,10},{10,2},{3,11},{11,3},{4,12},{12,4},... | collective-permute-start | bytes 3145736 | tf_op jit(solution)/shard_map/ppermute | solution.py:26
  139.2 29.3 %collective-permute-start.2 = (bf16[2048,512]{1,0:T(8,128)(2,1)}, bf16[2048,512]{1,0:T(8,128)(2,1)}, u32[]{:S(2)}, u32[]{:S(2)}) collective-permute-start(bf16[2048,512]{1,0:T(8,128)(2,1)} %all-gather.3.cloned.1.call-done.proj_ref), channel_id=1, source_target_pairs={{0,8},{8,0},{1,9},{9,1},{2,10},{10,2},{3,11},{11,3},{4,12},{12,4},... | collective-permute-start | bytes 6291464 | tf_op jit(solution)/shard_map/ppermute | solution.py:26
  141.2 44.0 %collective-permute-start.5 = (bf16[2432,256]{1,0:T(8,128)(2,1)S(1)}, bf16[2432,256]{1,0:T(8,128)(2,1)}, u32[]{:S(2)}, u32[]{:S(2)}) collective-permute-start(bf16[2432,256]{1,0:T(8,128)(2,1)S(1)} %fusion.3), channel_id=1, source_target_pairs={{0,16},{16,0},{1,17},{17,1},{2,18},{18,2},{3,19},{19,3},{4,20},{20... | collective-permute-start | bytes 3735560 | tf_op jit(solution)/shard_map/ppermute | solution.py:26
  147.4 17.8 %all-to-all-start.2 = ((bf16[8,16,768]{2,1,0:T(8,128)(2,1)}), bf16[8,16,768]{2,1,0:T(8,128)(2,1)S(1)}, u32[]{:S(2)}, u32[]{:S(2)}) async-start(bf16[8,16,768]{2,1,0:T(8,128)(2,1)} %broadcast_in_dim.116), calls=%async_computation.2 | async-start | bytes 393216 | tf_op jit(solution)/shard_map/all_to_all | solution.py:43
  155.2 70.6 %collective-permute-start.4 = (bf16[1152,256]{1,0:T(8,128)(2,1)}, bf16[1152,256]{1,0:T(8,128)(2,1)}, u32[]{:S(2)}, u32[]{:S(2)}) collective-permute-start(bf16[1152,256]{1,0:T(8,128)(2,1)} %fusion.8), channel_id=1, source_target_pairs={{0,16},{16,0},{1,17},{17,1},{2,18},{18,2},{3,19},{19,3},{4,20},{20... | collective-permute-start | bytes 1769480 | tf_op jit(solution)/shard_map/ppermute | solution.py:26
  165.1 0.7 copy-start.3
  171.2 42.2 %all-to-all-start.3 = ((bf16[8,16,512]{2,1,0:T(8,128)(2,1)}), bf16[8,16,512]{2,1,0:T(8,128)(2,1)S(1)}, u32[]{:S(2)}, u32[]{:S(2)}) async-start(bf16[8,16,512]{2,1,0:T(8,128)(2,1)} %get-tuple-element.10), calls=%async_computation.3 | async-start | bytes 262144 | tf_op jit(solution)/shard_map/all_to_all | solution.py:43
  185.1 54.3 %collective-permute-start.8 = (bf16[2432,256]{1,0:T(8,128)(2,1)}, bf16[2432,256]{1,0:T(8,128)(2,1)}, u32[]{:S(2)}, u32[]{:S(2)}) collective-permute-start(bf16[2432,256]{1,0:T(8,128)(2,1)} %collective-permute-done.5.gu_refs_2__1_), channel_id=1, source_target_pairs={{0,8},{8,0},{1,9},{9,1},{2,10},{10,2},{3,11},{11,3},{4,12},{12,4},... | collective-permute-start | bytes 3735560 | tf_op jit(solution)/shard_map/ppermute | solution.py:26
  214.6 28.8 %all-to-all-start.4 = ((bf16[8,96,512]{2,1,0:T(8,128)(2,1)}), bf16[8,96,512]{2,1,0:T(8,128)(2,1)}, u32[]{:S(2)}, u32[]{:S(2)}) async-start(bf16[8,96,512]{2,1,0:T(8,128)(2,1)} %bitcast.19), calls=%async_computation.4 | async-start | bytes 1572864 | tf_op jit(solution)/shard_map/all_to_all | solution.py:43
  223.1 20.4 %copy-start.2 = (bf16[128,4096]{1,0:T(8,128)(2,1)}, bf16[128,4096]{1,0:T(8,128)(2,1)S(1)}, u32[]{:S(2)}) copy-start(bf16[128,4096]{1,0:T(8,128)(2,1)S(1)} %constant_dynamic-slice_fusion.down_refs_2_) | copy-start | bytes 3145732
  223.1 17.0 %collective-permute-start.11 = (bf16[128,4096]{1,0:T(8,128)(2,1)S(1)}, bf16[128,4096]{1,0:T(8,128)(2,1)}, u32[]{:S(2)}, u32[]{:S(2)}) collective-permute-start(bf16[128,4096]{1,0:T(8,128)(2,1)S(1)} %constant_dynamic-slice_fusion.down_refs_2_), channel_id=1, source_target_pairs={{0,8},{8,0},{1,9},{9,1},{2,10},{10,2},{3,11},{11,3},{4,12},{12,4},... | collective-permute-start | bytes 3145736 | tf_op jit(solution)/shard_map/ppermute | solution.py:26
  225.8 10.8 %collective-permute-start.6 = (bf16[512,256]{1,0:T(8,128)(2,1)}, bf16[512,256]{1,0:T(8,128)(2,1)S(1)}, u32[]{:S(2)}, u32[]{:S(2)}) collective-permute-start(bf16[512,256]{1,0:T(8,128)(2,1)} %fusion.9), channel_id=1, source_target_pairs={{0,16},{16,0},{1,17},{17,1},{2,18},{18,2},{3,19},{19,3},{4,20},{20... | collective-permute-start | bytes 786440 | tf_op jit(solution)/shard_map/ppermute | solution.py:26
  228.2 11.2 %collective-permute-start.7 = (bf16[1152,256]{1,0:T(8,128)(2,1)}, bf16[1152,256]{1,0:T(8,128)(2,1)S(1)}, u32[]{:S(2)}, u32[]{:S(2)}) collective-permute-start(bf16[1152,256]{1,0:T(8,128)(2,1)} %collective-permute-done.4.gu_refs_2__0_), channel_id=1, source_target_pairs={{0,8},{8,0},{1,9},{9,1},{2,10},{10,2},{3,11},{11,3},{4,12},{12,4},... | collective-permute-start | bytes 1769480 | tf_op jit(solution)/shard_map/ppermute | solution.py:26
  236.6 6.8 %copy-start.6 = (bf16[512,256]{1,0:T(8,128)(2,1)}, bf16[512,256]{1,0:T(8,128)(2,1)S(1)}, u32[]{:S(2)}) copy-start(bf16[512,256]{1,0:T(8,128)(2,1)S(1)} %collective-permute-done.6.gu_refs_2__2_) | copy-start | bytes 786436
  236.6 3.4 %collective-permute-start.9 = (bf16[512,256]{1,0:T(8,128)(2,1)S(1)}, bf16[512,256]{1,0:T(8,128)(2,1)S(1)}, u32[]{:S(2)}, u32[]{:S(2)}) collective-permute-start(bf16[512,256]{1,0:T(8,128)(2,1)S(1)} %collective-permute-done.6.gu_refs_2__2_), channel_id=1, source_target_pairs={{0,8},{8,0},{1,9},{9,1},{2,10},{10,2},{3,11},{11,3},{4,12},{12,4},... | collective-permute-start | bytes 786440 | tf_op jit(solution)/shard_map/ppermute | solution.py:26
  239.4 4.0 %copy-start.5 = (bf16[1152,256]{1,0:T(8,128)(2,1)}, bf16[1152,256]{1,0:T(8,128)(2,1)S(1)}, u32[]{:S(2)}) copy-start(bf16[1152,256]{1,0:T(8,128)(2,1)S(1)} %collective-permute-done.7.gu_refs_3__0_) | copy-start | bytes 1769476
  240.1 3.4 %copy-start.7 = (bf16[512,256]{1,0:T(8,128)(2,1)}, bf16[512,256]{1,0:T(8,128)(2,1)S(1)}, u32[]{:S(2)}) copy-start(bf16[512,256]{1,0:T(8,128)(2,1)S(1)} %collective-permute-done.9.gu_refs_3__2_) | copy-start | bytes 786436
  251.2 54.9 %copy-start.10 = (bf16[16,512]{1,0:T(8,128)(2,1)S(1)}, bf16[16,512]{1,0:T(8,128)(2,1)}, u32[]{:S(2)}) copy-start(bf16[16,512]{1,0:T(8,128)(2,1)} %get-tuple-element.5) | copy-start | bytes 49156
  251.2 27.9 %all-to-all-start.5 = ((bf16[8,96,512]{2,1,0:T(8,128)(2,1)}), bf16[8,96,512]{2,1,0:T(8,128)(2,1)S(1)}, u32[]{:S(2)}, u32[]{:S(2)}) async-start(bf16[8,96,512]{2,1,0:T(8,128)(2,1)} %shard_map.167), calls=%async_computation.5 | async-start | bytes 1572864 | tf_op jit(solution)/shard_map/all_to_all | solution.py:43
  280.1 26.0 %all-to-all-start.6 = ((bf16[8,16,512]{2,1,0:T(8,128)(2,1)}), bf16[8,16,512]{2,1,0:T(8,128)(2,1)S(1)}, u32[]{:S(2)}, u32[]{:S(2)}) async-start(bf16[8,16,512]{2,1,0:T(8,128)(2,1)} %bitcast.27), calls=%async_computation.6 | async-start | bytes 262144 | tf_op jit(solution)/shard_map/all_to_all | solution.py:43
  292.3 14.4 %copy-start.11 = (bf16[16,1024]{1,0:T(8,128)(2,1)}, bf16[16,1024]{1,0:T(8,128)(2,1)S(1)}, u32[]{:S(2)}) copy-start(bf16[16,1024]{1,0:T(8,128)(2,1)S(1)} %get-tuple-element.30) | copy-start | bytes 98308
  292.3 14.4 %copy-start.12 = (bf16[16,1024]{1,0:T(8,128)(2,1)}, bf16[16,1024]{1,0:T(8,128)(2,1)S(1)}, u32[]{:S(2)}) copy-start(bf16[16,1024]{1,0:T(8,128)(2,1)S(1)} %get-tuple-element.31) | copy-start | bytes 98308
Sparse Core Ops, SparseCore 0:
  57.3 81.8 all-gather.2
  145.1 65.2 all-gather.4
